TPU v7x, 32 devices: a whole 2x2x4 slice. The times are simulated.
32 devices in a mesh: tm: 4 (over z), mem: 4 (over y, x), tile: 2 (over core).
Axes of the slice: x: 2, y: 2, z: 4, core: 2. Of those that a mesh axis runs over, the one named last changes fastest.
Arguments:
- control: float32 [40, 2, 8, 256], P('mem', None, 'tile'), may hold values from -6 to 6
- vertical_modes: float32 [64, 2], replicated, may hold values from -4 to 4
- mode_counts: int32 [8], P('tile'), may hold values from 1 to 2, as said below
- perturbations: bfloat16 [40, 8, 64, 8, 256], P('mem', 'tm', None, 'tile'), may hold values from -6 to 6
- slot_index: int32 [12], P('tm'), may hold values from 0 to 7, as said below
- blend_weight: float32 [12], P('tm'), may hold values from 0 to 1
Outputs:
- increment: float32 [12, 64, 8, 256], P('tm', None, 'tile')
Inputs may be any that keep to these rules, and one draw needn't show every extreme that they name: slot_index[w] // 2 == w // 3. `mode_counts`: both ends of the range occur.
All inputs are finite; a program needn't handle non-finite values.
Results may differ from a plain program's by a relative error of at most 0.0003.
Values sent between devices are 32-bit elements; how exact they have to be, the bound alone decides.
No kernel may reach another device: no remote copies, remote signals or barrier semaphores. Data moves between devices by JAX's collectives and lax.ppermute only.
A program may use at most 64 MiB of HBM per device.

v0:
```python
import math

import jax
import jax.numpy as jnp
from jax import lax
from jax.sharding import PartitionSpec as P

VM = 2
SMOOTH = 4


diffusion = 0.24


def padded_2(cells, sides, width):
    for axis, dim in sides:
        count = lax.axis_size(axis)
        head = lax.slice_in_dim(cells, 0, width, axis=dim)
        tail = lax.slice_in_dim(cells, cells.shape[dim] - width, cells.shape[dim], axis=dim)
        cells = jnp.concatenate(
            [
                lax.ppermute(tail, axis, [(i, (i + 1) % count) for i in range(count)]),
                cells,
                lax.ppermute(head, axis, [((i + 1) % count, i) for i in range(count)]),
            ],
            axis=dim,
        )
    return cells


def prefix(part, axis, combine, identity):
    place = lax.axis_index(axis)
    gathered = lax.all_gather(part, axis)
    state = jnp.zeros_like(part) + jnp.asarray(identity, part.dtype)

    def one(lap, state):
        return combine(state, lax.dynamic_index_in_dim(gathered, lap, 0, False))

    return lax.fori_loop(0, place, one, state)


def relax_local(padded):
    center = padded[:, :, 1:-1]
    neighbours = padded[:, :, 2:] + padded[:, :, :-2]
    bordered = jnp.pad(center, ((0, 0), (0, 0), (0, 0), (1, 1)))
    lateral = bordered[:, :, :, 2:] + bordered[:, :, :, :-2]
    return center + diffusion * (neighbours + lateral - 4.0 * center)


def add_terms(earlier, later):
    return earlier + later


def per_device(control, vertical_modes, mode_counts, perturbations, slot_index, blend_weight):
    field = control
    for repeat in range(SMOOTH):
        field = relax_local(padded_2(field, (("tile", 2),), 1))
    members = perturbations.shape[0]
    slot_count = perturbations.shape[1]
    levels = perturbations.shape[2]
    localized = jnp.zeros((members, levels) + field.shape[2:], jnp.float32)
    for mode_index in range(VM):
        keep_mode = (mode_index < mode_counts).astype(jnp.float32)
        masked = keep_mode[None, :, None] * field[:, mode_index]
        localized = localized + vertical_modes[:, mode_index][None, :, None, None] * masked[:, None]
    partial_sum = jnp.sum(localized[:, None] * perturbations.astype(jnp.float32), axis=0)
    norm_factor = 1.0 / math.sqrt(members * lax.axis_size("mem") - 1)
    member_total = lax.psum_scatter(partial_sum, "mem", scatter_dimension=1, tiled=True)
    running = jnp.cumsum(member_total * norm_factor, axis=0)
    earlier = prefix(running[-1], "tm", add_terms, jnp.zeros_like(running[-1]))
    extended = jnp.concatenate([earlier[None], earlier[None] + running], axis=0)
    local_slot = slot_index - lax.axis_index("tm") * slot_count
    positions = jnp.arange(slot_count + 1, dtype=jnp.int32)[None, :]
    weight = blend_weight[:, None]
    table = weight * (positions == local_slot[:, None] + 1).astype(jnp.float32)
    table = table + (1.0 - weight) * (positions == local_slot[:, None]).astype(jnp.float32)
    blended = jnp.einsum("we,elxy->wlxy", table, extended, precision=lax.Precision.HIGHEST)
    blended = lax.all_gather(blended, "mem", axis=1, tiled=True)
    return blended


def solution(mesh):
    placed = (
        P("mem", None, "tile", None),
        P(),
        P("tile"),
        P("mem", "tm", None, "tile", None),
        P("tm"),
        P("tm"),
    )
    return jax.shard_map(
        per_device,
        mesh=mesh,
        in_specs=placed,
        out_specs=P("tm", None, "tile", None),
        check_vma=False,
    )
```

profile of v0, /device:TPU:0, one launch (start us, length us, event | category | flops | bytes accessed | tf_op | source)
XLA Modules:
  0.0 102.7 jit_solution(3416503850323583249)
XLA Ops:
  6.5 0.0 all-reduce.7.cloned.1.call-start
  6.5 1.1 %fusion.45 = (f32[10,2,1,256]{3,2,1,0:T(1,128)S(1)}, f32[10,2,1,256]{3,2,1,0:T(1,128)S(1)}) fusion(f32[10,2,4,256]{3,2,1,0:T(4,128)} %param.8), kind=kLoop, calls=%fused_computation.79 | loop fusion | bytes 81920 | tf_op jit(solution)/shard_map/slice | solution.py:18
  7.7 0.6 collective-permute-start
  8.2 0.1 collective-permute-start.1
  8.3 0.8 collective-permute-done
  9.1 0.3 collective-permute-done.1
  9.4 1.3 %fusion.9 = f32[10,2,4,256]{3,2,1,0:T(4,128)S(1)} fusion(f32[10,2,4,256]{3,2,1,0:T(4,128)} %param.8, f32[10,2,1,256]{3,2,1,0:T(1,128)S(1)} %collective-permute-done.1, f32[10,2,1,256]{3,2,1,0:T(1,128)S(1)} %collective-permute-done), kind=kLoop, calls=%fused_computation.22 | loop fusion | flops 184320 | bytes 204800 | tf_op jit(solution)/shard_map/add | solution.py:47
  10.8 0.2 collective-permute-start.2
  11.0 0.3 collective-permute-start.3
  11.4 0.7 collective-permute-done.2
  12.0 0.2 collective-permute-done.3
  12.2 0.2 fusion.14
  12.4 0.4 collective-permute-start.4
  12.8 0.2 collective-permute-start.5
  13.0 0.8 slice_bitcast_fusion.1
  13.7 0.0 collective-permute-done.4
  13.8 0.3 collective-permute-done.5
  14.0 0.2 fusion.19
  14.2 0.2 collective-permute-start.6
  14.4 0.3 collective-permute-start.7
  14.8 0.7 compare_convert_fusion.1
  15.5 0.0 collective-permute-done.6
  15.5 0.2 collective-permute-done.7
  15.6 0.2 fusion.24
  15.8 0.1 fusion.30
  15.9 0.8 multiply_add_fusion
  16.7 0.0 copy-done
  16.7 0.0 copy-start.3
  16.7 0.0 copy-start.1
  16.7 0.0 copy-start.2
  16.7 1.6 %multiply_reduce_fusion = f32[2,64,4,256]{3,2,1,0:T(4,128)S(1)} fusion(bf16[10,2,64,4,256]{4,3,2,1,0:T(4,128)(2,1)S(1)} %copy-done, f32[10,64,4,256]{3,2,1,0:T(4,128)S(1)} %multiply_add_fusion), kind=kLoop, calls=%fused_computation.3 | loop fusion | flops 3801088 | bytes 5767168 | tf_op jit(solution)/shard_map/reduce_sum | solution.py:66
  18.3 0.8 copy.9
  19.1 0.0 all-reduce.7.cloned.1.call-update
  19.2 0.0 copy-done.3
  19.2 0.6 dynamic-slice
  20.4 0.0 copy-done.1
  20.5 0.0 copy-done.2
  20.5 46.8 %all-reduce.7.cloned.1.call-done = f32[2,64,4,256]{3,2,0,1:T(4,128)} async-done(((f32[2,64,4,256]{3,2,0,1:T(4,128)}), f32[2,64,4,256]{3,2,0,1:T(4,128)}) %all-reduce.7.cloned.1.call-update) | async-done | bytes 524304
  67.3 0.9 constant_dynamic-slice_fusion.1
  68.2 0.1 copy_multiply_fusion
  68.3 0.3 reduce_window_sum.11
  68.5 0.1 slice.132
  68.6 14.0 %all_gather.6 = f32[4,16,4,256]{3,1,2,0:T(8,128)S(1)} all-gather(f32[1,16,4,256]{3,1,2,0:T(8,128)S(1)} %copy.11), channel_id=1, replica_groups=mesh['tm'=4,'mem'=4,'tile'=2] {'tm'}, dimensions={0}, use_global_device_ids=true | all-gather | bytes 327680 | tf_op jit(solution)/shard_map/all_gather | solution.py:33
  82.7 0.1 broadcast_add_fusion
  82.8 0.6 fusion.1
  83.4 0.1 copy.13
  83.5 11.4 %all_gather.7 = f32[3,64,4,256]{3,2,0,1:T(4,128)S(1)} all-gather(f32[3,16,4,256]{3,2,0,1:T(4,128)S(1)} %copy.13), channel_id=1, replica_groups=mesh['tm'=4,'mem'=4,'tile'=2] {'mem'}, dimensions={1}, use_global_device_ids=true | all-gather | bytes 983040 | tf_op jit(solution)/shard_map/all_gather | solution.py:78
  94.9 1.0 copy.14
  (10 shorter events, 0.2 us)
Async XLA Ops:
  6.5 10.1 %copy-start = (bf16[10,2,64,4,256]{4,3,2,1,0:T(4,128)(2,1)S(1)}, bf16[10,2,64,4,256]{4,3,2,1,0:T(4,128)(2,1)}, u32[]{:S(2)}) copy-start(bf16[10,2,64,4,256]{4,3,2,1,0:T(4,128)(2,1)} %param.11) | copy-start | bytes 7864324
  6.5 60.7 %all-reduce.7.cloned.1.call-start = ((), (), s32[]{:S(2)}) async-start(), calls=%async_computation | async-start | bytes 1048576
  7.7 1.4 %collective-permute-start = (f32[10,2,1,256]{3,2,1,0:T(1,128)S(1)}, f32[10,2,1,256]{3,2,1,0:T(1,128)S(1)}, u32[]{:S(2)}, u32[]{:S(2)}) collective-permute-start(f32[10,2,1,256]{3,2,1,0:T(1,128)S(1)} %get-tuple-element.55), channel_id=1, source_target_pairs={{1,0},{0,1},{3,2},{2,3},{5,4},{4,5},{7,6},{6,7},{9,8},{8,9},{11,10... | collective-permute-start | bytes 61448 | tf_op jit(solution)/shard_map/ppermute | solution.py:24
  8.2 1.2 %collective-permute-start.1 = (f32[10,2,1,256]{3,2,1,0:T(1,128)S(1)}, f32[10,2,1,256]{3,2,1,0:T(1,128)S(1)}, u32[]{:S(2)}, u32[]{:S(2)}) collective-permute-start(f32[10,2,1,256]{3,2,1,0:T(1,128)S(1)} %get-tuple-element.56), channel_id=1, source_target_pairs={{0,1},{1,0},{2,3},{3,2},{4,5},{5,4},{6,7},{7,6},{8,9},{9,8},{10,11... | collective-permute-start | bytes 61448 | tf_op jit(solution)/shard_map/ppermute | solution.py:22
  10.8 1.3 %collective-permute-start.2 = (f32[10,2,1,256]{3,2,1,0:T(1,128)S(1)}, f32[10,2,1,256]{3,2,1,0:T(1,128)S(1)}, u32[]{:S(2)}, u32[]{:S(2)}) collective-permute-start(f32[10,2,1,256]{3,2,1,0:T(1,128)S(1)} %get-tuple-element.53), channel_id=1, source_target_pairs={{1,0},{0,1},{3,2},{2,3},{5,4},{4,5},{7,6},{6,7},{9,8},{8,9},{11,10... | collective-permute-start | bytes 61448 | tf_op jit(solution)/shard_map/ppermute | solution.py:24
  11.0 1.2 %collective-permute-start.3 = (f32[10,2,1,256]{3,2,1,0:T(1,128)S(1)}, f32[10,2,1,256]{3,2,1,0:T(1,128)S(1)}, u32[]{:S(2)}, u32[]{:S(2)}) collective-permute-start(f32[10,2,1,256]{3,2,1,0:T(1,128)S(1)} %get-tuple-element.54), channel_id=1, source_target_pairs={{0,1},{1,0},{2,3},{3,2},{4,5},{5,4},{6,7},{7,6},{8,9},{9,8},{10,11... | collective-permute-start | bytes 61448 | tf_op jit(solution)/shard_map/ppermute | solution.py:22
  12.4 1.3 %collective-permute-start.4 = (f32[10,2,1,256]{3,2,1,0:T(1,128)S(1)}, f32[10,2,1,256]{3,2,1,0:T(1,128)S(1)}, u32[]{:S(2)}, u32[]{:S(2)}) collective-permute-start(f32[10,2,1,256]{3,2,1,0:T(1,128)S(1)} %get-tuple-element.51), channel_id=1, source_target_pairs={{1,0},{0,1},{3,2},{2,3},{5,4},{4,5},{7,6},{6,7},{9,8},{8,9},{11,10... | collective-permute-start | bytes 61448 | tf_op jit(solution)/shard_map/ppermute | solution.py:24
  12.8 1.2 %collective-permute-start.5 = (f32[10,2,1,256]{3,2,1,0:T(1,128)S(1)}, f32[10,2,1,256]{3,2,1,0:T(1,128)S(1)}, u32[]{:S(2)}, u32[]{:S(2)}) collective-permute-start(f32[10,2,1,256]{3,2,1,0:T(1,128)S(1)} %get-tuple-element.52), channel_id=1, source_target_pairs={{0,1},{1,0},{2,3},{3,2},{4,5},{5,4},{6,7},{7,6},{8,9},{9,8},{10,11... | collective-permute-start | bytes 61448 | tf_op jit(solution)/shard_map/ppermute | solution.py:22
  14.2 1.3 %collective-permute-start.6 = (f32[10,2,1,256]{3,2,1,0:T(1,128)S(1)}, f32[10,2,1,256]{3,2,1,0:T(1,128)S(1)}, u32[]{:S(2)}, u32[]{:S(2)}) collective-permute-start(f32[10,2,1,256]{3,2,1,0:T(1,128)S(1)} %get-tuple-element.49), channel_id=1, source_target_pairs={{1,0},{0,1},{3,2},{2,3},{5,4},{4,5},{7,6},{6,7},{9,8},{8,9},{11,10... | collective-permute-start | bytes 61448 | tf_op jit(solution)/shard_map/ppermute | solution.py:24
  14.4 1.2 %collective-permute-start.7 = (f32[10,2,1,256]{3,2,1,0:T(1,128)S(1)}, f32[10,2,1,256]{3,2,1,0:T(1,128)S(1)}, u32[]{:S(2)}, u32[]{:S(2)}) collective-permute-start(f32[10,2,1,256]{3,2,1,0:T(1,128)S(1)} %get-tuple-element.50), channel_id=1, source_target_pairs={{0,1},{1,0},{2,3},{3,2},{4,5},{5,4},{6,7},{7,6},{8,9},{9,8},{10,11... | collective-permute-start | bytes 61448 | tf_op jit(solution)/shard_map/ppermute | solution.py:22
  16.7 2.5 %copy-start.3 = (u32[32]{0:T(128)S(1)}, u32[32]{0:T(128)}, u32[]{:S(2)}) copy-start(u32[32]{0:T(128)} %constant.52) | copy-start | bytes 388
  16.7 3.8 %copy-start.1 = (f32[3]{0:T(128)S(1)}, f32[3]{0:T(128)}, u32[]{:S(2)}) copy-start(f32[3]{0:T(128)} %param.13) | copy-start | bytes 40
  16.7 3.8 %copy-start.2 = (s32[3]{0:T(128)S(1)}, s32[3]{0:T(128)}, u32[]{:S(2)}) copy-start(s32[3]{0:T(128)} %param.12) | copy-start | bytes 40
Sparse Core Ops, SparseCore 0:
  19.3 47.9 all-reduce.6
where the time goes:
time: 103 us
  waiting for transfers between devices  49.2 us (48%)
  blocking collectives  25.4 us (25%)
  between operations  14.2 us (14%)
  local copies, waits for them, and re-layouts  5.55 us (5%)
  other arithmetic  5.36 us (5%)
  starting transfers between devices  2.36 us (2%)
    unnamed x2, waiting for transfers between devices  46.8 us
    all_gather x1, blocking collectives, prefix(): gathered = lax.all_gather(part, axis)  14 us
    all_gather x1, blocking collectives, per_device(): blended = lax.all_gather(blended, 'mem', axis=1, tiled=True)  11.4 us
  transfers between devices with their start and end apart: 9, of which 7 were waited for; matrix products, arithmetic and copies ran while one was open for 2% of the time, Pallas kernels for 0%

commit v1 on v0

v1 whole, which is shorter than its diff:
```python
import math

import jax
import jax.numpy as jnp
from jax import lax
from jax.sharding import PartitionSpec as P

VM = 2
SMOOTH = 4

diffusion = 0.24


def ring(count, shift):
    return [(i, (i + shift) % count) for i in range(count)]


def is_power(count):
    return count & (count - 1) == 0


def pairing(count, step):
    if is_power(count):
        return [(i, i ^ step) for i in range(count)]
    return ring(count, step)


def target_of(place, count, step):
    if is_power(count):
        return place ^ step
    return (place + step) % count


def source_of(place, count, step):
    if is_power(count):
        return place ^ step
    return (place - step) % count


def relax(field):
    neighbours = jnp.roll(field, -1, axis=2) + jnp.roll(field, 1, axis=2)
    bordered = jnp.pad(field, ((0, 0), (0, 0), (0, 0), (1, 1)))
    lateral = bordered[:, :, :, 2:] + bordered[:, :, :, :-2]
    return field + diffusion * (neighbours + lateral - 4.0 * field)


def smooth(field):
    count = lax.axis_size("tile")
    width = field.shape[2]
    left = SMOOTH
    while left:
        reach = min(left, width)
        if count == 1:
            wide, start = field, 0
        elif count == 2 and reach == width:
            other = lax.ppermute(field, "tile", ring(2, 1))
            wide, start = jnp.concatenate([field, other], axis=2), 0
        else:
            head = lax.slice_in_dim(field, 0, reach, axis=2)
            tail = lax.slice_in_dim(field, width - reach, width, axis=2)
            before = lax.ppermute(tail, "tile", ring(count, 1))
            after = lax.ppermute(head, "tile", ring(count, -1))
            wide, start = jnp.concatenate([before, field, after], axis=2), reach
        for _ in range(reach):
            wide = relax(wide)
        field = lax.slice_in_dim(wide, start, start + width, axis=2)
        left -= reach
    return field


def per_device(control, vertical_modes, mode_counts, perturbations, slot_index, blend_weight):
    members, slot_count, levels = perturbations.shape[:3]
    group = lax.axis_size("mem")
    place = lax.axis_index("mem")
    share = levels // group
    norm_factor = 1.0 / math.sqrt(members * group - 1)

    field = smooth(control)
    masked = []
    for mode_index in range(VM):
        keep_mode = (mode_index < mode_counts).astype(jnp.float32)
        masked.append(keep_mode[None, :, None] * field[:, mode_index])

    def terms(owner):
        part = lax.dynamic_slice_in_dim(perturbations, owner * share, share, axis=2)
        modes = lax.dynamic_slice_in_dim(vertical_modes, owner * share, share, axis=0)
        localized = sum(
            modes[:, m][None, :, None, None] * masked[m][:, None] for m in range(VM)
        )
        return jnp.sum(localized[:, None] * part.astype(jnp.float32), axis=0)

    arrived = []
    for step in range(group - 1, 0, -1):
        arrived.append(
            lax.ppermute(terms(target_of(place, group, step)), "mem", pairing(group, step))
        )
    slots = terms(place)
    for part in arrived:
        slots = slots + part
    slots = slots * norm_factor

    stages = lax.axis_size("tm")
    stage = lax.axis_index("tm")
    total = jnp.sum(slots, axis=0)
    earlier = jnp.zeros_like(total)
    for step in range(1, stages):
        came = lax.ppermute(total, "tm", ring(stages, step))
        earlier = earlier + jnp.where(stage >= step, came, 0.0)

    local_slot = slot_index - stage * slot_count
    blended = []
    for w in range(slot_index.shape[0]):
        mixed = earlier
        for s in range(slot_count):
            factor = jnp.where(
                local_slot[w] == s, blend_weight[w], jnp.where(local_slot[w] > s, 1.0, 0.0)
            )
            mixed = mixed + factor * slots[s]
        blended.append(mixed)
    blended = jnp.stack(blended)
    return lax.all_gather(blended, "mem", axis=1, tiled=True)


def solution(mesh):
    placed = (
        P("mem", None, "tile", None),
        P(),
        P("tile"),
        P("mem", "tm", None, "tile", None),
        P("tm"),
        P("tm"),
    )
    return jax.shard_map(
        per_device,
        mesh=mesh,
        in_specs=placed,
        out_specs=P("tm", None, "tile", None),
        check_vma=False,
    )
```

time: 103 us -> 44.7 us (0.43)
  waiting for transfers between devices: 49.2 us -> 0.02 us
  blocking collectives: 25.4 us -> 11.1 us
  starting transfers between devices: 2.36 us -> 10.6 us
  between operations: 14.2 us -> 11.5 us
    unnamed x2 -> x0, waiting for transfers between devices: 46.8 us -> none
    all_gather x2 -> x1, blocking collectives: 25.4 us -> 11.1 us  [per_device(): return lax.all_gather(blended, 'mem', axis=1, tiled=True)]
    ppermute x8 -> x7, starting transfers between devices: 2.36 us -> 10.6 us  [the longest x3 5.97 us: per_device(): came = lax.ppermute(total, 'tm', ring(stages, step))]
    ppermute x8 -> x7, waiting for transfers between devices: 2.41 us -> 0.02 us  [the longest x3 0.01 us: per_device(): lax.ppermute(terms(target_of(place, group, step)), 'mem', pairing(group,...]
    concatenate x0 -> x2, other arithmetic: none -> 1.96 us  [smooth(): wide, start = (jnp.concatenate([field, other], axis=2), 0)]
    add x7 -> x5, other arithmetic: 2.66 us -> 1.44 us  [the longest x1 0.76 us: terms(): sum((modes[:, m][None, :, None, None] * masked[m][:, None] for m in range...]
    slice x6 -> x10, local copies, waits for them, and re-layouts: 1.3 us -> 2.35 us  [the longest x8 1.08 us: relax(): neighbours = jnp.roll(field, -1, axis=2) + jnp.roll(field, 1, axis=2)]
  transfers between devices with their start and end apart: 9 -> 7, of which waited for: 7 -> 0; matrix products, arithmetic and copies ran while one was open for 2% -> 8% of each run, Pallas kernels for 0% -> 0%
where the time goes in v1:
time: 44.7 us; the launch traced here: 44.2 us
  between operations  11.5 us (26%)
  blocking collectives  11.1 us (25%)
  starting transfers between devices  10.6 us (24%)
  other arithmetic  5.92 us (13%)
  local copies, waits for them, and re-layouts  5.11 us (11%)
    all_gather x1, blocking collectives, per_device(): return lax.all_gather(blended, 'mem', axis=1, tiled=True)  11.1 us
    ppermute x3, starting transfers between devices, per_device(): came = lax.ppermute(total, 'tm', ring(stages, step))  5.97 us
    ppermute x3, starting transfers between devices, per_device(): lax.ppermute(terms(target_of(place, group, step)), 'mem', pairing(group,...  4.14 us
    concatenate x2, other arithmetic, smooth(): wide, start = (jnp.concatenate([field, other], axis=2), 0)  1.96 us
    unnamed x7, local copies, waits for them, and re-layouts  1.85 us
    reduce_sum x1, other arithmetic, terms(): return jnp.sum(localized[:, None] * part.astype(jnp.float32), axis=0)  1.54 us
    slice x8, local copies, waits for them, and re-layouts, relax(): neighbours = jnp.roll(field, -1, axis=2) + jnp.roll(field, 1, axis=2)  1.08 us
    dynamic_slice x1, local copies, waits for them, and re-layouts, terms(): lax.dynamic_slice_in_dim(vertical_modes, owner * share, share, axis=0)  0.9 us
  transfers between devices with their start and end apart: 7, of which 0 were waited for; matrix products, arithmetic and copies ran while one was open for 8% of the time, Pallas kernels for 0%

profile of v1, /device:TPU:0, one launch (start us, length us, event | category | flops | bytes accessed | tf_op | source)
XLA Modules:
  0.0 44.2 jit_solution(4025381710863709894)
XLA Ops:
  0.0 0.5 %collective-permute-start = (f32[10,2,4,256]{3,2,1,0:T(4,128)}, f32[10,2,4,256]{3,2,1,0:T(4,128)S(1)}, u32[]{:S(2)}, u32[]{:S(2)}) collective-permute-start(f32[10,2,4,256]{3,2,1,0:T(4,128)} %param.6), channel_id=1, source_target_pairs={{0,1},{1,0},{2,3},{3,2},{4,5},{5,4},{6,7},{7,6},{8,9},{9,8},{10,11... | collective-permute-start | bytes 245768 | tf_op jit(solution)/shard_map/ppermute | solution.py:56
  0.5 0.9 %constant_dynamic-slice_fusion.1 = (f32[16,2]{0,1:T(2,128)S(1)}, f32[16,2]{0,1:T(2,128)S(1)}, f32[16,2]{0,1:T(2,128)S(1)}, f32[16,2]{0,1:T(2,128)S(1)}) fusion(f32[64,2]{0,1:T(2,128)} %param.7, s32[]{:T(128)S(6)} %select_n.101, s32[]{:T(128)S(6)} %select_n.100, s32[]{:T(128)S(6)} %select_n.99, s32[]{:T(128)S(6)} %select_n.102), kind=kLoop, calls=%fused_computation.64 | loop fusion | bytes 1040 | tf_op jit(solution)/shard_map/dynamic_slice | solution.py:86
  1.4 0.7 %compare_convert_fusion.1 = (f32[4]{0:T(128)S(1)}, f32[4]{0:T(128)S(1)}) fusion(s32[4]{0:T(128)} %param.8), kind=kLoop, calls=%fused_computation.68 | loop fusion | flops 16 | bytes 48 | tf_op jit(solution)/shard_map/convert_element_type | solution.py:81
  2.1 0.9 %slice.153 = f32[10,2,1,256]{3,2,1,0:T(1,128)S(1)} slice(f32[10,2,4,256]{3,2,1,0:T(4,128)} %param.6), slice={[0:10], [0:2], [0:1], [0:256]} | slice | bytes 40960 | tf_op jit(solution)/shard_map/jit(_roll_static)/slice | solution.py:41
  3.0 0.0 collective-permute-done
  3.0 1.0 %fusion.1 = (f32[10,2,7,256]{3,2,1,0:T(8,128)S(1)}, f32[10,2,7,256]{3,2,1,0:T(8,128)S(1)}) fusion(f32[10,2,4,256]{3,2,1,0:T(4,128)} %param.6, f32[10,2,4,256]{3,2,1,0:T(4,128)S(1)} %collective-permute-done), kind=kLoop, calls=%fused_computation.23 | loop fusion | flops 71680 | bytes 450560 | tf_op jit(solution)/shard_map/concatenate | solution.py:57
  4.0 0.9 %pad_maximum_fusion = f32[10,2,8,256]{3,2,1,0:T(8,128)S(1)} fusion(f32[10,2,4,256]{3,2,1,0:T(4,128)S(1)} %collective-permute-done, f32[10,2,4,256]{3,2,1,0:T(4,128)} %param.6), kind=kLoop, calls=%fused_computation.18 | loop fusion | flops 40960 | bytes 327680 | tf_op jit(solution)/shard_map/concatenate | solution.py:57
  5.0 0.2 fusion.6
  5.2 0.2 fusion.11
  5.5 0.2 fusion.16
  5.7 0.2 fusion.21
  5.9 0.1 fusion.26
  5.9 0.0 copy-start
  6.0 0.8 %multiply_add_fusion.1 = (f32[10,16,4,256]{3,2,1,0:T(4,128)S(1)}, f32[10,16,4,256]{3,2,1,0:T(4,128)S(1)}, f32[10,16,4,256]{3,2,1,0:T(4,128)S(1)}, f32[10,16,4,256]{3,2,1,0:T(4,128)S(1)}) fusion(f32[16]{0:T(128)S(1)} %get-tuple-element.55, f32[16]{0:T(128)S(1)} %get-tuple-element.56, f32[10,4,256]{2,1,0:T(4,128)S(1)} %get-tuple-element.16, ...), kind=kLoop, calls=%fused_computation.5 | loop fusion | flops 1966080 | bytes 2703872 | tf_op jit(solution)/shard_map/add | solution.py:87
  6.7 1.0 %copy-done = bf16[10,2,64,4,256]{4,3,2,1,0:T(4,128)(2,1)S(1)} copy-done((bf16[10,2,64,4,256]{4,3,2,1,0:T(4,128)(2,1)S(1)}, bf16[10,2,64,4,256]{4,3,2,1,0:T(4,128)(2,1)}, u32[]{:S(2)}) %copy-start) | copy-done | bytes 2621464
  7.7 0.0 copy-start.2
  7.7 0.0 copy-start.1
  7.7 1.5 %multiply_reduce_fusion.2 = (f32[2,16,4,256]{3,2,1,0:T(4,128)S(1)}, f32[2,16,4,256]{3,2,1,0:T(4,128)S(1)}, f32[2,16,4,256]{3,2,1,0:T(4,128)S(1)}, f32[2,16,4,256]{3,2,1,0:T(4,128)S(1)}) fusion(bf16[10,2,64,4,256]{4,3,2,1,0:T(4,128)(2,1)S(1)} %copy-done, s32[]{:T(128)S(6)} %select_n.100, f32[10,16,4,256]{3,2,1,0:T(4,128)S(1)} %get-tuple-element.32, ...), kind=kLoop, calls=%fused_computation.2 | loop fusion | flops 3801088 | bytes 5767184 | tf_op jit(solution)/shard_map/reduce_sum | solution.py:90
  9.2 3.5 %collective-permute-start.1 = (f32[2,16,4,256]{3,2,1,0:T(4,128)S(1)}, f32[2,16,4,256]{3,2,1,0:T(4,128)S(1)}, u32[]{:S(2)}, u32[]{:S(2)}) collective-permute-start(f32[2,16,4,256]{3,2,1,0:T(4,128)S(1)} %get-tuple-element.5), channel_id=1, source_target_pairs={{0,6},{2,4},{4,2},{6,0},{1,7},{3,5},{5,3},{7,1},{8,14},{10,12},{12... | collective-permute-start | bytes 393224 | tf_op jit(solution)/shard_map/ppermute | solution.py:95
  12.7 0.5 %collective-permute-start.2 = (f32[2,16,4,256]{3,2,1,0:T(4,128)S(1)}, f32[2,16,4,256]{3,2,1,0:T(4,128)S(1)}, u32[]{:S(2)}, u32[]{:S(2)}) collective-permute-start(f32[2,16,4,256]{3,2,1,0:T(4,128)S(1)} %get-tuple-element.8), channel_id=1, source_target_pairs={{0,4},{2,6},{4,0},{6,2},{1,5},{3,7},{5,1},{7,3},{8,12},{10,14},{12... | collective-permute-start | bytes 393224 | tf_op jit(solution)/shard_map/ppermute | solution.py:95
  13.2 0.1 collective-permute-start.3
  13.4 0.0 copy-done.2
  13.4 0.7 %fusion.35 = (s32[1]{0:T(128)}, s32[1]{0:T(128)}, s32[1]{0:T(128)}) fusion(s32[3]{0:T(128)S(1)} %broadcast_subtract_fusion), kind=kLoop, calls=%fused_computation.86 | loop fusion | bytes 24 | tf_op jit(solution)/shard_map/slice | solution.py:116
  21.7 0.0 collective-permute-done.1
  21.7 0.0 collective-permute-done.2
  21.7 0.0 collective-permute-done.3
  21.7 0.1 fusion.27
  21.8 2.0 %collective-permute-start.4 = (f32[16,4,256]{2,1,0:T(4,128)S(1)}, f32[16,4,256]{2,1,0:T(4,128)S(1)}, u32[]{:S(2)}, u32[]{:S(2)}) collective-permute-start(f32[16,4,256]{2,1,0:T(4,128)S(1)} %get-tuple-element.11), channel_id=1, source_target_pairs={{0,8},{8,16},{16,24},{24,0},{1,9},{9,17},{17,25},{25,1},{2,10},{10... | collective-permute-start | bytes 196616 | tf_op jit(solution)/shard_map/ppermute | solution.py:107
  23.8 2.6 %collective-permute-start.5 = (f32[16,4,256]{2,1,0:T(4,128)S(1)}, f32[16,4,256]{2,1,0:T(4,128)S(1)}, u32[]{:S(2)}, u32[]{:S(2)}) collective-permute-start(f32[16,4,256]{2,1,0:T(4,128)S(1)} %get-tuple-element.11), channel_id=1, source_target_pairs={{0,16},{8,24},{16,0},{24,8},{1,17},{9,25},{17,1},{25,9},{2,18},{10... | collective-permute-start | bytes 196616 | tf_op jit(solution)/shard_map/ppermute | solution.py:107
  26.4 1.3 %collective-permute-start.6 = (f32[16,4,256]{2,1,0:T(4,128)S(1)}, f32[16,4,256]{2,1,0:T(4,128)S(1)}, u32[]{:S(2)}, u32[]{:S(2)}) collective-permute-start(f32[16,4,256]{2,1,0:T(4,128)S(1)} %get-tuple-element.11), channel_id=1, source_target_pairs={{0,24},{8,0},{16,8},{24,16},{1,25},{9,1},{17,9},{25,17},{2,26},{10... | collective-permute-start | bytes 196616 | tf_op jit(solution)/shard_map/ppermute | solution.py:107
  27.8 0.0 copy-done.1
  27.8 0.6 %fusion.34 = (f32[1]{0:T(128)}, f32[1]{0:T(128)}, f32[1]{0:T(128)}) fusion(f32[3]{0:T(128)S(1)} %copy-done.1), kind=kLoop, calls=%fused_computation.85 | loop fusion | bytes 24 | tf_op jit(solution)/shard_map/slice | solution.py:116
  32.0 0.0 collective-permute-done.4
  32.0 0.0 collective-permute-done.5
  32.0 0.0 collective-permute-done.6
  32.1 0.1 fusion.24
  32.2 11.1 %all_gather.3 = f32[3,64,4,256]{3,2,1,0:T(4,128)S(1)} all-gather(f32[3,16,4,256]{3,2,1,0:T(4,128)S(1)} %pad_maximum_fusion.1), channel_id=1, replica_groups=mesh['tm'=4,'mem'=4,'tile'=2] {'mem'}, dimensions={1}, use_global_device_ids=true | all-gather | bytes 983040 | tf_op jit(solution)/shard_map/all_gather | solution.py:121
  43.4 0.9 %copy.8 = f32[3,64,4,256]{3,2,1,0:T(4,128)} copy(f32[3,64,4,256]{3,2,1,0:T(4,128)S(1)} %all_gather.3) | data formatting | bytes 1572864
  (12 shorter events, 0.3 us)
Async XLA Ops:
  0.0 3.0 %collective-permute-start = (f32[10,2,4,256]{3,2,1,0:T(4,128)}, f32[10,2,4,256]{3,2,1,0:T(4,128)S(1)}, u32[]{:S(2)}, u32[]{:S(2)}) collective-permute-start(f32[10,2,4,256]{3,2,1,0:T(4,128)} %param.6), channel_id=1, source_target_pairs={{0,1},{1,0},{2,3},{3,2},{4,5},{5,4},{6,7},{7,6},{8,9},{9,8},{10,11... | collective-permute-start | bytes 245768 | tf_op jit(solution)/shard_map/ppermute | solution.py:56
  5.9 1.7 %copy-start = (bf16[10,2,64,4,256]{4,3,2,1,0:T(4,128)(2,1)S(1)}, bf16[10,2,64,4,256]{4,3,2,1,0:T(4,128)(2,1)}, u32[]{:S(2)}) copy-start(bf16[10,2,64,4,256]{4,3,2,1,0:T(4,128)(2,1)} %param.9) | copy-start | bytes 7864324
  7.7 5.7 %copy-start.2 = (s32[3]{0:T(128)S(1)}, s32[3]{0:T(128)}, u32[]{:S(2)}) copy-start(s32[3]{0:T(128)} %param.10) | copy-start | bytes 40
  7.7 20.1 %copy-start.1 = (f32[3]{0:T(128)S(1)}, f32[3]{0:T(128)}, u32[]{:S(2)}) copy-start(f32[3]{0:T(128)} %param.11) | copy-start | bytes 40
  9.2 12.4 %collective-permute-start.1 = (f32[2,16,4,256]{3,2,1,0:T(4,128)S(1)}, f32[2,16,4,256]{3,2,1,0:T(4,128)S(1)}, u32[]{:S(2)}, u32[]{:S(2)}) collective-permute-start(f32[2,16,4,256]{3,2,1,0:T(4,128)S(1)} %get-tuple-element.5), channel_id=1, source_target_pairs={{0,6},{2,4},{4,2},{6,0},{1,7},{3,5},{5,3},{7,1},{8,14},{10,12},{12... | collective-permute-start | bytes 393224 | tf_op jit(solution)/shard_map/ppermute | solution.py:95
  12.7 8.9 %collective-permute-start.2 = (f32[2,16,4,256]{3,2,1,0:T(4,128)S(1)}, f32[2,16,4,256]{3,2,1,0:T(4,128)S(1)}, u32[]{:S(2)}, u32[]{:S(2)}) collective-permute-start(f32[2,16,4,256]{3,2,1,0:T(4,128)S(1)} %get-tuple-element.8), channel_id=1, source_target_pairs={{0,4},{2,6},{4,0},{6,2},{1,5},{3,7},{5,1},{7,3},{8,12},{10,14},{12... | collective-permute-start | bytes 393224 | tf_op jit(solution)/shard_map/ppermute | solution.py:95
  13.2 8.4 %collective-permute-start.3 = (f32[2,16,4,256]{3,2,1,0:T(4,128)S(1)}, f32[2,16,4,256]{3,2,1,0:T(4,128)S(1)}, u32[]{:S(2)}, u32[]{:S(2)}) collective-permute-start(f32[2,16,4,256]{3,2,1,0:T(4,128)S(1)} %get-tuple-element.7), channel_id=1, source_target_pairs={{0,2},{2,0},{4,6},{6,4},{1,3},{3,1},{5,7},{7,5},{8,10},{10,8},{12,... | collective-permute-start | bytes 393224 | tf_op jit(solution)/shard_map/ppermute | solution.py:95
  21.8 10.2 %collective-permute-start.4 = (f32[16,4,256]{2,1,0:T(4,128)S(1)}, f32[16,4,256]{2,1,0:T(4,128)S(1)}, u32[]{:S(2)}, u32[]{:S(2)}) collective-permute-start(f32[16,4,256]{2,1,0:T(4,128)S(1)} %get-tuple-element.11), channel_id=1, source_target_pairs={{0,8},{8,16},{16,24},{24,0},{1,9},{9,17},{17,25},{25,1},{2,10},{10... | collective-permute-start | bytes 196616 | tf_op jit(solution)/shard_map/ppermute | solution.py:107
  23.8 8.2 %collective-permute-start.5 = (f32[16,4,256]{2,1,0:T(4,128)S(1)}, f32[16,4,256]{2,1,0:T(4,128)S(1)}, u32[]{:S(2)}, u32[]{:S(2)}) collective-permute-start(f32[16,4,256]{2,1,0:T(4,128)S(1)} %get-tuple-element.11), channel_id=1, source_target_pairs={{0,16},{8,24},{16,0},{24,8},{1,17},{9,25},{17,1},{25,9},{2,18},{10... | collective-permute-start | bytes 196616 | tf_op jit(solution)/shard_map/ppermute | solution.py:107
  26.4 5.6 %collective-permute-start.6 = (f32[16,4,256]{2,1,0:T(4,128)S(1)}, f32[16,4,256]{2,1,0:T(4,128)S(1)}, u32[]{:S(2)}, u32[]{:S(2)}) collective-permute-start(f32[16,4,256]{2,1,0:T(4,128)S(1)} %get-tuple-element.11), channel_id=1, source_target_pairs={{0,24},{8,0},{16,8},{24,16},{1,25},{9,1},{17,9},{25,17},{2,26},{10... | collective-permute-start | bytes 196616 | tf_op jit(solution)/shard_map/ppermute | solution.py:107

commit v2 on v1

v2 whole, which is shorter than its diff:
```python
import functools
import math

import jax
import jax.numpy as jnp
from jax import lax
from jax.experimental import pallas as pl
from jax.experimental.pallas import tpu as pltpu
from jax.sharding import PartitionSpec as P


SMOOTH = 4
LANES = 128
ROWS = 8
VMEM_BYTES = 64 * 1024 * 1024

diffusion = 0.24


def ring(count, shift):
    return [(i, (i + shift) % count) for i in range(count)]


def is_power(count):
    return count & (count - 1) == 0


def pairing(count, step):
    if is_power(count):
        return [(i, i ^ step) for i in range(count)]
    return ring(count, step)


def target_of(place, count, step):
    if is_power(count):
        return place ^ step
    return lax.rem(place + step, count)


def view(field):
    lead = field.shape[:-3]
    levels, x, y = field.shape[-3:]
    field = field.reshape(*lead, levels, x, y // LANES, LANES)
    field = jnp.swapaxes(field, -3, -2)
    return field.reshape(*lead, levels * x * (y // LANES), LANES)


def unview(rows, x, y):
    lead = rows.shape[:-2]
    tiles = y // LANES
    rows = rows.reshape(*lead, rows.shape[-2] // (x * tiles), tiles, x, LANES)
    rows = jnp.swapaxes(rows, -3, -2)
    return rows.reshape(*lead, -1, x, y)


def relax(field):
    neighbours = jnp.roll(field, -1, axis=2) + jnp.roll(field, 1, axis=2)
    bordered = jnp.pad(field, ((0, 0), (0, 0), (0, 0), (1, 1)))
    lateral = bordered[:, :, :, 2:] + bordered[:, :, :, :-2]
    return field + diffusion * (neighbours + lateral - 4.0 * field)


def smooth(field):
    count = lax.axis_size("tile")
    width = field.shape[2]
    left = SMOOTH
    while left:
        reach = min(left, width)
        head = lax.slice_in_dim(field, 0, reach, axis=2)
        tail = lax.slice_in_dim(field, width - reach, width, axis=2)
        before = lax.ppermute(tail, "tile", ring(count, 1))
        after = lax.ppermute(head, "tile", ring(count, -1))
        wide = jnp.concatenate([before, field, after], axis=2)
        for _ in range(reach):
            wide = relax(wide)
        field = lax.slice_in_dim(wide, reach, reach + width, axis=2)
        left -= reach
    return field


def load_kernel(
    x, modes_hbm, counts_hbm, index_hbm, weight_hbm, own_hbm, part_hbm,
    own_ref, part_ref, splat_ref, mask_ref, factor_ref,
    modes_ref, counts_ref, index_ref, weight_ref, sems,
):
    pairs = [
        (modes_hbm, modes_ref),
        (counts_hbm, counts_ref),
        (index_hbm, index_ref),
        (weight_hbm, weight_ref),
        (own_hbm, own_ref),
        (part_hbm, part_ref),
    ]
    copies = [pltpu.make_async_copy(a, b, sems.at[i]) for i, (a, b) in enumerate(pairs)]
    for copy in copies:
        copy.start()
    for copy in copies[:-2]:
        copy.wait()
    levels, modes = splat_ref.shape[:2]
    for l in range(levels):
        for m in range(modes):
            splat_ref[l, m] = jnp.full((ROWS, LANES), modes_ref[m, l], jnp.float32)
    column = lax.rem(lax.broadcasted_iota(jnp.int32, (ROWS, LANES), 0), x)
    count = jnp.zeros((ROWS, LANES), jnp.int32)
    for i in range(x):
        count = jnp.where(column == i, counts_ref[i], count)
    for m in range(modes):
        mask_ref[m] = (m < count).astype(jnp.float32)
    windows, slots = factor_ref.shape[:2]
    for w in range(windows):
        local = index_ref[w] - lax.axis_index("tm") * slots
        for t in range(slots):
            factor = jnp.where(local == t, weight_ref[w], jnp.where(local > t, 1.0, 0.0))
            factor_ref[w, t] = jnp.full((ROWS, LANES), factor, jnp.float32)
    for copy in copies[-2:]:
        copy.wait()


def smoothed_pair(own, other):
    row = lax.broadcasted_iota(jnp.int32, (ROWS, LANES), 0)
    lane = lax.broadcasted_iota(jnp.int32, (ROWS, LANES), 1)
    half = ROWS // 2
    low = jnp.where(row < half, own, pltpu.roll(other, half, 0))
    high = jnp.where(row < half, pltpu.roll(own, half, 0), other)
    first, last = lane == 0, lane == LANES - 1
    for _ in range(SMOOTH):
        low_up, high_up = pltpu.roll(low, 1, 1), pltpu.roll(high, 1, 1)
        low_down, high_down = pltpu.roll(low, LANES - 1, 1), pltpu.roll(high, LANES - 1, 1)
        low_side = jnp.where(first, 0.0, low_up) + jnp.where(last, high_down, low_down)
        high_side = jnp.where(first, low_up, high_up) + jnp.where(last, 0.0, high_down)
        low_next = pltpu.roll(low, 1, 0) + pltpu.roll(low, ROWS - 1, 0)
        high_next = pltpu.roll(high, 1, 0) + pltpu.roll(high, ROWS - 1, 0)
        low = low + diffusion * (low_next + low_side - 4.0 * low)
        high = high + diffusion * (high_next + high_side - 4.0 * high)
    return jnp.where(row < half, low, pltpu.roll(high, half, 0))


def product(group, step, share, splat_ref, field_ref, part_ref, out_ref):
    members, modes = field_ref.shape[:2]
    slots = part_ref.shape[1]
    owner = target_of(lax.axis_index("mem"), group, step)
    pair = 2 * ROWS
    for j in range(share // 2):
        level = owner * share + 2 * j
        start = pl.multiple_of(level * ROWS, pair)
        localized = []
        for k in range(members):
            halves = []
            for h in range(2):
                value = splat_ref[level + h, 0] * field_ref[k, 0]
                for m in range(1, modes):
                    value = value + splat_ref[level + h, m] * field_ref[k, m]
                halves.append(value)
            localized.append(jnp.concatenate(halves, axis=0))
        for t in range(slots):
            total = None
            for k in range(members):
                term = localized[k] * part_ref[k, t, pl.ds(start, pair), :].astype(jnp.float32)
                total = term if total is None else total + term
            out_ref[t, pl.ds(2 * j * ROWS, pair), :] = total


def smooth_kernel(group, step, share, mask_ref, own_ref, other_ref, splat_ref, part_ref, field_ref, out_ref):
    members, modes = own_ref.shape[:2]
    for k in range(members):
        for m in range(modes):
            field_ref[k, m] = smoothed_pair(own_ref[k, m], other_ref[k, m]) * mask_ref[m]
    product(group, step, share, splat_ref, field_ref, part_ref, out_ref)


def mask_kernel(group, step, share, mask_ref, own_ref, splat_ref, part_ref, field_ref, out_ref):
    members, modes = own_ref.shape[:2]
    for k in range(members):
        for m in range(modes):
            field_ref[k, m] = own_ref[k, m] * mask_ref[m]
    product(group, step, share, splat_ref, field_ref, part_ref, out_ref)


def gather_kernel(norm_factor, *refs):
    *arrived, slots_ref, total_ref = refs
    slots = slots_ref.shape[0]
    whole = None
    for t in range(slots):
        value = arrived[0][t]
        for ref in arrived[1:]:
            value = value + ref[t]
        value = value * norm_factor
        slots_ref[t] = value
        whole = value if whole is None else whole + value
    total_ref[...] = whole


def blend_kernel(factor_ref, slots_ref, *refs):
    *arrived, out_ref = refs
    windows, slots = factor_ref.shape[:2]
    height = slots_ref.shape[1]
    stage = lax.axis_index("tm")
    for r in range(0, height, ROWS):
        rows = slice(r, r + ROWS)
        earlier = None
        for step, ref in enumerate(arrived, 1):
            value = ref[rows] * jnp.where(stage >= step, 1.0, 0.0)
            earlier = value if earlier is None else earlier + value
        for w in range(windows):
            mixed = earlier
            for t in range(slots):
                term = factor_ref[w, t] * slots_ref[t, rows]
                mixed = term if mixed is None else mixed + term
            out_ref[w, rows] = mixed


def place_kernel(height, whole_ref, out_ref, sems):
    owners, windows = whole_ref.shape[:2]
    copies = []
    for i in range(owners):
        for w in range(windows):
            copies.append(
                pltpu.make_async_copy(
                    whole_ref.at[i, w], out_ref.at[w, pl.ds(i * height, height)], sems.at[i, w]
                )
            )
    for copy in copies:
        copy.start()
    for copy in copies:
        copy.wait()


VMEM_SPEC = pl.BlockSpec(memory_space=pltpu.VMEM)
HBM_SPEC = pl.BlockSpec(memory_space=pltpu.HBM)


def call(kernel, arrays, out_shape, cost):
    return pl.pallas_call(
        kernel,
        in_specs=[VMEM_SPEC] * len(arrays),
        out_specs=jax.tree.map(lambda _: VMEM_SPEC, out_shape),
        out_shape=out_shape,
        compiler_params=pltpu.CompilerParams(vmem_limit_bytes=16 * 1024 * 1024),
        cost_estimate=pl.CostEstimate(flops=cost, bytes_accessed=cost, transcendentals=0),
    )(*arrays)


def per_device(control, vertical_modes, mode_counts, perturbations, slot_index, blend_weight):
    members, slot_count, levels, x, y = perturbations.shape
    modes = vertical_modes.shape[1]
    windows = slot_index.shape[0]
    group = lax.axis_size("mem")
    stages = lax.axis_size("tm")
    share = levels // group
    height = share * ROWS
    norm_factor = 1.0 / math.sqrt(members * group - 1)
    f32 = lambda *shape: jax.ShapeDtypeStruct(shape, jnp.float32)
    parts = view(perturbations)
    own = view(control[:, :, None])

    room = parts.size * parts.dtype.itemsize + levels * modes * ROWS * LANES * 4

    loaded, parts, splats, masks, factors = pl.pallas_call(
        functools.partial(load_kernel, x),
        in_specs=[HBM_SPEC] * 6,
        out_specs=[VMEM_SPEC] * 5,
        out_shape=[
            pltpu.VMEM(own.shape, jnp.float32),
            pltpu.VMEM(parts.shape, parts.dtype),
            pltpu.VMEM((levels, modes, ROWS, LANES), jnp.float32),
            pltpu.VMEM((modes, ROWS, LANES), jnp.float32),
            pltpu.VMEM((windows, slot_count, ROWS, LANES), jnp.float32),
        ],
        scratch_shapes=[
            pltpu.SMEM((modes, levels), jnp.float32),
            pltpu.SMEM(mode_counts.shape, jnp.int32),
            pltpu.SMEM(slot_index.shape, jnp.int32),
            pltpu.SMEM(blend_weight.shape, jnp.float32),
            pltpu.SemaphoreType.DMA((6,)),
        ],
        compiler_params=pltpu.CompilerParams(vmem_limit_bytes=VMEM_BYTES - 2 * room),
        cost_estimate=pl.CostEstimate(flops=1000000, bytes_accessed=4000000, transcendentals=0),
    )(vertical_modes.T, mode_counts, slot_index, blend_weight, own, parts)

    def shape_of():
        return f32(slot_count, height, LANES)

    field_shape = f32(members, modes, ROWS, LANES)
    if lax.axis_size("tile") == 2 and x == SMOOTH:
        other = lax.ppermute(control, "tile", ring(2, 1))
        field, first = call(
            functools.partial(smooth_kernel, group, group - 1, share),
            [masks, loaded, view(other[:, :, None]), splats, parts],
            [field_shape, shape_of()],
            2000000,
        )
    else:
        field, first = call(
            functools.partial(mask_kernel, group, group - 1, share),
            [masks, view(smooth(control)[:, :, None]), splats, parts],
            [field_shape, shape_of()],
            2000000,
        )

    def terms(step):
        return call(
            functools.partial(product, group, step, share),
            [splats, field, parts],
            shape_of(),
            1000000,
        )

    arrived = []
    for step in range(group - 1, 0, -1):
        part = first if step == group - 1 else terms(step)
        arrived.append(lax.ppermute(part, "mem", pairing(group, step)))
    slots, total = call(
        functools.partial(gather_kernel, norm_factor),
        [terms(0) if group > 1 else first] + arrived,
        [shape_of(), f32(height, LANES)],
        1000000,
    )

    came = [lax.ppermute(total, "tm", ring(stages, step)) for step in range(1, stages)]
    blended = call(
        blend_kernel, [factors, slots] + came, f32(windows, height, LANES), 1000000
    )
    whole = lax.all_gather(blended, "mem", axis=0, tiled=False)
    placed = pl.pallas_call(
        functools.partial(place_kernel, height),
        in_specs=[VMEM_SPEC],
        out_specs=HBM_SPEC,
        out_shape=f32(windows, levels * ROWS, LANES),
        scratch_shapes=[pltpu.SemaphoreType.DMA((group, windows))],
        compiler_params=pltpu.CompilerParams(vmem_limit_bytes=16 * 1024 * 1024),
    )(whole)
    return unview(placed, x, y)


def solution(mesh):
    placed = (
        P("mem", None, "tile", None),
        P(),
        P("tile"),
        P("mem", "tm", None, "tile", None),
        P("tm"),
        P("tm"),
    )
    return jax.shard_map(
        per_device,
        mesh=mesh,
        in_specs=placed,
        out_specs=P("tm", None, "tile", None),
        check_vma=False,
    )
```

time: 44.7 us -> 36.6 us (0.82)
  waiting for transfers between devices: 0.02 us -> 11.7 us
  between operations: 11.5 us -> 0.04 us
  other arithmetic: 5.92 us -> 0 us
  local copies, waits for them, and re-layouts: 5.11 us -> 0 us
  Pallas kernels: 0 us -> 4.25 us
  starting transfers between devices: 10.6 us -> 9.42 us
    ppermute x7, waiting for transfers between devices: 0.02 us -> 11.7 us  [the longest x3 6.49 us: per_device(): arrived.append(lax.ppermute(part, 'mem', pairing(group, step)))]
    pallas_call x0 -> x8, Pallas kernels: none -> 4.25 us  [the longest x1 1.84 us: per_device(): pl.pallas_call(functools.partial(load_kernel, x), in_specs=[HBM_SPEC] * 6...]
    slice x10 -> x0, local copies, waits for them, and re-layouts: 2.35 us -> none  [the longest x8 1.08 us: relax(): neighbours = jnp.roll(field, -1, axis=2) + jnp.roll(field, 1, axis=2)]
    concatenate x2 -> x0, other arithmetic: 1.96 us -> none  [smooth(): wide, start = (jnp.concatenate([field, other], axis=2), 0)]
    unnamed x7 -> x0, local copies, waits for them, and re-layouts: 1.85 us -> none
    reduce_sum x2 -> x0, other arithmetic: 1.63 us -> none  [the longest x1 1.54 us: terms(): return jnp.sum(localized[:, None] * part.astype(jnp.float32), axis=0)]
    add x5 -> x0, other arithmetic: 1.44 us -> none  [the longest x1 0.76 us: terms(): sum((modes[:, m][None, :, None, None] * masked[m][:, None] for m in range...]
    ppermute x7, starting transfers between devices: 10.6 us -> 9.42 us  [the longest x3 4.82 us: per_device(): lax.ppermute(total, 'tm', ring(stages, step))]
  transfers between devices with their start and end apart: 7 -> 7, of which waited for: 0 -> 5; matrix products, arithmetic and copies ran while one was open for 8% -> 0% of each run, Pallas kernels for 0% -> 6%
where the time goes in v2:
time: 36.6 us; the launch traced here: 36.4 us
  waiting for transfers between devices  11.7 us (32%)
  blocking collectives  11 us (30%)
  starting transfers between devices  9.42 us (26%)
  Pallas kernels  4.25 us (12%)
    all_gather x1, blocking collectives, per_device(): whole = lax.all_gather(blended, 'mem', axis=0, tiled=False)  11 us
    ppermute x3, waiting for transfers between devices, per_device(): arrived.append(lax.ppermute(part, 'mem', pairing(group, step)))  6.49 us
    ppermute x3, waiting for transfers between devices, per_device(): lax.ppermute(total, 'tm', ring(stages, step))  5.19 us
    ppermute x3, starting transfers between devices, per_device(): lax.ppermute(total, 'tm', ring(stages, step))  4.82 us
    ppermute x3, starting transfers between devices, per_device(): arrived.append(lax.ppermute(part, 'mem', pairing(group, step)))  4.11 us
    pallas_call x1, Pallas kernels, per_device(): pl.pallas_call(functools.partial(load_kernel, x), in_specs=[HBM_SPEC] * 6...  1.84 us
    pallas_call x6, Pallas kernels, call(): pl.pallas_call(kernel, in_specs=[VMEM_SPEC] * len(arrays), out_specs=jax....  1.44 us
    pallas_call x1, Pallas kernels, per_device(): pl.pallas_call(functools.partial(place_kernel, height), in_specs=[VMEM_SP...  0.97 us
  transfers between devices with their start and end apart: 7, of which 5 were waited for; matrix products, arithmetic and copies ran while one was open for 0% of the time, Pallas kernels for 6%

profile of v2, /device:TPU:0, one launch (start us, length us, event | category | flops | bytes accessed | tf_op | source)
XLA Modules:
  0.0 36.4 jit_solution(12807781038112949221)
XLA Ops:
  0.0 0.5 %collective-permute-start = (f32[10,2,4,256]{3,2,1,0:T(4,128)}, f32[10,2,4,256]{3,2,1,0:T(4,128)S(1)}, u32[]{:S(2)}, u32[]{:S(2)}) collective-permute-start(f32[10,2,4,256]{3,2,1,0:T(4,128)} %param.6), channel_id=1, source_target_pairs={{0,1},{1,0},{2,3},{3,2},{4,5},{5,4},{6,7},{7,6},{8,9},{9,8},{10,11... | collective-permute-start | bytes 245768 | tf_op jit(solution)/shard_map/ppermute | solution.py:285
  0.5 1.8 %shard_map.64 = (f32[10,2,8,128]{3,2,1,0:T(8,128)S(1)}, bf16[10,2,512,128]{3,2,1,0:T(8,128)(2,1)S(1)}, f32[64,2,8,128]{3,2,1,0:T(8,128)S(1)}, f32[2,8,128]{2,1,0:T(8,128)S(1)}, f32[3,2,8,128]{3,2,1,0:T(8,128)S(1)}) custom-call(f32[2,64]{1,0:T(2,128)} %bitcast.26, s32[4]{0:T(128)} %counts_hbm.1, s32[3]{0:T(128)} %index_hbm.1, f32[3]{0:T(128)} %weight_hbm.1, ...), custom_call_target="tpu_custom_call" | custom-call | flops 1000000 | bytes 4000000 | tf_op jit(solution)/shard_map/pallas_call | solution.py:258
  2.3 0.0 collective-permute-done
  2.4 0.7 %shard_map.65 = (f32[10,2,8,128]{3,2,1,0:T(8,128)S(1)}, f32[2,128,128]{2,1,0:T(8,128)S(1)}) custom-call(f32[2,8,128]{2,1,0:T(8,128)S(1)} %get-tuple-element.16.mask_ref, f32[10,2,8,128]{3,2,1,0:T(8,128)S(1)} %get-tuple-element.17.own_ref, f32[10,2,8,128]{3,2,1,0:T(8,128)S(1)} %bitcast.23, f32[64,2,8,128]{3,2,1,0:T(8,128)S(1)} %get-tuple-element.15.splat_ref, ...), custom_call_target="tpu_custom_call" | custom-call | flops 2000000 | bytes 2000000 | tf_op jit(solution)/shard_map/pallas_call | solution.py:233
  3.1 0.2 shard_map.68
  3.3 0.2 shard_map.67
  3.5 2.6 %collective-permute-start.2 = (f32[2,128,128]{2,1,0:T(8,128)S(1)}, f32[2,128,128]{2,1,0:T(8,128)S(1)}, u32[]{:S(2)}, u32[]{:S(2)}) collective-permute-start(f32[2,128,128]{2,1,0:T(8,128)S(1)} %shard_map.67), channel_id=1, source_target_pairs={{0,4},{2,6},{4,0},{6,2},{1,5},{3,7},{5,1},{7,3},{8,12},{10,14},{12... | collective-permute-start | bytes 393224 | tf_op jit(solution)/shard_map/ppermute | solution.py:311
  6.1 1.5 %collective-permute-start.3 = (f32[2,128,128]{2,1,0:T(8,128)S(1)}, f32[2,128,128]{2,1,0:T(8,128)S(1)}, u32[]{:S(2)}, u32[]{:S(2)}) collective-permute-start(f32[2,128,128]{2,1,0:T(8,128)S(1)} %shard_map.68), channel_id=1, source_target_pairs={{0,2},{2,0},{4,6},{6,4},{1,3},{3,1},{5,7},{7,5},{8,10},{10,8},{12,... | collective-permute-start | bytes 393224 | tf_op jit(solution)/shard_map/ppermute | solution.py:311
  7.6 0.0 collective-permute-start.1
  7.6 0.2 shard_map.66.refs_0_
  7.8 2.4 %collective-permute-done.2.refs_2_ = f32[2,128,128]{2,1,0:T(8,128)S(1)} collective-permute-done((f32[2,128,128]{2,1,0:T(8,128)S(1)}, f32[2,128,128]{2,1,0:T(8,128)S(1)}, u32[]{:S(2)}, u32[]{:S(2)}) %collective-permute-start.2) | collective-permute-done | bytes 131104 | tf_op jit(solution)/shard_map/ppermute | solution.py:311
  10.3 2.2 %collective-permute-done.3.refs_3_ = f32[2,128,128]{2,1,0:T(8,128)S(1)} collective-permute-done((f32[2,128,128]{2,1,0:T(8,128)S(1)}, f32[2,128,128]{2,1,0:T(8,128)S(1)}, u32[]{:S(2)}, u32[]{:S(2)}) %collective-permute-start.3) | collective-permute-done | bytes 131104 | tf_op jit(solution)/shard_map/ppermute | solution.py:311
  12.5 1.9 %collective-permute-done.1.refs_1_ = f32[2,128,128]{2,1,0:T(8,128)S(1)} collective-permute-done((f32[2,128,128]{2,1,0:T(8,128)S(1)}, f32[2,128,128]{2,1,0:T(8,128)S(1)}, u32[]{:S(2)}, u32[]{:S(2)}) %collective-permute-start.1) | collective-permute-done | bytes 131104 | tf_op jit(solution)/shard_map/ppermute | solution.py:311
  14.4 3.8 %collective-permute-start.6 = (f32[128,128]{1,0:T(8,128)S(1)}, f32[128,128]{1,0:T(8,128)S(1)}, u32[]{:S(2)}, u32[]{:S(2)}) collective-permute-start(f32[128,128]{1,0:T(8,128)S(1)} %get-tuple-element.22), channel_id=1, source_target_pairs={{0,24},{8,0},{16,8},{24,16},{1,25},{9,1},{17,9},{25,17},{2,26},{10... | collective-permute-start | bytes 196616 | tf_op jit(solution)/shard_map/ppermute | solution.py:319
  18.2 0.0 collective-permute-start.5
  18.2 1.0 %collective-permute-start.4 = (f32[128,128]{1,0:T(8,128)S(1)}, f32[128,128]{1,0:T(8,128)S(1)}, u32[]{:S(2)}, u32[]{:S(2)}) collective-permute-start(f32[128,128]{1,0:T(8,128)S(1)} %get-tuple-element.22), channel_id=1, source_target_pairs={{0,8},{8,16},{16,24},{24,0},{1,9},{9,17},{17,25},{25,1},{2,10},{10... | collective-permute-start | bytes 196616 | tf_op jit(solution)/shard_map/ppermute | solution.py:319
  19.2 1.4 %collective-permute-done.6.refs_2_ = f32[128,128]{1,0:T(8,128)S(1)} collective-permute-done((f32[128,128]{1,0:T(8,128)S(1)}, f32[128,128]{1,0:T(8,128)S(1)}, u32[]{:S(2)}, u32[]{:S(2)}) %collective-permute-start.6) | collective-permute-done | bytes 65568 | tf_op jit(solution)/shard_map/ppermute | solution.py:319
  20.6 3.8 %collective-permute-done.5.refs_1_ = f32[128,128]{1,0:T(8,128)S(1)} collective-permute-done((f32[128,128]{1,0:T(8,128)S(1)}, f32[128,128]{1,0:T(8,128)S(1)}, u32[]{:S(2)}, u32[]{:S(2)}) %collective-permute-start.5) | collective-permute-done | bytes 65568 | tf_op jit(solution)/shard_map/ppermute | solution.py:319
  24.4 0.0 collective-permute-done.4.refs_0_
  24.4 0.1 shard_map.70
  24.4 11.0 %all-gather = f32[12,128,128]{2,1,0:T(8,128)S(1)} all-gather(f32[3,128,128]{2,1,0:T(8,128)S(1)} %shard_map.70), channel_id=2, replica_groups=mesh['tm'=4,'mem'=4,'tile'=2] {'mem'}, dimensions={0}, use_global_device_ids=true | all-gather | bytes 983040 | tf_op jit(solution)/shard_map/all_gather | solution.py:323
  35.4 1.0 %shard_map.71 = f32[3,512,128]{2,1,0:T(8,128)} custom-call(f32[4,3,128,128]{3,2,1,0:T(8,128)S(1)} %bitcast.22), custom_call_target="tpu_custom_call" | custom-call | tf_op jit(solution)/shard_map/pallas_call | solution.py:324
  (1 shorter events, 0.0 us)
Async XLA Ops:
  0.0 2.3 %collective-permute-start = (f32[10,2,4,256]{3,2,1,0:T(4,128)}, f32[10,2,4,256]{3,2,1,0:T(4,128)S(1)}, u32[]{:S(2)}, u32[]{:S(2)}) collective-permute-start(f32[10,2,4,256]{3,2,1,0:T(4,128)} %param.6), channel_id=1, source_target_pairs={{0,1},{1,0},{2,3},{3,2},{4,5},{5,4},{6,7},{7,6},{8,9},{9,8},{10,11... | collective-permute-start | bytes 245768 | tf_op jit(solution)/shard_map/ppermute | solution.py:285
  3.5 6.7 %collective-permute-start.2 = (f32[2,128,128]{2,1,0:T(8,128)S(1)}, f32[2,128,128]{2,1,0:T(8,128)S(1)}, u32[]{:S(2)}, u32[]{:S(2)}) collective-permute-start(f32[2,128,128]{2,1,0:T(8,128)S(1)} %shard_map.67), channel_id=1, source_target_pairs={{0,4},{2,6},{4,0},{6,2},{1,5},{3,7},{5,1},{7,3},{8,12},{10,14},{12... | collective-permute-start | bytes 393224 | tf_op jit(solution)/shard_map/ppermute | solution.py:311
  6.1 6.4 %collective-permute-start.3 = (f32[2,128,128]{2,1,0:T(8,128)S(1)}, f32[2,128,128]{2,1,0:T(8,128)S(1)}, u32[]{:S(2)}, u32[]{:S(2)}) collective-permute-start(f32[2,128,128]{2,1,0:T(8,128)S(1)} %shard_map.68), channel_id=1, source_target_pairs={{0,2},{2,0},{4,6},{6,4},{1,3},{3,1},{5,7},{7,5},{8,10},{10,8},{12,... | collective-permute-start | bytes 393224 | tf_op jit(solution)/shard_map/ppermute | solution.py:311
  7.6 6.7 %collective-permute-start.1 = (f32[2,128,128]{2,1,0:T(8,128)S(1)}, f32[2,128,128]{2,1,0:T(8,128)S(1)}, u32[]{:S(2)}, u32[]{:S(2)}) collective-permute-start(f32[2,128,128]{2,1,0:T(8,128)S(1)} %get-tuple-element.20), channel_id=1, source_target_pairs={{0,6},{2,4},{4,2},{6,0},{1,7},{3,5},{5,3},{7,1},{8,14},{10,12},{12... | collective-permute-start | bytes 393224 | tf_op jit(solution)/shard_map/ppermute | solution.py:311
  14.4 6.2 %collective-permute-start.6 = (f32[128,128]{1,0:T(8,128)S(1)}, f32[128,128]{1,0:T(8,128)S(1)}, u32[]{:S(2)}, u32[]{:S(2)}) collective-permute-start(f32[128,128]{1,0:T(8,128)S(1)} %get-tuple-element.22), channel_id=1, source_target_pairs={{0,24},{8,0},{16,8},{24,16},{1,25},{9,1},{17,9},{25,17},{2,26},{10... | collective-permute-start | bytes 196616 | tf_op jit(solution)/shard_map/ppermute | solution.py:319
  18.2 6.2 %collective-permute-start.5 = (f32[128,128]{1,0:T(8,128)S(1)}, f32[128,128]{1,0:T(8,128)S(1)}, u32[]{:S(2)}, u32[]{:S(2)}) collective-permute-start(f32[128,128]{1,0:T(8,128)S(1)} %get-tuple-element.22), channel_id=1, source_target_pairs={{0,16},{8,24},{16,0},{24,8},{1,17},{9,25},{17,1},{25,9},{2,18},{10... | collective-permute-start | bytes 196616 | tf_op jit(solution)/shard_map/ppermute | solution.py:319
  18.2 6.2 %collective-permute-start.4 = (f32[128,128]{1,0:T(8,128)S(1)}, f32[128,128]{1,0:T(8,128)S(1)}, u32[]{:S(2)}, u32[]{:S(2)}) collective-permute-start(f32[128,128]{1,0:T(8,128)S(1)} %get-tuple-element.22), channel_id=1, source_target_pairs={{0,8},{8,16},{16,24},{24,0},{1,9},{9,17},{17,25},{25,1},{2,10},{10... | collective-permute-start | bytes 196616 | tf_op jit(solution)/shard_map/ppermute | solution.py:319

commit v3 on v2

--- a/solution.py
+++ b/solution.py
@@ -135,7 +135,7 @@
     return jnp.where(row < half, low, pltpu.roll(high, half, 0))
 
 
-def product(group, step, share, splat_ref, field_ref, part_ref, out_ref):
+def product(group, step, share, splat_ref, field_ref, part_ref, total_ref, lead_ref):
     members, modes = field_ref.shape[:2]
     slots = part_ref.shape[1]
     owner = target_of(lax.axis_index("mem"), group, step)
@@ -152,48 +152,46 @@
                     value = value + splat_ref[level + h, m] * field_ref[k, m]
                 halves.append(value)
             localized.append(jnp.concatenate(halves, axis=0))
+        whole = None
         for t in range(slots):
             total = None
             for k in range(members):
                 term = localized[k] * part_ref[k, t, pl.ds(start, pair), :].astype(jnp.float32)
                 total = term if total is None else total + term
-            out_ref[t, pl.ds(2 * j * ROWS, pair), :] = total
-
-
-def smooth_kernel(group, step, share, mask_ref, own_ref, other_ref, splat_ref, part_ref, field_ref, out_ref):
+            if t < slots - 1:
+                lead_ref[t, pl.ds(2 * j * ROWS, pair), :] = total
+            whole = total if whole is None else whole + total
+        total_ref[pl.ds(2 * j * ROWS, pair), :] = whole
+
+
+def smooth_kernel(group, step, share, mask_ref, own_ref, other_ref, splat_ref, part_ref, field_ref, total_ref, lead_ref):
     members, modes = own_ref.shape[:2]
     for k in range(members):
         for m in range(modes):
             field_ref[k, m] = smoothed_pair(own_ref[k, m], other_ref[k, m]) * mask_ref[m]
-    product(group, step, share, splat_ref, field_ref, part_ref, out_ref)
-
-
-def mask_kernel(group, step, share, mask_ref, own_ref, splat_ref, part_ref, field_ref, out_ref):
+    product(group, step, share, splat_ref, field_ref, part_ref, total_ref, lead_ref)
+
+
+def mask_kernel(group, step, share, mask_ref, own_ref, splat_ref, part_ref, field_ref, total_ref, lead_ref):
     members, modes = own_ref.shape[:2]
     for k in range(members):
         for m in range(modes):
             field_ref[k, m] = own_ref[k, m] * mask_ref[m]
-    product(group, step, share, splat_ref, field_ref, part_ref, out_ref)
+    product(group, step, share, splat_ref, field_ref, part_ref, total_ref, lead_ref)
 
 
 def gather_kernel(norm_factor, *refs):
-    *arrived, slots_ref, total_ref = refs
-    slots = slots_ref.shape[0]
-    whole = None
-    for t in range(slots):
-        value = arrived[0][t]
-        for ref in arrived[1:]:
-            value = value + ref[t]
-        value = value * norm_factor
-        slots_ref[t] = value
-        whole = value if whole is None else whole + value
-    total_ref[...] = whole
-
-
-def blend_kernel(factor_ref, slots_ref, *refs):
     *arrived, out_ref = refs
+    value = arrived[0][...]
+    for ref in arrived[1:]:
+        value = value + ref[...]
+    out_ref[...] = value * norm_factor
+
+
+def blend_kernel(norm_factor, parts, factor_ref, total_ref, *refs):
+    leads, arrived, out_ref = refs[:parts], refs[parts:-1], refs[-1]
     windows, slots = factor_ref.shape[:2]
-    height = slots_ref.shape[1]
+    height = total_ref.shape[0]
     stage = lax.axis_index("tm")
     for r in range(0, height, ROWS):
         rows = slice(r, r + ROWS)
@@ -201,10 +199,18 @@
         for step, ref in enumerate(arrived, 1):
             value = ref[rows] * jnp.where(stage >= step, 1.0, 0.0)
             earlier = value if earlier is None else earlier + value
+        values, rest = [], total_ref[rows]
+        for t in range(slots - 1):
+            value = leads[0][t, rows]
+            for ref in leads[1:]:
+                value = value + ref[t, rows]
+            values.append(value * norm_factor)
+            rest = rest - values[-1]
+        values.append(rest)
         for w in range(windows):
             mixed = earlier
             for t in range(slots):
-                term = factor_ref[w, t] * slots_ref[t, rows]
+                term = factor_ref[w, t] * values[t]
                 mixed = term if mixed is None else mixed + term
             out_ref[w, rows] = mixed
 
@@ -277,48 +283,48 @@
         cost_estimate=pl.CostEstimate(flops=1000000, bytes_accessed=4000000, transcendentals=0),
     )(vertical_modes.T, mode_counts, slot_index, blend_weight, own, parts)
 
-    def shape_of():
-        return f32(slot_count, height, LANES)
-
+    shapes = [f32(height, LANES), f32(slot_count - 1, height, LANES)]
     field_shape = f32(members, modes, ROWS, LANES)
     if lax.axis_size("tile") == 2 and x == SMOOTH:
         other = lax.ppermute(control, "tile", ring(2, 1))
-        field, first = call(
+        field, *first = call(
             functools.partial(smooth_kernel, group, group - 1, share),
             [masks, loaded, view(other[:, :, None]), splats, parts],
-            [field_shape, shape_of()],
+            [field_shape] + shapes,
             2000000,
         )
     else:
-        field, first = call(
+        field, *first = call(
             functools.partial(mask_kernel, group, group - 1, share),
             [masks, view(smooth(control)[:, :, None]), splats, parts],
-            [field_shape, shape_of()],
+            [field_shape] + shapes,
             2000000,
         )
 
-    def terms(step):
-        return call(
+    products = {group - 1: first}
+    for step in range(group - 1):
+        products[step] = call(
             functools.partial(product, group, step, share),
             [splats, field, parts],
-            shape_of(),
+            shapes,
             1000000,
         )
 
-    arrived = []
+    totals, leads = [products[0][0]], [products[0][1]]
     for step in range(group - 1, 0, -1):
-        part = first if step == group - 1 else terms(step)
-        arrived.append(lax.ppermute(part, "mem", pairing(group, step)))
-    slots, total = call(
-        functools.partial(gather_kernel, norm_factor),
-        [terms(0) if group > 1 else first] + arrived,
-        [shape_of(), f32(height, LANES)],
+        totals.append(lax.ppermute(products[step][0], "mem", pairing(group, step)))
+    for step in range(group - 1, 0, -1):
+        leads.append(lax.ppermute(products[step][1], "mem", pairing(group, step)))
+    total = call(functools.partial(gather_kernel, norm_factor), totals, f32(height, LANES), 1000000)
+
+    came = []
+    for step in range(1, stages):
+        came.append(lax.ppermute(total, "tm", ring(stages, step)))
+    blended = call(
+        functools.partial(blend_kernel, norm_factor, len(leads)),
+        [factors, total] + leads + came,
+        f32(windows, height, LANES),
         1000000,
-    )
-
-    came = [lax.ppermute(total, "tm", ring(stages, step)) for step in range(1, stages)]
-    blended = call(
-        blend_kernel, [factors, slots] + came, f32(windows, height, LANES), 1000000
     )
     whole = lax.all_gather(blended, "mem", axis=0, tiled=False)
     placed = pl.pallas_call(

time: 36.6 us -> 35.7 us (0.975)
  waiting for transfers between devices: 11.7 us -> 6.91 us
  starting transfers between devices: 9.42 us -> 12.2 us
  blocking collectives: 11 us -> 12.1 us
    ppermute x6 -> x9, waiting for transfers between devices: 11.7 us -> 6.91 us  [the longest x3 5.05 us: per_device(): came.append(lax.ppermute(total, 'tm', ring(stages, step)))]
    ppermute x6 -> x9, starting transfers between devices: 8.93 us -> 11.7 us  [the longest x3 4.21 us: per_device(): totals.append(lax.ppermute(products[step][0], 'mem', pairing(group, step)))]
    all_gather x1, blocking collectives: 11 us -> 12.1 us  [per_device(): whole = lax.all_gather(blended, 'mem', axis=0, tiled=False)]
  transfers between devices with their start and end apart: 7 -> 10, of which waited for: 5 -> 4; matrix products, arithmetic and copies ran while one was open for 0% -> 0% of each run, Pallas kernels for 6% -> 7%
where the time goes in v3:
time: 35.7 us; the launch traced here: 35.6 us
  starting transfers between devices  12.2 us (34%)
  blocking collectives  12.1 us (34%)
  waiting for transfers between devices  6.91 us (19%)
  Pallas kernels  4.25 us (12%)
    all_gather x1, blocking collectives, per_device(): whole = lax.all_gather(blended, 'mem', axis=0, tiled=False)  12.1 us
    ppermute x3, waiting for transfers between devices, per_device(): came.append(lax.ppermute(total, 'tm', ring(stages, step)))  5.05 us
    ppermute x3, starting transfers between devices, per_device(): totals.append(lax.ppermute(products[step][0], 'mem', pairing(group, step)))  4.21 us
    ppermute x3, starting transfers between devices, per_device(): came.append(lax.ppermute(total, 'tm', ring(stages, step)))  3.93 us
    ppermute x3, starting transfers between devices, per_device(): leads.append(lax.ppermute(products[step][1], 'mem', pairing(group, step)))  3.58 us
    ppermute x3, waiting for transfers between devices, per_device(): totals.append(lax.ppermute(products[step][0], 'mem', pairing(group, step)))  1.86 us
    pallas_call x1, Pallas kernels, per_device(): pl.pallas_call(functools.partial(load_kernel, x), in_specs=[HBM_SPEC] * 6...  1.84 us
    pallas_call x6, Pallas kernels, call(): pl.pallas_call(kernel, in_specs=[VMEM_SPEC] * len(arrays), out_specs=jax....  1.44 us
  transfers between devices with their start and end apart: 10, of which 4 were waited for; matrix products, arithmetic and copies ran while one was open for 0% of the time, Pallas kernels for 7%

profile of v3, /device:TPU:0, one launch (start us, length us, event | category | flops | bytes accessed | tf_op | source)
XLA Modules:
  0.0 35.6 jit_solution(14013633749677702644)
XLA Ops:
  0.0 0.5 %collective-permute-start = (f32[10,2,4,256]{3,2,1,0:T(4,128)}, f32[10,2,4,256]{3,2,1,0:T(4,128)S(1)}, u32[]{:S(2)}, u32[]{:S(2)}) collective-permute-start(f32[10,2,4,256]{3,2,1,0:T(4,128)} %param.6), channel_id=1, source_target_pairs={{0,1},{1,0},{2,3},{3,2},{4,5},{5,4},{6,7},{7,6},{8,9},{9,8},{10,11... | collective-permute-start | bytes 245768 | tf_op jit(solution)/shard_map/ppermute | solution.py:289
  0.5 1.8 %shard_map.64 = (f32[10,2,8,128]{3,2,1,0:T(8,128)S(1)}, bf16[10,2,512,128]{3,2,1,0:T(8,128)(2,1)S(1)}, f32[64,2,8,128]{3,2,1,0:T(8,128)S(1)}, f32[2,8,128]{2,1,0:T(8,128)S(1)}, f32[3,2,8,128]{3,2,1,0:T(8,128)S(1)}) custom-call(f32[2,64]{1,0:T(2,128)} %bitcast.26, s32[4]{0:T(128)} %counts_hbm.1, s32[3]{0:T(128)} %index_hbm.1, f32[3]{0:T(128)} %weight_hbm.1, ...), custom_call_target="tpu_custom_call" | custom-call | flops 1000000 | bytes 4000000 | tf_op jit(solution)/shard_map/pallas_call | solution.py:264
  2.3 0.0 collective-permute-done
  2.4 0.8 %shard_map.65 = (f32[10,2,8,128]{3,2,1,0:T(8,128)S(1)}, f32[128,128]{1,0:T(8,128)S(1)}, f32[1,128,128]{2,1,0:T(8,128)S(1)}) custom-call(f32[2,8,128]{2,1,0:T(8,128)S(1)} %get-tuple-element.21.mask_ref, f32[10,2,8,128]{3,2,1,0:T(8,128)S(1)} %get-tuple-element.22.own_ref, f32[10,2,8,128]{3,2,1,0:T(8,128)S(1)} %bitcast.23, ...), custom_call_target="tpu_custom_call" | custom-call | flops 2000000 | bytes 2000000 | tf_op jit(solution)/shard_map/pallas_call | solution.py:239
  3.1 3.5 %collective-permute-start.1 = (f32[128,128]{1,0:T(8,128)S(1)}, f32[128,128]{1,0:T(8,128)S(1)}, u32[]{:S(2)}, u32[]{:S(2)}) collective-permute-start(f32[128,128]{1,0:T(8,128)S(1)} %get-tuple-element.26), channel_id=1, source_target_pairs={{0,6},{2,4},{4,2},{6,0},{1,7},{3,5},{5,3},{7,1},{8,14},{10,12},{12... | collective-permute-start | bytes 196616 | tf_op jit(solution)/shard_map/ppermute | solution.py:315
  6.6 0.2 shard_map.68
  6.8 0.6 %collective-permute-start.3 = (f32[128,128]{1,0:T(8,128)S(1)}, f32[128,128]{1,0:T(8,128)S(1)}, u32[]{:S(2)}, u32[]{:S(2)}) collective-permute-start(f32[128,128]{1,0:T(8,128)S(1)} %get-tuple-element.28), channel_id=1, source_target_pairs={{0,2},{2,0},{4,6},{6,4},{1,3},{3,1},{5,7},{7,5},{8,10},{10,8},{12,... | collective-permute-start | bytes 196616 | tf_op jit(solution)/shard_map/ppermute | solution.py:315
  7.4 0.2 shard_map.67
  7.6 0.1 collective-permute-start.2
  7.7 2.9 %collective-permute-start.4 = (f32[1,128,128]{2,1,0:T(8,128)S(1)}, f32[1,128,128]{2,1,0:T(8,128)S(1)}, u32[]{:S(2)}, u32[]{:S(2)}) collective-permute-start(f32[1,128,128]{2,1,0:T(8,128)S(1)} %get-tuple-element.30), channel_id=1, source_target_pairs={{0,6},{2,4},{4,2},{6,0},{1,7},{3,5},{5,3},{7,1},{8,14},{10,12},{12... | collective-permute-start | bytes 196616 | tf_op jit(solution)/shard_map/ppermute | solution.py:317
  10.6 0.5 %collective-permute-start.6 = (f32[1,128,128]{2,1,0:T(8,128)S(1)}, f32[1,128,128]{2,1,0:T(8,128)S(1)}, u32[]{:S(2)}, u32[]{:S(2)}) collective-permute-start(f32[1,128,128]{2,1,0:T(8,128)S(1)} %get-tuple-element.32), channel_id=1, source_target_pairs={{0,2},{2,0},{4,6},{6,4},{1,3},{3,1},{5,7},{7,5},{8,10},{10,8},{12,... | collective-permute-start | bytes 196616 | tf_op jit(solution)/shard_map/ppermute | solution.py:317
  11.2 0.2 shard_map.66
  11.4 0.0 collective-permute-done.1.refs_1_
  11.4 0.1 collective-permute-start.5
  11.5 0.0 collective-permute-done.3.refs_3_
  11.5 1.9 %collective-permute-done.2.refs_2_ = f32[128,128]{1,0:T(8,128)S(1)} collective-permute-done((f32[128,128]{1,0:T(8,128)S(1)}, f32[128,128]{1,0:T(8,128)S(1)}, u32[]{:S(2)}, u32[]{:S(2)}) %collective-permute-start.2) | collective-permute-done | bytes 65568 | tf_op jit(solution)/shard_map/ppermute | solution.py:315
  13.4 2.9 %collective-permute-start.9 = (f32[128,128]{1,0:T(8,128)S(1)}, f32[128,128]{1,0:T(8,128)S(1)}, u32[]{:S(2)}, u32[]{:S(2)}) collective-permute-start(f32[128,128]{1,0:T(8,128)S(1)} %shard_map.69.total_ref), channel_id=1, source_target_pairs={{0,24},{8,0},{16,8},{24,16},{1,25},{9,1},{17,9},{25,17},{2,26},{10... | collective-permute-start | bytes 196616 | tf_op jit(solution)/shard_map/ppermute | solution.py:322
  16.3 0.0 collective-permute-start.8
  16.3 0.0 collective-permute-done.4.refs_1_
  16.3 1.0 %collective-permute-start.7 = (f32[128,128]{1,0:T(8,128)S(1)}, f32[128,128]{1,0:T(8,128)S(1)}, u32[]{:S(2)}, u32[]{:S(2)}) collective-permute-start(f32[128,128]{1,0:T(8,128)S(1)} %shard_map.69.total_ref), channel_id=1, source_target_pairs={{0,8},{8,16},{16,24},{24,0},{1,9},{9,17},{17,25},{25,1},{2,10},{10... | collective-permute-start | bytes 196616 | tf_op jit(solution)/shard_map/ppermute | solution.py:322
  17.4 0.0 collective-permute-done.6.refs_3_
  17.4 0.0 collective-permute-done.5.refs_2_
  17.4 0.9 %collective-permute-done.9.refs_6_ = f32[128,128]{1,0:T(8,128)S(1)} collective-permute-done((f32[128,128]{1,0:T(8,128)S(1)}, f32[128,128]{1,0:T(8,128)S(1)}, u32[]{:S(2)}, u32[]{:S(2)}) %collective-permute-start.9) | collective-permute-done | bytes 65568 | tf_op jit(solution)/shard_map/ppermute | solution.py:322
  18.2 3.3 %collective-permute-done.8.refs_5_ = f32[128,128]{1,0:T(8,128)S(1)} collective-permute-done((f32[128,128]{1,0:T(8,128)S(1)}, f32[128,128]{1,0:T(8,128)S(1)}, u32[]{:S(2)}, u32[]{:S(2)}) %collective-permute-start.8) | collective-permute-done | bytes 65568 | tf_op jit(solution)/shard_map/ppermute | solution.py:322
  21.5 0.9 %collective-permute-done.7.refs_4_ = f32[128,128]{1,0:T(8,128)S(1)} collective-permute-done((f32[128,128]{1,0:T(8,128)S(1)}, f32[128,128]{1,0:T(8,128)S(1)}, u32[]{:S(2)}, u32[]{:S(2)}) %collective-permute-start.7) | collective-permute-done | bytes 65568 | tf_op jit(solution)/shard_map/ppermute | solution.py:322
  22.4 0.1 shard_map.70
  22.5 12.1 %all-gather = f32[12,128,128]{2,1,0:T(8,128)S(1)} all-gather(f32[3,128,128]{2,1,0:T(8,128)S(1)} %shard_map.70), channel_id=2, replica_groups=mesh['tm'=4,'mem'=4,'tile'=2] {'mem'}, dimensions={0}, use_global_device_ids=true | all-gather | bytes 983040 | tf_op jit(solution)/shard_map/all_gather | solution.py:329
  34.6 1.0 %shard_map.71 = f32[3,512,128]{2,1,0:T(8,128)} custom-call(f32[4,3,128,128]{3,2,1,0:T(8,128)S(1)} %bitcast.22), custom_call_target="tpu_custom_call" | custom-call | tf_op jit(solution)/shard_map/pallas_call | solution.py:330
  (1 shorter events, 0.0 us)
Async XLA Ops:
  0.0 2.3 %collective-permute-start = (f32[10,2,4,256]{3,2,1,0:T(4,128)}, f32[10,2,4,256]{3,2,1,0:T(4,128)S(1)}, u32[]{:S(2)}, u32[]{:S(2)}) collective-permute-start(f32[10,2,4,256]{3,2,1,0:T(4,128)} %param.6), channel_id=1, source_target_pairs={{0,1},{1,0},{2,3},{3,2},{4,5},{5,4},{6,7},{7,6},{8,9},{9,8},{10,11... | collective-permute-start | bytes 245768 | tf_op jit(solution)/shard_map/ppermute | solution.py:289
  3.1 8.3 %collective-permute-start.1 = (f32[128,128]{1,0:T(8,128)S(1)}, f32[128,128]{1,0:T(8,128)S(1)}, u32[]{:S(2)}, u32[]{:S(2)}) collective-permute-start(f32[128,128]{1,0:T(8,128)S(1)} %get-tuple-element.26), channel_id=1, source_target_pairs={{0,6},{2,4},{4,2},{6,0},{1,7},{3,5},{5,3},{7,1},{8,14},{10,12},{12... | collective-permute-start | bytes 196616 | tf_op jit(solution)/shard_map/ppermute | solution.py:315
  6.8 4.7 %collective-permute-start.3 = (f32[128,128]{1,0:T(8,128)S(1)}, f32[128,128]{1,0:T(8,128)S(1)}, u32[]{:S(2)}, u32[]{:S(2)}) collective-permute-start(f32[128,128]{1,0:T(8,128)S(1)} %get-tuple-element.28), channel_id=1, source_target_pairs={{0,2},{2,0},{4,6},{6,4},{1,3},{3,1},{5,7},{7,5},{8,10},{10,8},{12,... | collective-permute-start | bytes 196616 | tf_op jit(solution)/shard_map/ppermute | solution.py:315
  7.6 5.8 %collective-permute-start.2 = (f32[128,128]{1,0:T(8,128)S(1)}, f32[128,128]{1,0:T(8,128)S(1)}, u32[]{:S(2)}, u32[]{:S(2)}) collective-permute-start(f32[128,128]{1,0:T(8,128)S(1)} %get-tuple-element.27), channel_id=1, source_target_pairs={{0,4},{2,6},{4,0},{6,2},{1,5},{3,7},{5,1},{7,3},{8,12},{10,14},{12... | collective-permute-start | bytes 196616 | tf_op jit(solution)/shard_map/ppermute | solution.py:315
  7.7 8.6 %collective-permute-start.4 = (f32[1,128,128]{2,1,0:T(8,128)S(1)}, f32[1,128,128]{2,1,0:T(8,128)S(1)}, u32[]{:S(2)}, u32[]{:S(2)}) collective-permute-start(f32[1,128,128]{2,1,0:T(8,128)S(1)} %get-tuple-element.30), channel_id=1, source_target_pairs={{0,6},{2,4},{4,2},{6,0},{1,7},{3,5},{5,3},{7,1},{8,14},{10,12},{12... | collective-permute-start | bytes 196616 | tf_op jit(solution)/shard_map/ppermute | solution.py:317
  10.6 6.7 %collective-permute-start.6 = (f32[1,128,128]{2,1,0:T(8,128)S(1)}, f32[1,128,128]{2,1,0:T(8,128)S(1)}, u32[]{:S(2)}, u32[]{:S(2)}) collective-permute-start(f32[1,128,128]{2,1,0:T(8,128)S(1)} %get-tuple-element.32), channel_id=1, source_target_pairs={{0,2},{2,0},{4,6},{6,4},{1,3},{3,1},{5,7},{7,5},{8,10},{10,8},{12,... | collective-permute-start | bytes 196616 | tf_op jit(solution)/shard_map/ppermute | solution.py:317
  11.4 6.0 %collective-permute-start.5 = (f32[1,128,128]{2,1,0:T(8,128)S(1)}, f32[1,128,128]{2,1,0:T(8,128)S(1)}, u32[]{:S(2)}, u32[]{:S(2)}) collective-permute-start(f32[1,128,128]{2,1,0:T(8,128)S(1)} %get-tuple-element.31), channel_id=1, source_target_pairs={{0,4},{2,6},{4,0},{6,2},{1,5},{3,7},{5,1},{7,3},{8,12},{10,14},{12... | collective-permute-start | bytes 196616 | tf_op jit(solution)/shard_map/ppermute | solution.py:317
  13.4 4.8 %collective-permute-start.9 = (f32[128,128]{1,0:T(8,128)S(1)}, f32[128,128]{1,0:T(8,128)S(1)}, u32[]{:S(2)}, u32[]{:S(2)}) collective-permute-start(f32[128,128]{1,0:T(8,128)S(1)} %shard_map.69.total_ref), channel_id=1, source_target_pairs={{0,24},{8,0},{16,8},{24,16},{1,25},{9,1},{17,9},{25,17},{2,26},{10... | collective-permute-start | bytes 196616 | tf_op jit(solution)/shard_map/ppermute | solution.py:322
  16.3 5.2 %collective-permute-start.8 = (f32[128,128]{1,0:T(8,128)S(1)}, f32[128,128]{1,0:T(8,128)S(1)}, u32[]{:S(2)}, u32[]{:S(2)}) collective-permute-start(f32[128,128]{1,0:T(8,128)S(1)} %shard_map.69.total_ref), channel_id=1, source_target_pairs={{0,16},{8,24},{16,0},{24,8},{1,17},{9,25},{17,1},{25,9},{2,18},{10... | collective-permute-start | bytes 196616 | tf_op jit(solution)/shard_map/ppermute | solution.py:322
  16.3 6.1 %collective-permute-start.7 = (f32[128,128]{1,0:T(8,128)S(1)}, f32[128,128]{1,0:T(8,128)S(1)}, u32[]{:S(2)}, u32[]{:S(2)}) collective-permute-start(f32[128,128]{1,0:T(8,128)S(1)} %shard_map.69.total_ref), channel_id=1, source_target_pairs={{0,8},{8,16},{16,24},{24,0},{1,9},{9,17},{17,25},{25,1},{2,10},{10... | collective-permute-start | bytes 196616 | tf_op jit(solution)/shard_map/ppermute | solution.py:322

commit v4 on v3

--- a/solution.py
+++ b/solution.py
@@ -35,6 +35,16 @@
     if is_power(count):
         return place ^ step
     return lax.rem(place + step, count)
+
+
+def far_steps(group):
+    return [group - 1] if group > 2 else []
+
+
+def source_of(place, count, step):
+    if is_power(count):
+        return place ^ step
+    return lax.rem(place - step + count, count)
 
 
 def view(field):
@@ -188,45 +198,74 @@
     out_ref[...] = value * norm_factor
 
 
-def blend_kernel(norm_factor, parts, factor_ref, total_ref, *refs):
-    leads, arrived, out_ref = refs[:parts], refs[parts:-1], refs[-1]
-    windows, slots = factor_ref.shape[:2]
-    height = total_ref.shape[0]
+def slots_kernel(norm_factor, total_ref, *refs):
+    *leads, slots_ref = refs
+    slots = slots_ref.shape[0]
+    rest = total_ref[...]
+    for t in range(slots - 1):
+        value = leads[0][t]
+        for ref in leads[1:]:
+            value = value + ref[t]
+        value = value * norm_factor
+        slots_ref[t] = value
+        rest = rest - value
+    slots_ref[slots - 1] = rest
+
+
+def mix(factor_ref, slots_ref, earlier, w, rows):
+    for t in range(slots_ref.shape[0]):
+        earlier = earlier + factor_ref[w, t] * slots_ref[t, rows]
+    return earlier
+
+
+def blend_kernel(stages, factor_ref, slots_ref, *refs):
+    *arrived, earlier_ref, out_ref = refs
+    windows, height = out_ref.shape[:2]
     stage = lax.axis_index("tm")
     for r in range(0, height, ROWS):
         rows = slice(r, r + ROWS)
-        earlier = None
+        earlier = jnp.zeros((ROWS, LANES), jnp.float32)
         for step, ref in enumerate(arrived, 1):
-            value = ref[rows] * jnp.where(stage >= step, 1.0, 0.0)
-            earlier = value if earlier is None else earlier + value
-        values, rest = [], total_ref[rows]
-        for t in range(slots - 1):
-            value = leads[0][t, rows]
-            for ref in leads[1:]:
-                value = value + ref[t, rows]
-            values.append(value * norm_factor)
-            rest = rest - values[-1]
-        values.append(rest)
+            source = source_of(stage, stages, step)
+            earlier = earlier + ref[rows] * jnp.where(source < stage, 1.0, 0.0)
+        earlier_ref[rows] = earlier
         for w in range(windows):
-            mixed = earlier
-            for t in range(slots):
-                term = factor_ref[w, t] * values[t]
-                mixed = term if mixed is None else mixed + term
-            out_ref[w, rows] = mixed
-
-
-def place_kernel(height, whole_ref, out_ref, sems):
-    owners, windows = whole_ref.shape[:2]
+            out_ref[w, rows] = mix(factor_ref, slots_ref, earlier, w, rows)
+
+
+def copies_out(group, step, part_ref, out_ref, sems):
+    windows, height = part_ref.shape[:2]
+    owner = source_of(lax.axis_index("mem"), group, step)
+    start = pl.multiple_of(owner * height, height)
+    return [
+        pltpu.make_async_copy(part_ref.at[w], out_ref.at[w, pl.ds(start, height)], sems.at[w])
+        for w in range(windows)
+    ]
+
+
+def place_kernel(group, near, far, *refs):
+    refs = list(refs)
+    if near != [0]:
+        refs.pop(0)
+    near_refs = [refs.pop(0) for _ in near]
+    factor_ref = refs.pop(0) if far else None
+    far_refs = [(refs.pop(0), refs.pop(0)) for _ in far]
+    out_ref, *parts, sems = refs
     copies = []
-    for i in range(owners):
+    for i, (step, ref) in enumerate(zip(near, near_refs)):
+        started = copies_out(group, step, ref, out_ref, sems.at[i])
+        for copy in started:
+            copy.start()
+        copies += started
+    for i, (step, (slots_ref, earlier_ref), part_ref) in enumerate(zip(far, far_refs, parts)):
+        windows, height = part_ref.shape[:2]
+        started = copies_out(group, step, part_ref, out_ref, sems.at[len(near) + i])
         for w in range(windows):
-            copies.append(
-                pltpu.make_async_copy(
-                    whole_ref.at[i, w], out_ref.at[w, pl.ds(i * height, height)], sems.at[i, w]
-                )
-            )
-    for copy in copies:
-        copy.start()
+            for r in range(0, height, ROWS):
+                rows = slice(r, r + ROWS)
+                part_ref[w, rows] = mix(factor_ref, slots_ref, earlier_ref[rows], w, rows)
+            started[w].start()
+        copies += started
     for copy in copies:
         copy.wait()
 
@@ -319,23 +358,51 @@
 
     came = []
     for step in range(1, stages):
-        came.append(lax.ppermute(total, "tm", ring(stages, step)))
-    blended = call(
-        functools.partial(blend_kernel, norm_factor, len(leads)),
-        [factors, total] + leads + came,
-        f32(windows, height, LANES),
+        came.append(lax.ppermute(total, "tm", pairing(stages, step)))
+    slots = call(
+        functools.partial(slots_kernel, norm_factor),
+        [total] + leads,
+        f32(slot_count, height, LANES),
         1000000,
     )
-    whole = lax.all_gather(blended, "mem", axis=0, tiled=False)
-    placed = pl.pallas_call(
-        functools.partial(place_kernel, height),
-        in_specs=[VMEM_SPEC],
-        out_specs=HBM_SPEC,
-        out_shape=f32(windows, levels * ROWS, LANES),
-        scratch_shapes=[pltpu.SemaphoreType.DMA((group, windows))],
-        compiler_params=pltpu.CompilerParams(vmem_limit_bytes=16 * 1024 * 1024),
-    )(whole)
-    return unview(placed, x, y)
+    far = far_steps(group)
+    slots_far = {}
+    for step in far:
+        slots_far[step] = lax.ppermute(slots, "mem", pairing(group, step))
+    earlier, blended = call(
+        functools.partial(blend_kernel, stages),
+        [factors, slots] + came,
+        [f32(height, LANES), f32(windows, height, LANES)],
+        1000000,
+    )
+    final = {}
+    for step in range(1, group):
+        final[step] = lax.ppermute(earlier if step in far else blended, "mem", pairing(group, step))
+
+    def put(near, far, arrays):
+        goes_on = near != [0]
+        return pl.pallas_call(
+            functools.partial(place_kernel, group, near, far),
+            in_specs=[HBM_SPEC] * goes_on + [VMEM_SPEC] * (len(arrays) - goes_on),
+            out_specs=HBM_SPEC,
+            out_shape=pltpu.HBM((windows, levels * ROWS, LANES), jnp.float32),
+            scratch_shapes=[pltpu.VMEM((windows, height, LANES), jnp.float32)] * len(far)
+            + [pltpu.SemaphoreType.DMA((len(near) + len(far), windows))],
+            input_output_aliases={0: 0} if goes_on else {},
+            compiler_params=pltpu.CompilerParams(vmem_limit_bytes=16 * 1024 * 1024),
+            cost_estimate=pl.CostEstimate(flops=1000000, bytes_accessed=0, transcendentals=0),
+        )(*arrays)
+
+    whole = put([0], [], [blended])
+    near = [step for step in range(1, group) if step not in far]
+    for step in near[:-1]:
+        whole = put([step], [], [whole, final[step]])
+    if near:
+        arrays = [whole, final[near[-1]]] + [factors] * (len(far) > 0)
+        for step in far:
+            arrays += [slots_far[step], final[step]]
+        whole = put(near[-1:], far, arrays)
+    return unview(whole, x, y)
 
 
 def solution(mesh):

time: 35.7 us -> 33.5 us (0.938)
  blocking collectives: 12.1 us -> 0 us
  starting transfers between devices: 12.2 us -> 18.1 us
  waiting for transfers between devices: 6.91 us -> 9.65 us
  Pallas kernels: 4.25 us -> 5.48 us
    all_gather x1 -> x0, blocking collectives: 12.1 us -> none  [per_device(): whole = lax.all_gather(blended, 'mem', axis=0, tiled=False)]
    ppermute x3 -> x7, starting transfers between devices: 3.93 us -> 9.8 us  [the longest x3 4.45 us: per_device(): came.append(lax.ppermute(total, 'tm', pairing(stages, step)))]
    ppermute x3 -> x7, waiting for transfers between devices: 5.05 us -> 7.78 us  [the longest x3 3.75 us: per_device(): came.append(lax.ppermute(total, 'tm', pairing(stages, step)))]
    pallas_call x1 -> x3, Pallas kernels: 0.97 us -> 2.19 us  [put(): pl.pallas_call(functools.partial(place_kernel, group, near, far), in_spec...]
    pallas_call x6 -> x7, Pallas kernels: 1.44 us -> 1.45 us  [call(): pl.pallas_call(kernel, in_specs=[VMEM_SPEC] * len(arrays), out_specs=jax....]
  transfers between devices with their start and end apart: 10 -> 14, of which waited for: 4 -> 7; matrix products, arithmetic and copies ran while one was open for 0% -> 0% of each run, Pallas kernels for 7% -> 12%
where the time goes in v4:
time: 33.5 us; the launch traced here: 33.3 us
  starting transfers between devices  18.1 us (54%)
  waiting for transfers between devices  9.65 us (29%)
  Pallas kernels  5.48 us (16%)
    ppermute x3, starting transfers between devices, per_device(): came.append(lax.ppermute(total, 'tm', pairing(stages, step)))  4.45 us
    ppermute x3, starting transfers between devices, per_device(): totals.append(lax.ppermute(products[step][0], 'mem', pairing(group, step)))  4.21 us
    ppermute x3, starting transfers between devices, per_device(): lax.ppermute(earlier if step in far else blended, 'mem', pairing(group, s...  4.21 us
    ppermute x3, waiting for transfers between devices, per_device(): came.append(lax.ppermute(total, 'tm', pairing(stages, step)))  3.75 us
    ppermute x3, starting transfers between devices, per_device(): leads.append(lax.ppermute(products[step][1], 'mem', pairing(group, step)))  3.58 us
    ppermute x3, waiting for transfers between devices, per_device(): lax.ppermute(earlier if step in far else blended, 'mem', pairing(group, s...  2.27 us
    pallas_call x3, Pallas kernels, put(): pl.pallas_call(functools.partial(place_kernel, group, near, far), in_spec...  2.19 us
    ppermute x3, waiting for transfers between devices, per_device(): totals.append(lax.ppermute(products[step][0], 'mem', pairing(group, step)))  1.86 us
  transfers between devices with their start and end apart: 14, of which 7 were waited for; matrix products, arithmetic and copies ran while one was open for 0% of the time, Pallas kernels for 12%

profile of v4, /device:TPU:0, one launch (start us, length us, event | category | flops | bytes accessed | tf_op | source)
XLA Modules:
  0.0 33.3 jit_solution(4509384918787124111)
XLA Ops:
  0.0 0.5 %collective-permute-start = (f32[10,2,4,256]{3,2,1,0:T(4,128)}, f32[10,2,4,256]{3,2,1,0:T(4,128)S(1)}, u32[]{:S(2)}, u32[]{:S(2)}) collective-permute-start(f32[10,2,4,256]{3,2,1,0:T(4,128)} %param.6), channel_id=1, source_target_pairs={{0,1},{1,0},{2,3},{3,2},{4,5},{5,4},{6,7},{7,6},{8,9},{9,8},{10,11... | collective-permute-start | bytes 245768 | tf_op jit(solution)/shard_map/ppermute | solution.py:328
  0.5 1.8 %shard_map.64 = (f32[10,2,8,128]{3,2,1,0:T(8,128)S(1)}, bf16[10,2,512,128]{3,2,1,0:T(8,128)(2,1)S(1)}, f32[64,2,8,128]{3,2,1,0:T(8,128)S(1)}, f32[2,8,128]{2,1,0:T(8,128)S(1)}, f32[3,2,8,128]{3,2,1,0:T(8,128)S(1)}) custom-call(f32[2,64]{1,0:T(2,128)} %bitcast.24, s32[4]{0:T(128)} %counts_hbm.1, s32[3]{0:T(128)} %index_hbm.1, f32[3]{0:T(128)} %weight_hbm.1, ...), custom_call_target="tpu_custom_call" | custom-call | flops 1000000 | bytes 4000000 | tf_op jit(solution)/shard_map/pallas_call | solution.py:303
  2.3 0.0 collective-permute-done
  2.4 0.8 %shard_map.65 = (f32[10,2,8,128]{3,2,1,0:T(8,128)S(1)}, f32[128,128]{1,0:T(8,128)S(1)}, f32[1,128,128]{2,1,0:T(8,128)S(1)}) custom-call(f32[2,8,128]{2,1,0:T(8,128)S(1)} %get-tuple-element.23.mask_ref, f32[10,2,8,128]{3,2,1,0:T(8,128)S(1)} %get-tuple-element.24.own_ref, f32[10,2,8,128]{3,2,1,0:T(8,128)S(1)} %bitcast.21, ...), custom_call_target="tpu_custom_call" | custom-call | flops 2000000 | bytes 2000000 | tf_op jit(solution)/shard_map/pallas_call | solution.py:278
  3.1 3.5 %collective-permute-start.1 = (f32[128,128]{1,0:T(8,128)S(1)}, f32[128,128]{1,0:T(8,128)S(1)}, u32[]{:S(2)}, u32[]{:S(2)}) collective-permute-start(f32[128,128]{1,0:T(8,128)S(1)} %get-tuple-element.28), channel_id=1, source_target_pairs={{0,6},{2,4},{4,2},{6,0},{1,7},{3,5},{5,3},{7,1},{8,14},{10,12},{12... | collective-permute-start | bytes 196616 | tf_op jit(solution)/shard_map/ppermute | solution.py:354
  6.6 0.2 shard_map.68
  6.8 0.6 %collective-permute-start.3 = (f32[128,128]{1,0:T(8,128)S(1)}, f32[128,128]{1,0:T(8,128)S(1)}, u32[]{:S(2)}, u32[]{:S(2)}) collective-permute-start(f32[128,128]{1,0:T(8,128)S(1)} %get-tuple-element.30), channel_id=1, source_target_pairs={{0,2},{2,0},{4,6},{6,4},{1,3},{3,1},{5,7},{7,5},{8,10},{10,8},{12,... | collective-permute-start | bytes 196616 | tf_op jit(solution)/shard_map/ppermute | solution.py:354
  7.4 0.2 shard_map.67
  7.6 0.1 collective-permute-start.2
  7.7 2.9 %collective-permute-start.4 = (f32[1,128,128]{2,1,0:T(8,128)S(1)}, f32[1,128,128]{2,1,0:T(8,128)S(1)}, u32[]{:S(2)}, u32[]{:S(2)}) collective-permute-start(f32[1,128,128]{2,1,0:T(8,128)S(1)} %get-tuple-element.32), channel_id=1, source_target_pairs={{0,6},{2,4},{4,2},{6,0},{1,7},{3,5},{5,3},{7,1},{8,14},{10,12},{12... | collective-permute-start | bytes 196616 | tf_op jit(solution)/shard_map/ppermute | solution.py:356
  10.6 0.5 %collective-permute-start.6 = (f32[1,128,128]{2,1,0:T(8,128)S(1)}, f32[1,128,128]{2,1,0:T(8,128)S(1)}, u32[]{:S(2)}, u32[]{:S(2)}) collective-permute-start(f32[1,128,128]{2,1,0:T(8,128)S(1)} %get-tuple-element.34), channel_id=1, source_target_pairs={{0,2},{2,0},{4,6},{6,4},{1,3},{3,1},{5,7},{7,5},{8,10},{10,8},{12,... | collective-permute-start | bytes 196616 | tf_op jit(solution)/shard_map/ppermute | solution.py:356
  11.2 0.2 shard_map.66
  11.4 0.0 collective-permute-done.1.refs_1_
  11.4 0.1 collective-permute-start.5
  11.5 0.0 collective-permute-done.3.refs_3_
  11.5 1.9 %collective-permute-done.2.refs_2_ = f32[128,128]{1,0:T(8,128)S(1)} collective-permute-done((f32[128,128]{1,0:T(8,128)S(1)}, f32[128,128]{1,0:T(8,128)S(1)}, u32[]{:S(2)}, u32[]{:S(2)}) %collective-permute-start.2) | collective-permute-done | bytes 65568 | tf_op jit(solution)/shard_map/ppermute | solution.py:354
  13.4 2.9 %collective-permute-start.9 = (f32[128,128]{1,0:T(8,128)S(1)}, f32[128,128]{1,0:T(8,128)S(1)}, u32[]{:S(2)}, u32[]{:S(2)}) collective-permute-start(f32[128,128]{1,0:T(8,128)S(1)} %shard_map.69.total_ref), channel_id=1, source_target_pairs={{0,24},{8,16},{16,8},{24,0},{1,25},{9,17},{17,9},{25,1},{2,26},{10... | collective-permute-start | bytes 196616 | tf_op jit(solution)/shard_map/ppermute | solution.py:361
  16.3 0.0 collective-permute-start.8
  16.4 0.0 collective-permute-done.4.refs_1_
  16.4 1.5 %collective-permute-start.7 = (f32[128,128]{1,0:T(8,128)S(1)}, f32[128,128]{1,0:T(8,128)S(1)}, u32[]{:S(2)}, u32[]{:S(2)}) collective-permute-start(f32[128,128]{1,0:T(8,128)S(1)} %shard_map.69.total_ref), channel_id=1, source_target_pairs={{0,8},{8,0},{16,24},{24,16},{1,9},{9,1},{17,25},{25,17},{2,10},{10... | collective-permute-start | bytes 196616 | tf_op jit(solution)/shard_map/ppermute | solution.py:361
  17.9 0.0 collective-permute-done.6.refs_3_
  17.9 0.0 collective-permute-done.5.refs_2_
  17.9 2.1 %collective-permute-done.9.refs_2_ = f32[128,128]{1,0:T(8,128)S(1)} collective-permute-done((f32[128,128]{1,0:T(8,128)S(1)}, f32[128,128]{1,0:T(8,128)S(1)}, u32[]{:S(2)}, u32[]{:S(2)}) %collective-permute-start.9) | collective-permute-done | bytes 65568 | tf_op jit(solution)/shard_map/ppermute | solution.py:361
  20.0 1.7 %collective-permute-done.8.refs_1_ = f32[128,128]{1,0:T(8,128)S(1)} collective-permute-done((f32[128,128]{1,0:T(8,128)S(1)}, f32[128,128]{1,0:T(8,128)S(1)}, u32[]{:S(2)}, u32[]{:S(2)}) %collective-permute-start.8) | collective-permute-done | bytes 65568 | tf_op jit(solution)/shard_map/ppermute | solution.py:361
  21.7 0.0 collective-permute-done.7.refs_0_
  21.7 0.1 shard_map.71
  21.7 1.4 %collective-permute-start.10 = (f32[3,128,128]{2,1,0:T(8,128)S(1)}, f32[3,128,128]{2,1,0:T(8,128)S(1)}, u32[]{:S(2)}, u32[]{:S(2)}) collective-permute-start(f32[3,128,128]{2,1,0:T(8,128)S(1)} %get-tuple-element.35.refs_0_), channel_id=1, source_target_pairs={{0,2},{2,0},{4,6},{6,4},{1,3},{3,1},{5,7},{7,5},{8,10},{10,8},{12,... | collective-permute-start | bytes 589832 | tf_op jit(solution)/shard_map/ppermute | solution.py:380
  23.1 1.0 %collective-permute-start.11 = (f32[3,128,128]{2,1,0:T(8,128)S(1)}, f32[3,128,128]{2,1,0:T(8,128)S(1)}, u32[]{:S(2)}, u32[]{:S(2)}) collective-permute-start(f32[3,128,128]{2,1,0:T(8,128)S(1)} %get-tuple-element.35.refs_0_), channel_id=1, source_target_pairs={{0,4},{2,6},{4,0},{6,2},{1,5},{3,7},{5,1},{7,3},{8,12},{10,14},{12... | collective-permute-start | bytes 589832 | tf_op jit(solution)/shard_map/ppermute | solution.py:380
  24.1 1.1 %collective-permute-start.12 = (f32[2,128,128]{2,1,0:T(8,128)S(1)}, f32[2,128,128]{2,1,0:T(8,128)S(1)}, u32[]{:S(2)}, u32[]{:S(2)}) collective-permute-start(f32[2,128,128]{2,1,0:T(8,128)S(1)} %shard_map.70.slots_ref), channel_id=1, source_target_pairs={{0,6},{2,4},{4,2},{6,0},{1,7},{3,5},{5,3},{7,1},{8,14},{10,12},{12... | collective-permute-start | bytes 393224 | tf_op jit(solution)/shard_map/ppermute | solution.py:371
  25.3 1.8 %collective-permute-start.13 = (f32[128,128]{1,0:T(8,128)S(1)}, f32[128,128]{1,0:T(8,128)S(1)}, u32[]{:S(2)}, u32[]{:S(2)}) collective-permute-start(f32[128,128]{1,0:T(8,128)S(1)} %get-tuple-element.36), channel_id=1, source_target_pairs={{0,6},{2,4},{4,2},{6,0},{1,7},{3,5},{5,3},{7,1},{8,14},{10,12},{12... | collective-permute-start | bytes 196616 | tf_op jit(solution)/shard_map/ppermute | solution.py:380
  27.1 0.7 %shard_map.72.refs_0_ = f32[3,512,128]{2,1,0:T(8,128)} custom-call(f32[3,128,128]{2,1,0:T(8,128)S(1)} %get-tuple-element.35.refs_0_), custom_call_target="tpu_custom_call" | custom-call | flops 1000000 | tf_op jit(solution)/shard_map/pallas_call | solution.py:384
  27.8 1.1 %collective-permute-done.10.refs_1_ = f32[3,128,128]{2,1,0:T(8,128)S(1)} collective-permute-done((f32[3,128,128]{2,1,0:T(8,128)S(1)}, f32[3,128,128]{2,1,0:T(8,128)S(1)}, u32[]{:S(2)}, u32[]{:S(2)}) %collective-permute-start.10) | collective-permute-done | bytes 196640 | tf_op jit(solution)/shard_map/ppermute | solution.py:380
  28.9 0.7 %shard_map.73.refs_0_ = f32[3,512,128]{2,1,0:T(8,128)} custom-call(f32[3,512,128]{2,1,0:T(8,128)} %shard_map.72.refs_0_, f32[3,128,128]{2,1,0:T(8,128)S(1)} %collective-permute-done.10.refs_1_), custom_call_target="tpu_custom_call", output_to_operand_aliasing={{}: (0, {})} | custom-call | flops 1000000 | tf_op jit(solution)/shard_map/pallas_call | solution.py:384
  29.6 1.8 %collective-permute-done.12.refs_3_ = f32[2,128,128]{2,1,0:T(8,128)S(1)} collective-permute-done((f32[2,128,128]{2,1,0:T(8,128)S(1)}, f32[2,128,128]{2,1,0:T(8,128)S(1)}, u32[]{:S(2)}, u32[]{:S(2)}) %collective-permute-start.12) | collective-permute-done | bytes 131104 | tf_op jit(solution)/shard_map/ppermute | solution.py:371
  31.4 0.7 %collective-permute-done.13.refs_4_ = f32[128,128]{1,0:T(8,128)S(1)} collective-permute-done((f32[128,128]{1,0:T(8,128)S(1)}, f32[128,128]{1,0:T(8,128)S(1)}, u32[]{:S(2)}, u32[]{:S(2)}) %collective-permute-start.13) | collective-permute-done | bytes 65568 | tf_op jit(solution)/shard_map/ppermute | solution.py:380
  32.1 0.4 %collective-permute-done.11.refs_1_ = f32[3,128,128]{2,1,0:T(8,128)S(1)} collective-permute-done((f32[3,128,128]{2,1,0:T(8,128)S(1)}, f32[3,128,128]{2,1,0:T(8,128)S(1)}, u32[]{:S(2)}, u32[]{:S(2)}) %collective-permute-start.11) | collective-permute-done | bytes 196640 | tf_op jit(solution)/shard_map/ppermute | solution.py:380
  32.5 0.8 %shard_map.74 = f32[3,512,128]{2,1,0:T(8,128)} custom-call(f32[3,512,128]{2,1,0:T(8,128)} %shard_map.73.refs_0_, f32[3,128,128]{2,1,0:T(8,128)S(1)} %collective-permute-done.11.refs_1_, f32[3,2,8,128]{3,2,1,0:T(8,128)S(1)} %get-tuple-element.21.factor_ref.refs_2_, ...), custom_call_target="tpu_custom_call", output_to_operand_aliasing={{}: (0, {})} | custom-call | flops 1000000 | tf_op jit(solution)/shard_map/pallas_call | solution.py:384
  (2 shorter events, 0.0 us)
Async XLA Ops:
  0.0 2.3 %collective-permute-start = (f32[10,2,4,256]{3,2,1,0:T(4,128)}, f32[10,2,4,256]{3,2,1,0:T(4,128)S(1)}, u32[]{:S(2)}, u32[]{:S(2)}) collective-permute-start(f32[10,2,4,256]{3,2,1,0:T(4,128)} %param.6), channel_id=1, source_target_pairs={{0,1},{1,0},{2,3},{3,2},{4,5},{5,4},{6,7},{7,6},{8,9},{9,8},{10,11... | collective-permute-start | bytes 245768 | tf_op jit(solution)/shard_map/ppermute | solution.py:328
  3.1 8.3 %collective-permute-start.1 = (f32[128,128]{1,0:T(8,128)S(1)}, f32[128,128]{1,0:T(8,128)S(1)}, u32[]{:S(2)}, u32[]{:S(2)}) collective-permute-start(f32[128,128]{1,0:T(8,128)S(1)} %get-tuple-element.28), channel_id=1, source_target_pairs={{0,6},{2,4},{4,2},{6,0},{1,7},{3,5},{5,3},{7,1},{8,14},{10,12},{12... | collective-permute-start | bytes 196616 | tf_op jit(solution)/shard_map/ppermute | solution.py:354
  6.8 4.7 %collective-permute-start.3 = (f32[128,128]{1,0:T(8,128)S(1)}, f32[128,128]{1,0:T(8,128)S(1)}, u32[]{:S(2)}, u32[]{:S(2)}) collective-permute-start(f32[128,128]{1,0:T(8,128)S(1)} %get-tuple-element.30), channel_id=1, source_target_pairs={{0,2},{2,0},{4,6},{6,4},{1,3},{3,1},{5,7},{7,5},{8,10},{10,8},{12,... | collective-permute-start | bytes 196616 | tf_op jit(solution)/shard_map/ppermute | solution.py:354
  7.6 5.8 %collective-permute-start.2 = (f32[128,128]{1,0:T(8,128)S(1)}, f32[128,128]{1,0:T(8,128)S(1)}, u32[]{:S(2)}, u32[]{:S(2)}) collective-permute-start(f32[128,128]{1,0:T(8,128)S(1)} %get-tuple-element.29), channel_id=1, source_target_pairs={{0,4},{2,6},{4,0},{6,2},{1,5},{3,7},{5,1},{7,3},{8,12},{10,14},{12... | collective-permute-start | bytes 196616 | tf_op jit(solution)/shard_map/ppermute | solution.py:354
  7.7 8.6 %collective-permute-start.4 = (f32[1,128,128]{2,1,0:T(8,128)S(1)}, f32[1,128,128]{2,1,0:T(8,128)S(1)}, u32[]{:S(2)}, u32[]{:S(2)}) collective-permute-start(f32[1,128,128]{2,1,0:T(8,128)S(1)} %get-tuple-element.32), channel_id=1, source_target_pairs={{0,6},{2,4},{4,2},{6,0},{1,7},{3,5},{5,3},{7,1},{8,14},{10,12},{12... | collective-permute-start | bytes 196616 | tf_op jit(solution)/shard_map/ppermute | solution.py:356
  10.6 7.2 %collective-permute-start.6 = (f32[1,128,128]{2,1,0:T(8,128)S(1)}, f32[1,128,128]{2,1,0:T(8,128)S(1)}, u32[]{:S(2)}, u32[]{:S(2)}) collective-permute-start(f32[1,128,128]{2,1,0:T(8,128)S(1)} %get-tuple-element.34), channel_id=1, source_target_pairs={{0,2},{2,0},{4,6},{6,4},{1,3},{3,1},{5,7},{7,5},{8,10},{10,8},{12,... | collective-permute-start | bytes 196616 | tf_op jit(solution)/shard_map/ppermute | solution.py:356
  11.4 6.5 %collective-permute-start.5 = (f32[1,128,128]{2,1,0:T(8,128)S(1)}, f32[1,128,128]{2,1,0:T(8,128)S(1)}, u32[]{:S(2)}, u32[]{:S(2)}) collective-permute-start(f32[1,128,128]{2,1,0:T(8,128)S(1)} %get-tuple-element.33), channel_id=1, source_target_pairs={{0,4},{2,6},{4,0},{6,2},{1,5},{3,7},{5,1},{7,3},{8,12},{10,14},{12... | collective-permute-start | bytes 196616 | tf_op jit(solution)/shard_map/ppermute | solution.py:356
  13.4 6.5 %collective-permute-start.9 = (f32[128,128]{1,0:T(8,128)S(1)}, f32[128,128]{1,0:T(8,128)S(1)}, u32[]{:S(2)}, u32[]{:S(2)}) collective-permute-start(f32[128,128]{1,0:T(8,128)S(1)} %shard_map.69.total_ref), channel_id=1, source_target_pairs={{0,24},{8,16},{16,8},{24,0},{1,25},{9,17},{17,9},{25,1},{2,26},{10... | collective-permute-start | bytes 196616 | tf_op jit(solution)/shard_map/ppermute | solution.py:361
  16.3 5.3 %collective-permute-start.8 = (f32[128,128]{1,0:T(8,128)S(1)}, f32[128,128]{1,0:T(8,128)S(1)}, u32[]{:S(2)}, u32[]{:S(2)}) collective-permute-start(f32[128,128]{1,0:T(8,128)S(1)} %shard_map.69.total_ref), channel_id=1, source_target_pairs={{0,16},{8,24},{16,0},{24,8},{1,17},{9,25},{17,1},{25,9},{2,18},{10... | collective-permute-start | bytes 196616 | tf_op jit(solution)/shard_map/ppermute | solution.py:361
  16.4 5.3 %collective-permute-start.7 = (f32[128,128]{1,0:T(8,128)S(1)}, f32[128,128]{1,0:T(8,128)S(1)}, u32[]{:S(2)}, u32[]{:S(2)}) collective-permute-start(f32[128,128]{1,0:T(8,128)S(1)} %shard_map.69.total_ref), channel_id=1, source_target_pairs={{0,8},{8,0},{16,24},{24,16},{1,9},{9,1},{17,25},{25,17},{2,10},{10... | collective-permute-start | bytes 196616 | tf_op jit(solution)/shard_map/ppermute | solution.py:361
  21.7 7.2 %collective-permute-start.10 = (f32[3,128,128]{2,1,0:T(8,128)S(1)}, f32[3,128,128]{2,1,0:T(8,128)S(1)}, u32[]{:S(2)}, u32[]{:S(2)}) collective-permute-start(f32[3,128,128]{2,1,0:T(8,128)S(1)} %get-tuple-element.35.refs_0_), channel_id=1, source_target_pairs={{0,2},{2,0},{4,6},{6,4},{1,3},{3,1},{5,7},{7,5},{8,10},{10,8},{12,... | collective-permute-start | bytes 589832 | tf_op jit(solution)/shard_map/ppermute | solution.py:380
  23.1 9.4 %collective-permute-start.11 = (f32[3,128,128]{2,1,0:T(8,128)S(1)}, f32[3,128,128]{2,1,0:T(8,128)S(1)}, u32[]{:S(2)}, u32[]{:S(2)}) collective-permute-start(f32[3,128,128]{2,1,0:T(8,128)S(1)} %get-tuple-element.35.refs_0_), channel_id=1, source_target_pairs={{0,4},{2,6},{4,0},{6,2},{1,5},{3,7},{5,1},{7,3},{8,12},{10,14},{12... | collective-permute-start | bytes 589832 | tf_op jit(solution)/shard_map/ppermute | solution.py:380
  24.1 7.2 %collective-permute-start.12 = (f32[2,128,128]{2,1,0:T(8,128)S(1)}, f32[2,128,128]{2,1,0:T(8,128)S(1)}, u32[]{:S(2)}, u32[]{:S(2)}) collective-permute-start(f32[2,128,128]{2,1,0:T(8,128)S(1)} %shard_map.70.slots_ref), channel_id=1, source_target_pairs={{0,6},{2,4},{4,2},{6,0},{1,7},{3,5},{5,3},{7,1},{8,14},{10,12},{12... | collective-permute-start | bytes 393224 | tf_op jit(solution)/shard_map/ppermute | solution.py:371
  25.3 6.8 %collective-permute-start.13 = (f32[128,128]{1,0:T(8,128)S(1)}, f32[128,128]{1,0:T(8,128)S(1)}, u32[]{:S(2)}, u32[]{:S(2)}) collective-permute-start(f32[128,128]{1,0:T(8,128)S(1)} %get-tuple-element.36), channel_id=1, source_target_pairs={{0,6},{2,4},{4,2},{6,0},{1,7},{3,5},{5,3},{7,1},{8,14},{10,12},{12... | collective-permute-start | bytes 196616 | tf_op jit(solution)/shard_map/ppermute | solution.py:380

commit v5 on v4

--- a/solution.py
+++ b/solution.py
@@ -37,8 +37,8 @@
     return lax.rem(place + step, count)
 
 
-def far_steps(group):
-    return [group - 1] if group > 2 else []
+def plan_of(group):
+    return list(range(group - 1, 0, -1))
 
 
 def source_of(place, count, step):
@@ -89,8 +89,8 @@
 
 
 def load_kernel(
-    x, modes_hbm, counts_hbm, index_hbm, weight_hbm, own_hbm, part_hbm,
-    own_ref, part_ref, splat_ref, mask_ref, factor_ref,
+    x, modes_hbm, counts_hbm, index_hbm, weight_hbm, own_hbm,
+    own_ref, splat_ref, mask_ref, factor_ref,
     modes_ref, counts_ref, index_ref, weight_ref, sems,
 ):
     pairs = [
@@ -99,12 +99,11 @@
         (index_hbm, index_ref),
         (weight_hbm, weight_ref),
         (own_hbm, own_ref),
-        (part_hbm, part_ref),
     ]
     copies = [pltpu.make_async_copy(a, b, sems.at[i]) for i, (a, b) in enumerate(pairs)]
     for copy in copies:
         copy.start()
-    for copy in copies[:-2]:
+    for copy in copies[:-1]:
         copy.wait()
     levels, modes = splat_ref.shape[:2]
     for l in range(levels):
@@ -122,7 +121,7 @@
         for t in range(slots):
             factor = jnp.where(local == t, weight_ref[w], jnp.where(local > t, 1.0, 0.0))
             factor_ref[w, t] = jnp.full((ROWS, LANES), factor, jnp.float32)
-    for copy in copies[-2:]:
+    for copy in copies[-1:]:
         copy.wait()
 
 
@@ -174,20 +173,18 @@
         total_ref[pl.ds(2 * j * ROWS, pair), :] = whole
 
 
-def smooth_kernel(group, step, share, mask_ref, own_ref, other_ref, splat_ref, part_ref, field_ref, total_ref, lead_ref):
+def smooth_kernel(mask_ref, own_ref, other_ref, field_ref):
     members, modes = own_ref.shape[:2]
     for k in range(members):
         for m in range(modes):
             field_ref[k, m] = smoothed_pair(own_ref[k, m], other_ref[k, m]) * mask_ref[m]
-    product(group, step, share, splat_ref, field_ref, part_ref, total_ref, lead_ref)
-
-
-def mask_kernel(group, step, share, mask_ref, own_ref, splat_ref, part_ref, field_ref, total_ref, lead_ref):
+
+
+def mask_kernel(mask_ref, own_ref, field_ref):
     members, modes = own_ref.shape[:2]
     for k in range(members):
         for m in range(modes):
             field_ref[k, m] = own_ref[k, m] * mask_ref[m]
-    product(group, step, share, splat_ref, field_ref, part_ref, total_ref, lead_ref)
 
 
 def gather_kernel(norm_factor, *refs):
@@ -198,39 +195,42 @@
     out_ref[...] = value * norm_factor
 
 
-def slots_kernel(norm_factor, total_ref, *refs):
+def scale_kernel(norm_factor, lead_ref, out_ref):
+    out_ref[...] = lead_ref[...] * norm_factor
+
+
+def slots_kernel(norm_factor, total_ref, own_ref, *refs):
     *leads, slots_ref = refs
     slots = slots_ref.shape[0]
     rest = total_ref[...]
     for t in range(slots - 1):
-        value = leads[0][t]
-        for ref in leads[1:]:
-            value = value + ref[t]
-        value = value * norm_factor
+        value = own_ref[t]
+        for ref in leads:
+            value = value + ref[t] * norm_factor
         slots_ref[t] = value
         rest = rest - value
     slots_ref[slots - 1] = rest
 
 
-def mix(factor_ref, slots_ref, earlier, w, rows):
-    for t in range(slots_ref.shape[0]):
-        earlier = earlier + factor_ref[w, t] * slots_ref[t, rows]
-    return earlier
-
-
-def blend_kernel(stages, factor_ref, slots_ref, *refs):
-    *arrived, earlier_ref, out_ref = refs
+def mix_kernel(factor_ref, slots_ref, out_ref):
     windows, height = out_ref.shape[:2]
-    stage = lax.axis_index("tm")
     for r in range(0, height, ROWS):
         rows = slice(r, r + ROWS)
-        earlier = jnp.zeros((ROWS, LANES), jnp.float32)
-        for step, ref in enumerate(arrived, 1):
-            source = source_of(stage, stages, step)
-            earlier = earlier + ref[rows] * jnp.where(source < stage, 1.0, 0.0)
-        earlier_ref[rows] = earlier
         for w in range(windows):
-            out_ref[w, rows] = mix(factor_ref, slots_ref, earlier, w, rows)
+            mixed = factor_ref[w, 0] * slots_ref[0, rows]
+            for t in range(1, slots_ref.shape[0]):
+                mixed = mixed + factor_ref[w, t] * slots_ref[t, rows]
+            out_ref[w, rows] = mixed
+
+
+def earlier_kernel(stages, *refs):
+    *arrived, earlier_ref = refs
+    stage = lax.axis_index("tm")
+    earlier = jnp.zeros(earlier_ref.shape, jnp.float32)
+    for step, ref in enumerate(arrived, 1):
+        source = source_of(stage, stages, step)
+        earlier = earlier + ref[...] * jnp.where(source < stage, 1.0, 0.0)
+    earlier_ref[...] = earlier
 
 
 def copies_out(group, step, part_ref, out_ref, sems):
@@ -243,27 +243,26 @@
     ]
 
 
-def place_kernel(group, near, far, *refs):
+def place_kernel(group, plan, goes_on, factor_ref, *refs):
     refs = list(refs)
-    if near != [0]:
+    if goes_on:
         refs.pop(0)
-    near_refs = [refs.pop(0) for _ in near]
-    factor_ref = refs.pop(0) if far else None
-    far_refs = [(refs.pop(0), refs.pop(0)) for _ in far]
+    quarters = [(refs.pop(0), refs.pop(0)) for _ in plan]
     out_ref, *parts, sems = refs
     copies = []
-    for i, (step, ref) in enumerate(zip(near, near_refs)):
-        started = copies_out(group, step, ref, out_ref, sems.at[i])
-        for copy in started:
-            copy.start()
-        copies += started
-    for i, (step, (slots_ref, earlier_ref), part_ref) in enumerate(zip(far, far_refs, parts)):
+    for i, (step, (slots_ref, earlier_ref), part_ref) in enumerate(zip(plan, quarters, parts)):
         windows, height = part_ref.shape[:2]
-        started = copies_out(group, step, part_ref, out_ref, sems.at[len(near) + i])
+        started = copies_out(group, step, part_ref, out_ref, sems.at[i])
         for w in range(windows):
             for r in range(0, height, ROWS):
                 rows = slice(r, r + ROWS)
-                part_ref[w, rows] = mix(factor_ref, slots_ref, earlier_ref[rows], w, rows)
+                value = earlier_ref[rows]
+                if step == 0:
+                    value = value + slots_ref[w, rows]
+                else:
+                    for t in range(slots_ref.shape[0]):
+                        value = value + factor_ref[w, t] * slots_ref[t, rows]
+                part_ref[w, rows] = value
             started[w].start()
         copies += started
     for copy in copies:
@@ -300,13 +299,12 @@
 
     room = parts.size * parts.dtype.itemsize + levels * modes * ROWS * LANES * 4
 
-    loaded, parts, splats, masks, factors = pl.pallas_call(
+    loaded, splats, masks, factors = pl.pallas_call(
         functools.partial(load_kernel, x),
-        in_specs=[HBM_SPEC] * 6,
-        out_specs=[VMEM_SPEC] * 5,
+        in_specs=[HBM_SPEC] * 5,
+        out_specs=[VMEM_SPEC] * 4,
         out_shape=[
             pltpu.VMEM(own.shape, jnp.float32),
-            pltpu.VMEM(parts.shape, parts.dtype),
             pltpu.VMEM((levels, modes, ROWS, LANES), jnp.float32),
             pltpu.VMEM((modes, ROWS, LANES), jnp.float32),
             pltpu.VMEM((windows, slot_count, ROWS, LANES), jnp.float32),
@@ -316,92 +314,84 @@
             pltpu.SMEM(mode_counts.shape, jnp.int32),
             pltpu.SMEM(slot_index.shape, jnp.int32),
             pltpu.SMEM(blend_weight.shape, jnp.float32),
-            pltpu.SemaphoreType.DMA((6,)),
+            pltpu.SemaphoreType.DMA((5,)),
         ],
         compiler_params=pltpu.CompilerParams(vmem_limit_bytes=VMEM_BYTES - 2 * room),
-        cost_estimate=pl.CostEstimate(flops=1000000, bytes_accessed=4000000, transcendentals=0),
-    )(vertical_modes.T, mode_counts, slot_index, blend_weight, own, parts)
+        cost_estimate=pl.CostEstimate(flops=1000000000, bytes_accessed=1000000000, transcendentals=0),
+    )(vertical_modes.T, mode_counts, slot_index, blend_weight, own)
 
     shapes = [f32(height, LANES), f32(slot_count - 1, height, LANES)]
     field_shape = f32(members, modes, ROWS, LANES)
+    plan = plan_of(group)
     if lax.axis_size("tile") == 2 and x == SMOOTH:
         other = lax.ppermute(control, "tile", ring(2, 1))
-        field, *first = call(
-            functools.partial(smooth_kernel, group, group - 1, share),
-            [masks, loaded, view(other[:, :, None]), splats, parts],
-            [field_shape] + shapes,
-            2000000,
+        field = call(
+            smooth_kernel, [masks, loaded, view(other[:, :, None])], field_shape, 1000
         )
     else:
-        field, *first = call(
-            functools.partial(mask_kernel, group, group - 1, share),
-            [masks, view(smooth(control)[:, :, None]), splats, parts],
-            [field_shape] + shapes,
-            2000000,
+        field = call(mask_kernel, [masks, view(smooth(control)[:, :, None])], field_shape, 1000)
+
+    products = []
+    for step in plan + [0]:
+        products.append(
+            call(
+                functools.partial(product, group, step, share),
+                [splats, field, parts],
+                shapes,
+                1000000,
+            )
         )
 
-    products = {group - 1: first}
-    for step in range(group - 1):
-        products[step] = call(
-            functools.partial(product, group, step, share),
-            [splats, field, parts],
-            shapes,
-            1000000,
-        )
-
-    totals, leads = [products[0][0]], [products[0][1]]
-    for step in range(group - 1, 0, -1):
-        totals.append(lax.ppermute(products[step][0], "mem", pairing(group, step)))
-    for step in range(group - 1, 0, -1):
-        leads.append(lax.ppermute(products[step][1], "mem", pairing(group, step)))
+    totals, leads = [products[-1][0]], [products[-1][1]]
+    for i, step in enumerate(plan):
+        totals.append(lax.ppermute(products[i][0], "mem", pairing(group, step)))
+        leads.append(lax.ppermute(products[i][1], "mem", pairing(group, step)))
     total = call(functools.partial(gather_kernel, norm_factor), totals, f32(height, LANES), 1000000)
 
     came = []
     for step in range(1, stages):
         came.append(lax.ppermute(total, "tm", pairing(stages, step)))
+    scaled = call(
+        functools.partial(scale_kernel, norm_factor), [leads[0]], shapes[1], 1000000
+    )
     slots = call(
         functools.partial(slots_kernel, norm_factor),
-        [total] + leads,
+        [total, scaled] + leads[1:],
         f32(slot_count, height, LANES),
         1000000,
     )
-    far = far_steps(group)
-    slots_far = {}
-    for step in far:
-        slots_far[step] = lax.ppermute(slots, "mem", pairing(group, step))
-    earlier, blended = call(
-        functools.partial(blend_kernel, stages),
-        [factors, slots] + came,
-        [f32(height, LANES), f32(windows, height, LANES)],
-        1000000,
+    slots_far = []
+    for step in plan:
+        slots_far.append(lax.ppermute(slots, "mem", pairing(group, step)))
+    mixed = call(mix_kernel, [factors, slots], f32(windows, height, LANES), 1000000)
+    earlier = call(
+        functools.partial(earlier_kernel, stages), came, f32(height, LANES), 1000000
     )
-    final = {}
-    for step in range(1, group):
-        final[step] = lax.ppermute(earlier if step in far else blended, "mem", pairing(group, step))
-
-    def put(near, far, arrays):
-        goes_on = near != [0]
+    earlier_far = []
+    for step in plan:
+        earlier_far.append(lax.ppermute(earlier, "mem", pairing(group, step)))
+
+    def put(steps, whole, quarters):
+        first = [] if whole is None else [whole]
         return pl.pallas_call(
-            functools.partial(place_kernel, group, near, far),
-            in_specs=[HBM_SPEC] * goes_on + [VMEM_SPEC] * (len(arrays) - goes_on),
+            functools.partial(place_kernel, group, steps, bool(first)),
+            in_specs=[VMEM_SPEC] + [HBM_SPEC] * len(first) + [VMEM_SPEC] * (2 * len(steps)),
             out_specs=HBM_SPEC,
             out_shape=pltpu.HBM((windows, levels * ROWS, LANES), jnp.float32),
-            scratch_shapes=[pltpu.VMEM((windows, height, LANES), jnp.float32)] * len(far)
-            + [pltpu.SemaphoreType.DMA((len(near) + len(far), windows))],
-            input_output_aliases={0: 0} if goes_on else {},
+            scratch_shapes=[pltpu.VMEM((windows, height, LANES), jnp.float32)] * len(steps)
+            + [pltpu.SemaphoreType.DMA((len(steps), windows))],
+            input_output_aliases={1: 0} if first else {},
             compiler_params=pltpu.CompilerParams(vmem_limit_bytes=16 * 1024 * 1024),
             cost_estimate=pl.CostEstimate(flops=1000000, bytes_accessed=0, transcendentals=0),
-        )(*arrays)
-
-    whole = put([0], [], [blended])
-    near = [step for step in range(1, group) if step not in far]
-    for step in near[:-1]:
-        whole = put([step], [], [whole, final[step]])
-    if near:
-        arrays = [whole, final[near[-1]]] + [factors] * (len(far) > 0)
-        for step in far:
-            arrays += [slots_far[step], final[step]]
-        whole = put(near[-1:], far, arrays)
+        )(factors, *first, *[ref for pair in quarters for ref in pair])
+
+    whole = put([0], None, [(mixed, earlier)])
+    quarters = list(zip(slots_far, earlier_far))
+    if len(plan) > 1:
+        whole = put(plan[:1], whole, quarters[:1])
+        plan, quarters = plan[1:], quarters[1:]
+    if plan:
+        whole = put(plan, whole, quarters)
     return unview(whole, x, y)
 
 

time: 33.5 us -> 33.6 us (level)
  starting transfers between devices: 18.1 us -> 21.2 us
  waiting for transfers between devices: 9.65 us -> 7.15 us
  Pallas kernels: 5.48 us -> 4.99 us
    ppermute x3, waiting for transfers between devices: 3.75 us -> 1.7 us  [per_device(): came.append(lax.ppermute(total, 'tm', pairing(stages, step)))]
    ppermute x10 -> x12, starting transfers between devices: 13.1 us -> 14.8 us  [the longest x3 4.49 us: per_device(): totals.append(lax.ppermute(products[i][0], 'mem', pairing(group, step)))]
    ppermute x3, starting transfers between devices: 4.45 us -> 5.98 us  [per_device(): came.append(lax.ppermute(total, 'tm', pairing(stages, step)))]
    pallas_call x4, Pallas kernels: 4.03 us -> 3.4 us  [the longest x3 2.22 us: put(): pl.pallas_call(functools.partial(place_kernel, group, steps, bool(first))...]
    ppermute x10 -> x12, waiting for transfers between devices: 5.9 us -> 5.45 us  [the longest x3 2.25 us: per_device(): earlier_far.append(lax.ppermute(earlier, 'mem', pairing(group, step)))]
    pallas_call x7 -> x10, Pallas kernels: 1.45 us -> 1.59 us  [call(): pl.pallas_call(kernel, in_specs=[VMEM_SPEC] * len(arrays), out_specs=jax....]
  transfers between devices with their start and end apart: 14 -> 16, of which waited for: 7 -> 7; matrix products, arithmetic and copies ran while one was open for 0% -> 0% of each run, Pallas kernels for 12% -> 10%
where the time goes in v5:
time: 33.6 us; the launch traced here: 33.5 us
  starting transfers between devices  21.2 us (63%)
  waiting for transfers between devices  7.15 us (21%)
  Pallas kernels  4.99 us (15%)
    ppermute x3, starting transfers between devices, per_device(): came.append(lax.ppermute(total, 'tm', pairing(stages, step)))  5.98 us
    ppermute x3, starting transfers between devices, per_device(): totals.append(lax.ppermute(products[i][0], 'mem', pairing(group, step)))  4.49 us
    ppermute x3, starting transfers between devices, per_device(): earlier_far.append(lax.ppermute(earlier, 'mem', pairing(group, step)))  3.55 us
    ppermute x3, starting transfers between devices, per_device(): leads.append(lax.ppermute(products[i][1], 'mem', pairing(group, step)))  3.55 us
    ppermute x3, starting transfers between devices, per_device(): slots_far.append(lax.ppermute(slots, 'mem', pairing(group, step)))  3.16 us
    ppermute x3, waiting for transfers between devices, per_device(): earlier_far.append(lax.ppermute(earlier, 'mem', pairing(group, step)))  2.25 us
    pallas_call x3, Pallas kernels, put(): pl.pallas_call(functools.partial(place_kernel, group, steps, bool(first))...  2.22 us
    ppermute x3, waiting for transfers between devices, per_device(): leads.append(lax.ppermute(products[i][1], 'mem', pairing(group, step)))  1.8 us
  transfers between devices with their start and end apart: 16, of which 7 were waited for; matrix products, arithmetic and copies ran while one was open for 0% of the time, Pallas kernels for 10%

profile of v5, /device:TPU:0, one launch (start us, length us, event | category | flops | bytes accessed | tf_op | source)
XLA Modules:
  0.0 33.5 jit_solution(1646372461941864195)
XLA Ops:
  0.0 0.0 copy-start
  0.0 0.5 %collective-permute-start = (f32[10,2,4,256]{3,2,1,0:T(4,128)}, f32[10,2,4,256]{3,2,1,0:T(4,128)S(1)}, u32[]{:S(2)}, u32[]{:S(2)}) collective-permute-start(f32[10,2,4,256]{3,2,1,0:T(4,128)} %param.6), channel_id=1, source_target_pairs={{0,1},{1,0},{2,3},{3,2},{4,5},{5,4},{6,7},{7,6},{8,9},{9,8},{10,11... | collective-permute-start | bytes 245768 | tf_op jit(solution)/shard_map/ppermute | solution.py:327
  0.5 1.2 %shard_map.64 = (f32[10,2,8,128]{3,2,1,0:T(8,128)S(1)}, f32[64,2,8,128]{3,2,1,0:T(8,128)S(1)}, f32[2,8,128]{2,1,0:T(8,128)S(1)}, f32[3,2,8,128]{3,2,1,0:T(8,128)S(1)}) custom-call(f32[2,64]{1,0:T(2,128)} %bitcast.27, s32[4]{0:T(128)} %counts_hbm.1, s32[3]{0:T(128)} %index_hbm.1, f32[3]{0:T(128)} %weight_hbm.1, f32[10,2,8,128]{3,2,1,0:T(8,128)} %bitcast.26), custom_call_target="tpu_custom_call" | custom-call | flops 1000000000 | bytes 1000000000 | tf_op jit(solution)/shard_map/pallas_call | solution.py:302
  1.7 0.0 collective-permute-done
  1.7 0.7 %shard_map.65.field_ref = f32[10,2,8,128]{3,2,1,0:T(8,128)S(1)} custom-call(f32[2,8,128]{2,1,0:T(8,128)S(1)} %get-tuple-element.19.mask_ref, f32[10,2,8,128]{3,2,1,0:T(8,128)S(1)} %get-tuple-element.20.own_ref, f32[10,2,8,128]{3,2,1,0:T(8,128)S(1)} %bitcast.25), custom_call_target="tpu_custom_call" | custom-call | flops 1000 | bytes 1000 | tf_op jit(solution)/shard_map/pallas_call | solution.py:277
  2.4 0.0 copy-done
  2.4 0.2 shard_map.69
  2.6 2.8 %collective-permute-start.3 = (f32[128,128]{1,0:T(8,128)S(1)}, f32[128,128]{1,0:T(8,128)S(1)}, u32[]{:S(2)}, u32[]{:S(2)}) collective-permute-start(f32[128,128]{1,0:T(8,128)S(1)} %get-tuple-element.24), channel_id=1, source_target_pairs={{0,2},{2,0},{4,6},{6,4},{1,3},{3,1},{5,7},{7,5},{8,10},{10,8},{12,... | collective-permute-start | bytes 196616 | tf_op jit(solution)/shard_map/ppermute | solution.py:347
  5.4 0.2 shard_map.68
  5.6 1.6 %collective-permute-start.2 = (f32[128,128]{1,0:T(8,128)S(1)}, f32[128,128]{1,0:T(8,128)S(1)}, u32[]{:S(2)}, u32[]{:S(2)}) collective-permute-start(f32[128,128]{1,0:T(8,128)S(1)} %get-tuple-element.23), channel_id=1, source_target_pairs={{0,4},{2,6},{4,0},{6,2},{1,5},{3,7},{5,1},{7,3},{8,12},{10,14},{12... | collective-permute-start | bytes 196616 | tf_op jit(solution)/shard_map/ppermute | solution.py:347
  7.2 0.2 shard_map.67
  7.4 0.1 collective-permute-start.1
  7.5 2.0 %collective-permute-start.6 = (f32[1,128,128]{2,1,0:T(8,128)S(1)}, f32[1,128,128]{2,1,0:T(8,128)S(1)}, u32[]{:S(2)}, u32[]{:S(2)}) collective-permute-start(f32[1,128,128]{2,1,0:T(8,128)S(1)} %get-tuple-element.28), channel_id=1, source_target_pairs={{0,2},{2,0},{4,6},{6,4},{1,3},{3,1},{5,7},{7,5},{8,10},{10,8},{12,... | collective-permute-start | bytes 196616 | tf_op jit(solution)/shard_map/ppermute | solution.py:348
  9.5 1.5 %collective-permute-start.5 = (f32[1,128,128]{2,1,0:T(8,128)S(1)}, f32[1,128,128]{2,1,0:T(8,128)S(1)}, u32[]{:S(2)}, u32[]{:S(2)}) collective-permute-start(f32[1,128,128]{2,1,0:T(8,128)S(1)} %get-tuple-element.27), channel_id=1, source_target_pairs={{0,4},{2,6},{4,0},{6,2},{1,5},{3,7},{5,1},{7,3},{8,12},{10,14},{12... | collective-permute-start | bytes 196616 | tf_op jit(solution)/shard_map/ppermute | solution.py:348
  11.0 0.0 collective-permute-done.3.refs_3_
  11.0 0.1 collective-permute-start.4
  11.1 0.2 shard_map.66
  11.3 0.0 collective-permute-done.2.refs_2_
  11.3 1.4 %collective-permute-done.1.refs_1_ = f32[128,128]{1,0:T(8,128)S(1)} collective-permute-done((f32[128,128]{1,0:T(8,128)S(1)}, f32[128,128]{1,0:T(8,128)S(1)}, u32[]{:S(2)}, u32[]{:S(2)}) %collective-permute-start.1) | collective-permute-done | bytes 65568 | tf_op jit(solution)/shard_map/ppermute | solution.py:347
  12.7 1.6 %collective-permute-start.7 = (f32[128,128]{1,0:T(8,128)S(1)}, f32[128,128]{1,0:T(8,128)S(1)}, u32[]{:S(2)}, u32[]{:S(2)}) collective-permute-start(f32[128,128]{1,0:T(8,128)S(1)} %shard_map.70.total_ref), channel_id=1, source_target_pairs={{0,8},{8,0},{16,24},{24,16},{1,9},{9,1},{17,25},{25,17},{2,10},{10... | collective-permute-start | bytes 196616 | tf_op jit(solution)/shard_map/ppermute | solution.py:353
  14.3 0.0 collective-permute-done.6.refs_2_
  14.3 0.1 collective-permute-done.5.refs_1_
  14.4 1.7 %collective-permute-done.4.refs_0_ = f32[1,128,128]{2,1,0:T(8,128)S(1)} collective-permute-done((f32[1,128,128]{2,1,0:T(8,128)S(1)}, f32[1,128,128]{2,1,0:T(8,128)S(1)}, u32[]{:S(2)}, u32[]{:S(2)}) %collective-permute-start.4) | collective-permute-done | bytes 65568 | tf_op jit(solution)/shard_map/ppermute | solution.py:348
  16.2 0.1 collective-permute-start.10
  16.3 3.0 %collective-permute-start.8 = (f32[128,128]{1,0:T(8,128)S(1)}, f32[128,128]{1,0:T(8,128)S(1)}, u32[]{:S(2)}, u32[]{:S(2)}) collective-permute-start(f32[128,128]{1,0:T(8,128)S(1)} %shard_map.70.total_ref), channel_id=1, source_target_pairs={{0,16},{8,24},{16,0},{24,8},{1,17},{9,25},{17,1},{25,9},{2,18},{10... | collective-permute-start | bytes 196616 | tf_op jit(solution)/shard_map/ppermute | solution.py:353
  19.3 1.3 %collective-permute-start.9 = (f32[128,128]{1,0:T(8,128)S(1)}, f32[128,128]{1,0:T(8,128)S(1)}, u32[]{:S(2)}, u32[]{:S(2)}) collective-permute-start(f32[128,128]{1,0:T(8,128)S(1)} %shard_map.70.total_ref), channel_id=1, source_target_pairs={{0,24},{8,16},{16,8},{24,0},{1,25},{9,17},{17,9},{25,1},{2,26},{10... | collective-permute-start | bytes 196616 | tf_op jit(solution)/shard_map/ppermute | solution.py:353
  20.7 1.5 %collective-permute-start.12 = (f32[2,128,128]{2,1,0:T(8,128)S(1)}, f32[2,128,128]{2,1,0:T(8,128)S(1)}, u32[]{:S(2)}, u32[]{:S(2)}) collective-permute-start(f32[2,128,128]{2,1,0:T(8,128)S(1)} %shard_map.72.slots_ref), channel_id=1, source_target_pairs={{0,4},{2,6},{4,0},{6,2},{1,5},{3,7},{5,1},{7,3},{8,12},{10,14},{12... | collective-permute-start | bytes 393224 | tf_op jit(solution)/shard_map/ppermute | solution.py:365
  22.2 0.0 collective-permute-done.7.refs_0_
  22.2 1.5 %collective-permute-start.14 = (f32[2,128,128]{2,1,0:T(8,128)S(1)}, f32[2,128,128]{2,1,0:T(8,128)S(1)}, u32[]{:S(2)}, u32[]{:S(2)}) collective-permute-start(f32[2,128,128]{2,1,0:T(8,128)S(1)} %shard_map.72.slots_ref), channel_id=1, source_target_pairs={{0,2},{2,0},{4,6},{6,4},{1,3},{3,1},{5,7},{7,5},{8,10},{10,8},{12,... | collective-permute-start | bytes 393224 | tf_op jit(solution)/shard_map/ppermute | solution.py:365
  23.7 0.0 collective-permute-done.8.refs_1_
  23.7 1.7 %collective-permute-done.9.refs_2_ = f32[128,128]{1,0:T(8,128)S(1)} collective-permute-done((f32[128,128]{1,0:T(8,128)S(1)}, f32[128,128]{1,0:T(8,128)S(1)}, u32[]{:S(2)}, u32[]{:S(2)}) %collective-permute-start.9) | collective-permute-done | bytes 65568 | tf_op jit(solution)/shard_map/ppermute | solution.py:353
  25.4 2.5 %collective-permute-start.11 = (f32[128,128]{1,0:T(8,128)S(1)}, f32[128,128]{1,0:T(8,128)S(1)}, u32[]{:S(2)}, u32[]{:S(2)}) collective-permute-start(f32[128,128]{1,0:T(8,128)S(1)} %shard_map.74.refs_1_), channel_id=1, source_target_pairs={{0,6},{2,4},{4,2},{6,0},{1,7},{3,5},{5,3},{7,1},{8,14},{10,12},{12... | collective-permute-start | bytes 196616 | tf_op jit(solution)/shard_map/ppermute | solution.py:372
  27.9 0.5 %collective-permute-start.13 = (f32[128,128]{1,0:T(8,128)S(1)}, f32[128,128]{1,0:T(8,128)S(1)}, u32[]{:S(2)}, u32[]{:S(2)}) collective-permute-start(f32[128,128]{1,0:T(8,128)S(1)} %shard_map.74.refs_1_), channel_id=1, source_target_pairs={{0,4},{2,6},{4,0},{6,2},{1,5},{3,7},{5,1},{7,3},{8,12},{10,14},{12... | collective-permute-start | bytes 196616 | tf_op jit(solution)/shard_map/ppermute | solution.py:372
  28.4 0.0 collective-permute-done.10.refs_1_
  28.4 0.5 %collective-permute-start.15 = (f32[128,128]{1,0:T(8,128)S(1)}, f32[128,128]{1,0:T(8,128)S(1)}, u32[]{:S(2)}, u32[]{:S(2)}) collective-permute-start(f32[128,128]{1,0:T(8,128)S(1)} %shard_map.74.refs_1_), channel_id=1, source_target_pairs={{0,2},{2,0},{4,6},{6,4},{1,3},{3,1},{5,7},{7,5},{8,10},{10,8},{12,... | collective-permute-start | bytes 196616 | tf_op jit(solution)/shard_map/ppermute | solution.py:372
  29.0 0.7 %shard_map.75.refs_0_ = f32[3,512,128]{2,1,0:T(8,128)} custom-call(f32[3,2,8,128]{3,2,1,0:T(8,128)S(1)} %get-tuple-element.17.factor_ref, f32[3,128,128]{2,1,0:T(8,128)S(1)} %shard_map.73.refs_0_, f32[128,128]{1,0:T(8,128)S(1)} %shard_map.74.refs_1_), custom_call_target="tpu_custom_call" | custom-call | flops 1000000 | tf_op jit(solution)/shard_map/pallas_call | solution.py:376
  29.7 0.9 %collective-permute-done.11.refs_2_ = f32[128,128]{1,0:T(8,128)S(1)} collective-permute-done((f32[128,128]{1,0:T(8,128)S(1)}, f32[128,128]{1,0:T(8,128)S(1)}, u32[]{:S(2)}, u32[]{:S(2)}) %collective-permute-start.11) | collective-permute-done | bytes 65568 | tf_op jit(solution)/shard_map/ppermute | solution.py:372
  30.6 0.7 %shard_map.76.refs_0_ = f32[3,512,128]{2,1,0:T(8,128)} custom-call(f32[3,2,8,128]{3,2,1,0:T(8,128)S(1)} %get-tuple-element.17.factor_ref, f32[3,512,128]{2,1,0:T(8,128)} %shard_map.75.refs_0_, f32[2,128,128]{2,1,0:T(8,128)S(1)} %collective-permute-done.10.refs_1_, f32[128,128]{1,0:T(8,128)S(1)} %collective-permute-done.11.refs_2_), custom_call_target="tpu_custom_call", output_to_operand_aliasing={{}: (1, {})} | custom-call | flops 1000000 | tf_op jit(solution)/shard_map/pallas_call | solution.py:376
  31.3 0.0 collective-permute-done.12.refs_1_
  31.4 0.0 collective-permute-done.14.refs_3_
  31.4 0.8 %collective-permute-done.13.refs_2_ = f32[128,128]{1,0:T(8,128)S(1)} collective-permute-done((f32[128,128]{1,0:T(8,128)S(1)}, f32[128,128]{1,0:T(8,128)S(1)}, u32[]{:S(2)}, u32[]{:S(2)}) %collective-permute-start.13) | collective-permute-done | bytes 65568 | tf_op jit(solution)/shard_map/ppermute | solution.py:372
  32.2 0.5 %collective-permute-done.15.refs_4_ = f32[128,128]{1,0:T(8,128)S(1)} collective-permute-done((f32[128,128]{1,0:T(8,128)S(1)}, f32[128,128]{1,0:T(8,128)S(1)}, u32[]{:S(2)}, u32[]{:S(2)}) %collective-permute-start.15) | collective-permute-done | bytes 65568 | tf_op jit(solution)/shard_map/ppermute | solution.py:372
  32.7 0.8 %shard_map.77 = f32[3,512,128]{2,1,0:T(8,128)} custom-call(f32[3,2,8,128]{3,2,1,0:T(8,128)S(1)} %get-tuple-element.17.factor_ref, f32[3,512,128]{2,1,0:T(8,128)} %shard_map.76.refs_0_, f32[2,128,128]{2,1,0:T(8,128)S(1)} %collective-permute-done.12.refs_1_, f32[128,128]{1,0:T(8,128)S(1)} %collective-permute-done.13.refs_2_, ...), custom_call_target="tpu_custom_call", output_to_operand_aliasing={{}: (1, {})} | custom-call | flops 1000000 | tf_op jit(solution)/shard_map/pallas_call | solution.py:376
  (5 shorter events, 0.1 us)
Async XLA Ops:
  0.0 2.4 %copy-start = (bf16[10,2,64,4,256]{4,3,2,1,0:T(4,128)(2,1)S(1)}, bf16[10,2,64,4,256]{4,3,2,1,0:T(4,128)(2,1)}, u32[]{:S(2)}) copy-start(bf16[10,2,64,4,256]{4,3,2,1,0:T(4,128)(2,1)} %param.9) | copy-start | bytes 7864324
  0.0 1.7 %collective-permute-start = (f32[10,2,4,256]{3,2,1,0:T(4,128)}, f32[10,2,4,256]{3,2,1,0:T(4,128)S(1)}, u32[]{:S(2)}, u32[]{:S(2)}) collective-permute-start(f32[10,2,4,256]{3,2,1,0:T(4,128)} %param.6), channel_id=1, source_target_pairs={{0,1},{1,0},{2,3},{3,2},{4,5},{5,4},{6,7},{7,6},{8,9},{9,8},{10,11... | collective-permute-start | bytes 245768 | tf_op jit(solution)/shard_map/ppermute | solution.py:327
  2.6 8.4 %collective-permute-start.3 = (f32[128,128]{1,0:T(8,128)S(1)}, f32[128,128]{1,0:T(8,128)S(1)}, u32[]{:S(2)}, u32[]{:S(2)}) collective-permute-start(f32[128,128]{1,0:T(8,128)S(1)} %get-tuple-element.24), channel_id=1, source_target_pairs={{0,2},{2,0},{4,6},{6,4},{1,3},{3,1},{5,7},{7,5},{8,10},{10,8},{12,... | collective-permute-start | bytes 196616 | tf_op jit(solution)/shard_map/ppermute | solution.py:347
  5.6 5.7 %collective-permute-start.2 = (f32[128,128]{1,0:T(8,128)S(1)}, f32[128,128]{1,0:T(8,128)S(1)}, u32[]{:S(2)}, u32[]{:S(2)}) collective-permute-start(f32[128,128]{1,0:T(8,128)S(1)} %get-tuple-element.23), channel_id=1, source_target_pairs={{0,4},{2,6},{4,0},{6,2},{1,5},{3,7},{5,1},{7,3},{8,12},{10,14},{12... | collective-permute-start | bytes 196616 | tf_op jit(solution)/shard_map/ppermute | solution.py:347
  7.4 5.3 %collective-permute-start.1 = (f32[128,128]{1,0:T(8,128)S(1)}, f32[128,128]{1,0:T(8,128)S(1)}, u32[]{:S(2)}, u32[]{:S(2)}) collective-permute-start(f32[128,128]{1,0:T(8,128)S(1)} %get-tuple-element.22), channel_id=1, source_target_pairs={{0,6},{2,4},{4,2},{6,0},{1,7},{3,5},{5,3},{7,1},{8,14},{10,12},{12... | collective-permute-start | bytes 196616 | tf_op jit(solution)/shard_map/ppermute | solution.py:347
  7.5 6.8 %collective-permute-start.6 = (f32[1,128,128]{2,1,0:T(8,128)S(1)}, f32[1,128,128]{2,1,0:T(8,128)S(1)}, u32[]{:S(2)}, u32[]{:S(2)}) collective-permute-start(f32[1,128,128]{2,1,0:T(8,128)S(1)} %get-tuple-element.28), channel_id=1, source_target_pairs={{0,2},{2,0},{4,6},{6,4},{1,3},{3,1},{5,7},{7,5},{8,10},{10,8},{12,... | collective-permute-start | bytes 196616 | tf_op jit(solution)/shard_map/ppermute | solution.py:348
  9.5 5.0 %collective-permute-start.5 = (f32[1,128,128]{2,1,0:T(8,128)S(1)}, f32[1,128,128]{2,1,0:T(8,128)S(1)}, u32[]{:S(2)}, u32[]{:S(2)}) collective-permute-start(f32[1,128,128]{2,1,0:T(8,128)S(1)} %get-tuple-element.27), channel_id=1, source_target_pairs={{0,4},{2,6},{4,0},{6,2},{1,5},{3,7},{5,1},{7,3},{8,12},{10,14},{12... | collective-permute-start | bytes 196616 | tf_op jit(solution)/shard_map/ppermute | solution.py:348
  11.0 5.2 %collective-permute-start.4 = (f32[1,128,128]{2,1,0:T(8,128)S(1)}, f32[1,128,128]{2,1,0:T(8,128)S(1)}, u32[]{:S(2)}, u32[]{:S(2)}) collective-permute-start(f32[1,128,128]{2,1,0:T(8,128)S(1)} %get-tuple-element.26), channel_id=1, source_target_pairs={{0,6},{2,4},{4,2},{6,0},{1,7},{3,5},{5,3},{7,1},{8,14},{10,12},{12... | collective-permute-start | bytes 196616 | tf_op jit(solution)/shard_map/ppermute | solution.py:348
  12.7 9.5 %collective-permute-start.7 = (f32[128,128]{1,0:T(8,128)S(1)}, f32[128,128]{1,0:T(8,128)S(1)}, u32[]{:S(2)}, u32[]{:S(2)}) collective-permute-start(f32[128,128]{1,0:T(8,128)S(1)} %shard_map.70.total_ref), channel_id=1, source_target_pairs={{0,8},{8,0},{16,24},{24,16},{1,9},{9,1},{17,25},{25,17},{2,10},{10... | collective-permute-start | bytes 196616 | tf_op jit(solution)/shard_map/ppermute | solution.py:353
  16.2 12.2 %collective-permute-start.10 = (f32[2,128,128]{2,1,0:T(8,128)S(1)}, f32[2,128,128]{2,1,0:T(8,128)S(1)}, u32[]{:S(2)}, u32[]{:S(2)}) collective-permute-start(f32[2,128,128]{2,1,0:T(8,128)S(1)} %shard_map.72.slots_ref), channel_id=1, source_target_pairs={{0,6},{2,4},{4,2},{6,0},{1,7},{3,5},{5,3},{7,1},{8,14},{10,12},{12... | collective-permute-start | bytes 393224 | tf_op jit(solution)/shard_map/ppermute | solution.py:365
  16.3 7.4 %collective-permute-start.8 = (f32[128,128]{1,0:T(8,128)S(1)}, f32[128,128]{1,0:T(8,128)S(1)}, u32[]{:S(2)}, u32[]{:S(2)}) collective-permute-start(f32[128,128]{1,0:T(8,128)S(1)} %shard_map.70.total_ref), channel_id=1, source_target_pairs={{0,16},{8,24},{16,0},{24,8},{1,17},{9,25},{17,1},{25,9},{2,18},{10... | collective-permute-start | bytes 196616 | tf_op jit(solution)/shard_map/ppermute | solution.py:353
  19.3 6.1 %collective-permute-start.9 = (f32[128,128]{1,0:T(8,128)S(1)}, f32[128,128]{1,0:T(8,128)S(1)}, u32[]{:S(2)}, u32[]{:S(2)}) collective-permute-start(f32[128,128]{1,0:T(8,128)S(1)} %shard_map.70.total_ref), channel_id=1, source_target_pairs={{0,24},{8,16},{16,8},{24,0},{1,25},{9,17},{17,9},{25,1},{2,26},{10... | collective-permute-start | bytes 196616 | tf_op jit(solution)/shard_map/ppermute | solution.py:353
  20.7 10.7 %collective-permute-start.12 = (f32[2,128,128]{2,1,0:T(8,128)S(1)}, f32[2,128,128]{2,1,0:T(8,128)S(1)}, u32[]{:S(2)}, u32[]{:S(2)}) collective-permute-start(f32[2,128,128]{2,1,0:T(8,128)S(1)} %shard_map.72.slots_ref), channel_id=1, source_target_pairs={{0,4},{2,6},{4,0},{6,2},{1,5},{3,7},{5,1},{7,3},{8,12},{10,14},{12... | collective-permute-start | bytes 393224 | tf_op jit(solution)/shard_map/ppermute | solution.py:365
  22.2 9.2 %collective-permute-start.14 = (f32[2,128,128]{2,1,0:T(8,128)S(1)}, f32[2,128,128]{2,1,0:T(8,128)S(1)}, u32[]{:S(2)}, u32[]{:S(2)}) collective-permute-start(f32[2,128,128]{2,1,0:T(8,128)S(1)} %shard_map.72.slots_ref), channel_id=1, source_target_pairs={{0,2},{2,0},{4,6},{6,4},{1,3},{3,1},{5,7},{7,5},{8,10},{10,8},{12,... | collective-permute-start | bytes 393224 | tf_op jit(solution)/shard_map/ppermute | solution.py:365
  25.4 5.2 %collective-permute-start.11 = (f32[128,128]{1,0:T(8,128)S(1)}, f32[128,128]{1,0:T(8,128)S(1)}, u32[]{:S(2)}, u32[]{:S(2)}) collective-permute-start(f32[128,128]{1,0:T(8,128)S(1)} %shard_map.74.refs_1_), channel_id=1, source_target_pairs={{0,6},{2,4},{4,2},{6,0},{1,7},{3,5},{5,3},{7,1},{8,14},{10,12},{12... | collective-permute-start | bytes 196616 | tf_op jit(solution)/shard_map/ppermute | solution.py:372
  27.9 4.3 %collective-permute-start.13 = (f32[128,128]{1,0:T(8,128)S(1)}, f32[128,128]{1,0:T(8,128)S(1)}, u32[]{:S(2)}, u32[]{:S(2)}) collective-permute-start(f32[128,128]{1,0:T(8,128)S(1)} %shard_map.74.refs_1_), channel_id=1, source_target_pairs={{0,4},{2,6},{4,0},{6,2},{1,5},{3,7},{5,1},{7,3},{8,12},{10,14},{12... | collective-permute-start | bytes 196616 | tf_op jit(solution)/shard_map/ppermute | solution.py:372
  28.4 4.3 %collective-permute-start.15 = (f32[128,128]{1,0:T(8,128)S(1)}, f32[128,128]{1,0:T(8,128)S(1)}, u32[]{:S(2)}, u32[]{:S(2)}) collective-permute-start(f32[128,128]{1,0:T(8,128)S(1)} %shard_map.74.refs_1_), channel_id=1, source_target_pairs={{0,2},{2,0},{4,6},{6,4},{1,3},{3,1},{5,7},{7,5},{8,10},{10,8},{12,... | collective-permute-start | bytes 196616 | tf_op jit(solution)/shard_map/ppermute | solution.py:372

commit v6 on v5

--- a/solution.py
+++ b/solution.py
@@ -53,6 +53,10 @@
     field = field.reshape(*lead, levels, x, y // LANES, LANES)
     field = jnp.swapaxes(field, -3, -2)
     return field.reshape(*lead, levels * x * (y // LANES), LANES)
+
+
+def flat(field):
+    return view(field.reshape(-1, *field.shape[2:]))
 
 
 def unview(rows, x, y):
@@ -109,12 +113,9 @@
     for l in range(levels):
         for m in range(modes):
             splat_ref[l, m] = jnp.full((ROWS, LANES), modes_ref[m, l], jnp.float32)
-    column = lax.rem(lax.broadcasted_iota(jnp.int32, (ROWS, LANES), 0), x)
-    count = jnp.zeros((ROWS, LANES), jnp.int32)
+    mode = lax.rem(lax.broadcasted_iota(jnp.int32, mask_ref.shape[1:], 0), modes)
     for i in range(x):
-        count = jnp.where(column == i, counts_ref[i], count)
-    for m in range(modes):
-        mask_ref[m] = (m < count).astype(jnp.float32)
+        mask_ref[i] = (mode < counts_ref[i]).astype(jnp.float32)
     windows, slots = factor_ref.shape[:2]
     for w in range(windows):
         local = index_ref[w] - lax.axis_index("tm") * slots
@@ -125,28 +126,9 @@
         copy.wait()
 
 
-def smoothed_pair(own, other):
-    row = lax.broadcasted_iota(jnp.int32, (ROWS, LANES), 0)
-    lane = lax.broadcasted_iota(jnp.int32, (ROWS, LANES), 1)
-    half = ROWS // 2
-    low = jnp.where(row < half, own, pltpu.roll(other, half, 0))
-    high = jnp.where(row < half, pltpu.roll(own, half, 0), other)
-    first, last = lane == 0, lane == LANES - 1
-    for _ in range(SMOOTH):
-        low_up, high_up = pltpu.roll(low, 1, 1), pltpu.roll(high, 1, 1)
-        low_down, high_down = pltpu.roll(low, LANES - 1, 1), pltpu.roll(high, LANES - 1, 1)
-        low_side = jnp.where(first, 0.0, low_up) + jnp.where(last, high_down, low_down)
-        high_side = jnp.where(first, low_up, high_up) + jnp.where(last, 0.0, high_down)
-        low_next = pltpu.roll(low, 1, 0) + pltpu.roll(low, ROWS - 1, 0)
-        high_next = pltpu.roll(high, 1, 0) + pltpu.roll(high, ROWS - 1, 0)
-        low = low + diffusion * (low_next + low_side - 4.0 * low)
-        high = high + diffusion * (high_next + high_side - 4.0 * high)
-    return jnp.where(row < half, low, pltpu.roll(high, half, 0))
-
-
 def product(group, step, share, splat_ref, field_ref, part_ref, total_ref, lead_ref):
-    members, modes = field_ref.shape[:2]
-    slots = part_ref.shape[1]
+    members, slots = part_ref.shape[:2]
+    modes = splat_ref.shape[1]
     owner = target_of(lax.axis_index("mem"), group, step)
     pair = 2 * ROWS
     for j in range(share // 2):
@@ -156,9 +138,9 @@
         for k in range(members):
             halves = []
             for h in range(2):
-                value = splat_ref[level + h, 0] * field_ref[k, 0]
+                value = splat_ref[level + h, 0] * field_ref[pl.ds(k * modes * ROWS, ROWS), :]
                 for m in range(1, modes):
-                    value = value + splat_ref[level + h, m] * field_ref[k, m]
+                    value = value + splat_ref[level + h, m] * field_ref[pl.ds((k * modes + m) * ROWS, ROWS), :]
                 halves.append(value)
             localized.append(jnp.concatenate(halves, axis=0))
         whole = None
@@ -174,17 +156,39 @@
 
 
 def smooth_kernel(mask_ref, own_ref, other_ref, field_ref):
-    members, modes = own_ref.shape[:2]
-    for k in range(members):
-        for m in range(modes):
-            field_ref[k, m] = smoothed_pair(own_ref[k, m], other_ref[k, m]) * mask_ref[m]
+    x, pairs = mask_ref.shape[:2]
+    tiles = ROWS // x
+    cells = [
+        [ref[pl.ds(tile * x + i, pairs, stride=ROWS), :] for tile in range(tiles)]
+        for ref in (own_ref, other_ref)
+        for i in range(x)
+    ]
+    lane = lax.broadcasted_iota(jnp.int32, (pairs, LANES), 1)
+    first, last = lane == 0, lane == LANES - 1
+    round_ = len(cells)
+    for left in range(SMOOTH - 1, -1, -1):
+        fresh = list(cells)
+        for i in sorted({j % round_ for j in range(-left, x + left)}):
+            up = [pltpu.roll(part, 1, 1) for part in cells[i]]
+            down = [pltpu.roll(part, LANES - 1, 1) for part in cells[i]]
+            fresh[i] = []
+            for tile in range(tiles):
+                before = up[tile - 1] if tile else 0.0
+                after = down[tile + 1] if tile + 1 < tiles else 0.0
+                near = jnp.where(first, before, up[tile]) + jnp.where(last, after, down[tile])
+                near = near + (cells[i - 1][tile] + cells[(i + 1) % round_][tile])
+                fresh[i].append((1.0 - 4.0 * diffusion) * cells[i][tile] + diffusion * near)
+        cells = fresh
+    for i in range(x):
+        for tile in range(tiles):
+            field_ref[pl.ds(tile * x + i, pairs, stride=ROWS), :] = cells[i][tile] * mask_ref[i]
 
 
 def mask_kernel(mask_ref, own_ref, field_ref):
-    members, modes = own_ref.shape[:2]
-    for k in range(members):
-        for m in range(modes):
-            field_ref[k, m] = own_ref[k, m] * mask_ref[m]
+    x, pairs = mask_ref.shape[:2]
+    for i in range(ROWS):
+        rows = pl.ds(i, pairs, stride=ROWS)
+        field_ref[rows, :] = own_ref[rows, :] * mask_ref[i % x]
 
 
 def gather_kernel(norm_factor, *refs):
@@ -243,27 +247,18 @@
     ]
 
 
-def place_kernel(group, plan, goes_on, factor_ref, *refs):
+def place_kernel(group, plan, goes_on, *refs):
     refs = list(refs)
     if goes_on:
         refs.pop(0)
     quarters = [(refs.pop(0), refs.pop(0)) for _ in plan]
     out_ref, *parts, sems = refs
     copies = []
-    for i, (step, (slots_ref, earlier_ref), part_ref) in enumerate(zip(plan, quarters, parts)):
-        windows, height = part_ref.shape[:2]
+    for i, (step, (mixed_ref, earlier_ref), part_ref) in enumerate(zip(plan, quarters, parts)):
         started = copies_out(group, step, part_ref, out_ref, sems.at[i])
-        for w in range(windows):
-            for r in range(0, height, ROWS):
-                rows = slice(r, r + ROWS)
-                value = earlier_ref[rows]
-                if step == 0:
-                    value = value + slots_ref[w, rows]
-                else:
-                    for t in range(slots_ref.shape[0]):
-                        value = value + factor_ref[w, t] * slots_ref[t, rows]
-                part_ref[w, rows] = value
-            started[w].start()
+        for w, copy in enumerate(started):
+            part_ref[w] = mixed_ref[w] + earlier_ref[...]
+            copy.start()
         copies += started
     for copy in copies:
         copy.wait()
@@ -295,7 +290,7 @@
     norm_factor = 1.0 / math.sqrt(members * group - 1)
     f32 = lambda *shape: jax.ShapeDtypeStruct(shape, jnp.float32)
     parts = view(perturbations)
-    own = view(control[:, :, None])
+    own = flat(control)
 
     room = parts.size * parts.dtype.itemsize + levels * modes * ROWS * LANES * 4
 
@@ -306,7 +301,7 @@
         out_shape=[
             pltpu.VMEM(own.shape, jnp.float32),
             pltpu.VMEM((levels, modes, ROWS, LANES), jnp.float32),
-            pltpu.VMEM((modes, ROWS, LANES), jnp.float32),
+            pltpu.VMEM((x, members * modes, LANES), jnp.float32),
             pltpu.VMEM((windows, slot_count, ROWS, LANES), jnp.float32),
         ],
         scratch_shapes=[
@@ -321,15 +316,15 @@
     )(vertical_modes.T, mode_counts, slot_index, blend_weight, own)
 
     shapes = [f32(height, LANES), f32(slot_count - 1, height, LANES)]
-    field_shape = f32(members, modes, ROWS, LANES)
+    field_shape = f32(members * modes * ROWS, LANES)
     plan = plan_of(group)
     if lax.axis_size("tile") == 2 and x == SMOOTH:
         other = lax.ppermute(control, "tile", ring(2, 1))
         field = call(
-            smooth_kernel, [masks, loaded, view(other[:, :, None])], field_shape, 1000
+            smooth_kernel, [masks, loaded, flat(other)], field_shape, 1000
         )
     else:
-        field = call(mask_kernel, [masks, view(smooth(control)[:, :, None])], field_shape, 1000)
+        field = call(mask_kernel, [masks, flat(smooth(control))], field_shape, 1000)
 
     products = []
     for step in plan + [0]:
@@ -375,18 +370,21 @@
         first = [] if whole is None else [whole]
         return pl.pallas_call(
             functools.partial(place_kernel, group, steps, bool(first)),
-            in_specs=[VMEM_SPEC] + [HBM_SPEC] * len(first) + [VMEM_SPEC] * (2 * len(steps)),
+            in_specs=[HBM_SPEC] * len(first) + [VMEM_SPEC] * (2 * len(steps)),
             out_specs=HBM_SPEC,
             out_shape=pltpu.HBM((windows, levels * ROWS, LANES), jnp.float32),
             scratch_shapes=[pltpu.VMEM((windows, height, LANES), jnp.float32)] * len(steps)
             + [pltpu.SemaphoreType.DMA((len(steps), windows))],
-            input_output_aliases={1: 0} if first else {},
+            input_output_aliases={0: 0} if first else {},
             compiler_params=pltpu.CompilerParams(vmem_limit_bytes=16 * 1024 * 1024),
             cost_estimate=pl.CostEstimate(flops=1000000, bytes_accessed=0, transcendentals=0),
-        )(factors, *first, *[ref for pair in quarters for ref in pair])
+        )(*first, *[ref for pair in quarters for ref in pair])
 
     whole = put([0], None, [(mixed, earlier)])
-    quarters = list(zip(slots_far, earlier_far))
+    quarters = []
+    for i, part in enumerate(slots_far):
+        part = call(mix_kernel, [factors, part], f32(windows, height, LANES), 1000000)
+        quarters.append((part, earlier_far[i]))
     if len(plan) > 1:
         whole = put(plan[:1], whole, quarters[:1])
         plan, quarters = plan[1:], quarters[1:]

time: 33.6 us -> 34.9 us (1.039)
  waiting for transfers between devices: 7.15 us -> 8.57 us
    ppermute x3, waiting for transfers between devices: 1.7 us -> 3.22 us  [per_device(): came.append(lax.ppermute(total, 'tm', pairing(stages, step)))]
    pallas_call x10 -> x13, Pallas kernels: 1.59 us -> 1.4 us  [call(): pl.pallas_call(kernel, in_specs=[VMEM_SPEC] * len(arrays), out_specs=jax....]
  transfers between devices with their start and end apart: 16 -> 16, of which waited for: 7 -> 6; matrix products, arithmetic and copies ran while one was open for 0% -> 0% of each run, Pallas kernels for 10% -> 10%
where the time goes in v6:
time: 34.9 us; the launch traced here: 34.7 us
  starting transfers between devices  21.2 us (61%)
  waiting for transfers between devices  8.57 us (25%)
  Pallas kernels  4.79 us (14%)
    ppermute x3, starting transfers between devices, per_device(): came.append(lax.ppermute(total, 'tm', pairing(stages, step)))  5.98 us
    ppermute x3, starting transfers between devices, per_device(): totals.append(lax.ppermute(products[i][0], 'mem', pairing(group, step)))  4.49 us
    ppermute x3, starting transfers between devices, per_device(): earlier_far.append(lax.ppermute(earlier, 'mem', pairing(group, step)))  3.55 us
    ppermute x3, starting transfers between devices, per_device(): leads.append(lax.ppermute(products[i][1], 'mem', pairing(group, step)))  3.55 us
    ppermute x3, waiting for transfers between devices, per_device(): came.append(lax.ppermute(total, 'tm', pairing(stages, step)))  3.22 us
    ppermute x3, starting transfers between devices, per_device(): slots_far.append(lax.ppermute(slots, 'mem', pairing(group, step)))  3.16 us
    pallas_call x3, Pallas kernels, put(): pl.pallas_call(functools.partial(place_kernel, group, steps, bool(first))...  2.21 us
    ppermute x3, waiting for transfers between devices, per_device(): earlier_far.append(lax.ppermute(earlier, 'mem', pairing(group, step)))  2.14 us
  transfers between devices with their start and end apart: 16, of which 6 were waited for; matrix products, arithmetic and copies ran while one was open for 0% of the time, Pallas kernels for 10%

profile of v6, /device:TPU:0, one launch (start us, length us, event | category | flops | bytes accessed | tf_op | source)
XLA Modules:
  0.0 34.7 jit_solution(14498927525857040936)
XLA Ops:
  0.0 0.0 copy-start
  0.0 0.5 %collective-permute-start = (f32[10,2,4,256]{3,2,1,0:T(4,128)}, f32[10,2,4,256]{3,2,1,0:T(4,128)S(1)}, u32[]{:S(2)}, u32[]{:S(2)}) collective-permute-start(f32[10,2,4,256]{3,2,1,0:T(4,128)} %param.6), channel_id=1, source_target_pairs={{0,1},{1,0},{2,3},{3,2},{4,5},{5,4},{6,7},{7,6},{8,9},{9,8},{10,11... | collective-permute-start | bytes 245768 | tf_op jit(solution)/shard_map/ppermute | solution.py:322
  0.5 1.2 %shard_map.64 = (f32[160,128]{1,0:T(8,128)S(1)}, f32[64,2,8,128]{3,2,1,0:T(8,128)S(1)}, f32[4,20,128]{2,1,0:T(8,128)S(1)}, f32[3,2,8,128]{3,2,1,0:T(8,128)S(1)}) custom-call(f32[2,64]{1,0:T(2,128)} %bitcast.27, s32[4]{0:T(128)} %counts_hbm.1, s32[3]{0:T(128)} %index_hbm.1, f32[3]{0:T(128)} %weight_hbm.1, f32[160,128]{1,0:T(8,128)} %bitcast.26), custom_call_target="tpu_custom_call" | custom-call | flops 1000000000 | bytes 1000000000 | tf_op jit(solution)/shard_map/pallas_call | solution.py:297
  1.7 0.0 collective-permute-done
  1.7 0.4 %shard_map.65.field_ref = f32[160,128]{1,0:T(8,128)S(1)} custom-call(f32[4,20,128]{2,1,0:T(8,128)S(1)} %get-tuple-element.19.mask_ref, f32[160,128]{1,0:T(8,128)S(1)} %get-tuple-element.20.own_ref, f32[160,128]{1,0:T(8,128)S(1)} %bitcast.25), custom_call_target="tpu_custom_call" | custom-call | flops 1000 | bytes 1000 | tf_op jit(solution)/shard_map/pallas_call | solution.py:272
  2.1 0.0 copy-done
  2.1 0.2 shard_map.69
  2.3 2.8 %collective-permute-start.3 = (f32[128,128]{1,0:T(8,128)S(1)}, f32[128,128]{1,0:T(8,128)S(1)}, u32[]{:S(2)}, u32[]{:S(2)}) collective-permute-start(f32[128,128]{1,0:T(8,128)S(1)} %get-tuple-element.24), channel_id=1, source_target_pairs={{0,2},{2,0},{4,6},{6,4},{1,3},{3,1},{5,7},{7,5},{8,10},{10,8},{12,... | collective-permute-start | bytes 196616 | tf_op jit(solution)/shard_map/ppermute | solution.py:342
  5.2 0.2 shard_map.68
  5.4 1.6 %collective-permute-start.2 = (f32[128,128]{1,0:T(8,128)S(1)}, f32[128,128]{1,0:T(8,128)S(1)}, u32[]{:S(2)}, u32[]{:S(2)}) collective-permute-start(f32[128,128]{1,0:T(8,128)S(1)} %get-tuple-element.23), channel_id=1, source_target_pairs={{0,4},{2,6},{4,0},{6,2},{1,5},{3,7},{5,1},{7,3},{8,12},{10,14},{12... | collective-permute-start | bytes 196616 | tf_op jit(solution)/shard_map/ppermute | solution.py:342
  7.0 0.2 shard_map.67
  7.2 0.1 collective-permute-start.1
  7.2 2.0 %collective-permute-start.6 = (f32[1,128,128]{2,1,0:T(8,128)S(1)}, f32[1,128,128]{2,1,0:T(8,128)S(1)}, u32[]{:S(2)}, u32[]{:S(2)}) collective-permute-start(f32[1,128,128]{2,1,0:T(8,128)S(1)} %get-tuple-element.28), channel_id=1, source_target_pairs={{0,2},{2,0},{4,6},{6,4},{1,3},{3,1},{5,7},{7,5},{8,10},{10,8},{12,... | collective-permute-start | bytes 196616 | tf_op jit(solution)/shard_map/ppermute | solution.py:343
  9.2 1.5 %collective-permute-start.5 = (f32[1,128,128]{2,1,0:T(8,128)S(1)}, f32[1,128,128]{2,1,0:T(8,128)S(1)}, u32[]{:S(2)}, u32[]{:S(2)}) collective-permute-start(f32[1,128,128]{2,1,0:T(8,128)S(1)} %get-tuple-element.27), channel_id=1, source_target_pairs={{0,4},{2,6},{4,0},{6,2},{1,5},{3,7},{5,1},{7,3},{8,12},{10,14},{12... | collective-permute-start | bytes 196616 | tf_op jit(solution)/shard_map/ppermute | solution.py:343
  10.7 0.0 collective-permute-done.3.refs_3_
  10.7 0.1 collective-permute-start.4
  10.8 0.2 shard_map.66
  11.0 0.0 collective-permute-done.2.refs_2_
  11.0 1.4 %collective-permute-done.1.refs_1_ = f32[128,128]{1,0:T(8,128)S(1)} collective-permute-done((f32[128,128]{1,0:T(8,128)S(1)}, f32[128,128]{1,0:T(8,128)S(1)}, u32[]{:S(2)}, u32[]{:S(2)}) %collective-permute-start.1) | collective-permute-done | bytes 65568 | tf_op jit(solution)/shard_map/ppermute | solution.py:342
  12.4 1.6 %collective-permute-start.7 = (f32[128,128]{1,0:T(8,128)S(1)}, f32[128,128]{1,0:T(8,128)S(1)}, u32[]{:S(2)}, u32[]{:S(2)}) collective-permute-start(f32[128,128]{1,0:T(8,128)S(1)} %shard_map.70.total_ref), channel_id=1, source_target_pairs={{0,8},{8,0},{16,24},{24,16},{1,9},{9,1},{17,25},{25,17},{2,10},{10... | collective-permute-start | bytes 196616 | tf_op jit(solution)/shard_map/ppermute | solution.py:348
  14.1 0.0 collective-permute-done.6.refs_2_
  14.1 0.1 collective-permute-done.5.refs_1_
  14.2 1.7 %collective-permute-done.4.refs_0_ = f32[1,128,128]{2,1,0:T(8,128)S(1)} collective-permute-done((f32[1,128,128]{2,1,0:T(8,128)S(1)}, f32[1,128,128]{2,1,0:T(8,128)S(1)}, u32[]{:S(2)}, u32[]{:S(2)}) %collective-permute-start.4) | collective-permute-done | bytes 65568 | tf_op jit(solution)/shard_map/ppermute | solution.py:343
  15.9 0.1 collective-permute-start.10
  16.1 3.0 %collective-permute-start.8 = (f32[128,128]{1,0:T(8,128)S(1)}, f32[128,128]{1,0:T(8,128)S(1)}, u32[]{:S(2)}, u32[]{:S(2)}) collective-permute-start(f32[128,128]{1,0:T(8,128)S(1)} %shard_map.70.total_ref), channel_id=1, source_target_pairs={{0,16},{8,24},{16,0},{24,8},{1,17},{9,25},{17,1},{25,9},{2,18},{10... | collective-permute-start | bytes 196616 | tf_op jit(solution)/shard_map/ppermute | solution.py:348
  19.0 1.5 %collective-permute-start.12 = (f32[2,128,128]{2,1,0:T(8,128)S(1)}, f32[2,128,128]{2,1,0:T(8,128)S(1)}, u32[]{:S(2)}, u32[]{:S(2)}) collective-permute-start(f32[2,128,128]{2,1,0:T(8,128)S(1)} %shard_map.72.slots_ref), channel_id=1, source_target_pairs={{0,4},{2,6},{4,0},{6,2},{1,5},{3,7},{5,1},{7,3},{8,12},{10,14},{12... | collective-permute-start | bytes 393224 | tf_op jit(solution)/shard_map/ppermute | solution.py:360
  20.6 1.3 %collective-permute-start.9 = (f32[128,128]{1,0:T(8,128)S(1)}, f32[128,128]{1,0:T(8,128)S(1)}, u32[]{:S(2)}, u32[]{:S(2)}) collective-permute-start(f32[128,128]{1,0:T(8,128)S(1)} %shard_map.70.total_ref), channel_id=1, source_target_pairs={{0,24},{8,16},{16,8},{24,0},{1,25},{9,17},{17,9},{25,1},{2,26},{10... | collective-permute-start | bytes 196616 | tf_op jit(solution)/shard_map/ppermute | solution.py:348
  21.9 0.0 collective-permute-done.7.refs_0_
  21.9 1.5 %collective-permute-start.14 = (f32[2,128,128]{2,1,0:T(8,128)S(1)}, f32[2,128,128]{2,1,0:T(8,128)S(1)}, u32[]{:S(2)}, u32[]{:S(2)}) collective-permute-start(f32[2,128,128]{2,1,0:T(8,128)S(1)} %shard_map.72.slots_ref), channel_id=1, source_target_pairs={{0,2},{2,0},{4,6},{6,4},{1,3},{3,1},{5,7},{7,5},{8,10},{10,8},{12,... | collective-permute-start | bytes 393224 | tf_op jit(solution)/shard_map/ppermute | solution.py:360
  23.4 0.0 collective-permute-done.8.refs_1_
  23.4 3.2 %collective-permute-done.9.refs_2_ = f32[128,128]{1,0:T(8,128)S(1)} collective-permute-done((f32[128,128]{1,0:T(8,128)S(1)}, f32[128,128]{1,0:T(8,128)S(1)}, u32[]{:S(2)}, u32[]{:S(2)}) %collective-permute-start.9) | collective-permute-done | bytes 65568 | tf_op jit(solution)/shard_map/ppermute | solution.py:348
  26.6 1.5 %collective-permute-start.11 = (f32[128,128]{1,0:T(8,128)S(1)}, f32[128,128]{1,0:T(8,128)S(1)}, u32[]{:S(2)}, u32[]{:S(2)}) collective-permute-start(f32[128,128]{1,0:T(8,128)S(1)} %shard_map.74.refs_1_), channel_id=1, source_target_pairs={{0,6},{2,4},{4,2},{6,0},{1,7},{3,5},{5,3},{7,1},{8,14},{10,12},{12... | collective-permute-start | bytes 196616 | tf_op jit(solution)/shard_map/ppermute | solution.py:367
  28.1 1.5 %collective-permute-start.13 = (f32[128,128]{1,0:T(8,128)S(1)}, f32[128,128]{1,0:T(8,128)S(1)}, u32[]{:S(2)}, u32[]{:S(2)}) collective-permute-start(f32[128,128]{1,0:T(8,128)S(1)} %shard_map.74.refs_1_), channel_id=1, source_target_pairs={{0,4},{2,6},{4,0},{6,2},{1,5},{3,7},{5,1},{7,3},{8,12},{10,14},{12... | collective-permute-start | bytes 196616 | tf_op jit(solution)/shard_map/ppermute | solution.py:367
  29.7 0.0 collective-permute-done.10.slots_ref
  29.7 0.5 %collective-permute-start.15 = (f32[128,128]{1,0:T(8,128)S(1)}, f32[128,128]{1,0:T(8,128)S(1)}, u32[]{:S(2)}, u32[]{:S(2)}) collective-permute-start(f32[128,128]{1,0:T(8,128)S(1)} %shard_map.74.refs_1_), channel_id=1, source_target_pairs={{0,2},{2,0},{4,6},{6,4},{1,3},{3,1},{5,7},{7,5},{8,10},{10,8},{12,... | collective-permute-start | bytes 196616 | tf_op jit(solution)/shard_map/ppermute | solution.py:367
  30.2 0.7 %shard_map.75.refs_0_ = f32[3,512,128]{2,1,0:T(8,128)} custom-call(f32[3,128,128]{2,1,0:T(8,128)S(1)} %shard_map.73.refs_0_, f32[128,128]{1,0:T(8,128)S(1)} %shard_map.74.refs_1_), custom_call_target="tpu_custom_call" | custom-call | flops 1000000 | tf_op jit(solution)/shard_map/pallas_call | solution.py:371
  31.0 0.0 collective-permute-done.12.slots_ref
  31.0 0.0 collective-permute-done.14.slots_ref
  31.1 0.8 %collective-permute-done.11.refs_2_ = f32[128,128]{1,0:T(8,128)S(1)} collective-permute-done((f32[128,128]{1,0:T(8,128)S(1)}, f32[128,128]{1,0:T(8,128)S(1)}, u32[]{:S(2)}, u32[]{:S(2)}) %collective-permute-start.11) | collective-permute-done | bytes 65568 | tf_op jit(solution)/shard_map/ppermute | solution.py:367
  31.9 0.7 %shard_map.77.refs_0_ = f32[3,512,128]{2,1,0:T(8,128)} custom-call(f32[3,512,128]{2,1,0:T(8,128)} %shard_map.75.refs_0_, f32[3,128,128]{2,1,0:T(8,128)S(1)} %shard_map.76.refs_1_, f32[128,128]{1,0:T(8,128)S(1)} %collective-permute-done.11.refs_2_), custom_call_target="tpu_custom_call", output_to_operand_aliasing={{}: (0, {})} | custom-call | flops 1000000 | tf_op jit(solution)/shard_map/pallas_call | solution.py:371
  32.6 0.0 collective-permute-done.13.refs_2_
  32.6 1.3 %collective-permute-done.15.refs_4_ = f32[128,128]{1,0:T(8,128)S(1)} collective-permute-done((f32[128,128]{1,0:T(8,128)S(1)}, f32[128,128]{1,0:T(8,128)S(1)}, u32[]{:S(2)}, u32[]{:S(2)}) %collective-permute-start.15) | collective-permute-done | bytes 65568 | tf_op jit(solution)/shard_map/ppermute | solution.py:367
  33.9 0.8 %shard_map.80 = f32[3,512,128]{2,1,0:T(8,128)} custom-call(f32[3,512,128]{2,1,0:T(8,128)} %shard_map.77.refs_0_, f32[3,128,128]{2,1,0:T(8,128)S(1)} %shard_map.78.refs_1_, f32[128,128]{1,0:T(8,128)S(1)} %collective-permute-done.13.refs_2_, f32[3,128,128]{2,1,0:T(8,128)S(1)} %shard_map.79.refs_3_, ...), custom_call_target="tpu_custom_call", output_to_operand_aliasing={{}: (0, {})} | custom-call | flops 1000000 | tf_op jit(solution)/shard_map/pallas_call | solution.py:371
  (8 shorter events, 0.2 us)
Async XLA Ops:
  0.0 2.1 %copy-start = (bf16[10,2,64,4,256]{4,3,2,1,0:T(4,128)(2,1)S(1)}, bf16[10,2,64,4,256]{4,3,2,1,0:T(4,128)(2,1)}, u32[]{:S(2)}) copy-start(bf16[10,2,64,4,256]{4,3,2,1,0:T(4,128)(2,1)} %param.9) | copy-start | bytes 7864324
  0.0 1.7 %collective-permute-start = (f32[10,2,4,256]{3,2,1,0:T(4,128)}, f32[10,2,4,256]{3,2,1,0:T(4,128)S(1)}, u32[]{:S(2)}, u32[]{:S(2)}) collective-permute-start(f32[10,2,4,256]{3,2,1,0:T(4,128)} %param.6), channel_id=1, source_target_pairs={{0,1},{1,0},{2,3},{3,2},{4,5},{5,4},{6,7},{7,6},{8,9},{9,8},{10,11... | collective-permute-start | bytes 245768 | tf_op jit(solution)/shard_map/ppermute | solution.py:322
  2.3 8.4 %collective-permute-start.3 = (f32[128,128]{1,0:T(8,128)S(1)}, f32[128,128]{1,0:T(8,128)S(1)}, u32[]{:S(2)}, u32[]{:S(2)}) collective-permute-start(f32[128,128]{1,0:T(8,128)S(1)} %get-tuple-element.24), channel_id=1, source_target_pairs={{0,2},{2,0},{4,6},{6,4},{1,3},{3,1},{5,7},{7,5},{8,10},{10,8},{12,... | collective-permute-start | bytes 196616 | tf_op jit(solution)/shard_map/ppermute | solution.py:342
  5.4 5.6 %collective-permute-start.2 = (f32[128,128]{1,0:T(8,128)S(1)}, f32[128,128]{1,0:T(8,128)S(1)}, u32[]{:S(2)}, u32[]{:S(2)}) collective-permute-start(f32[128,128]{1,0:T(8,128)S(1)} %get-tuple-element.23), channel_id=1, source_target_pairs={{0,4},{2,6},{4,0},{6,2},{1,5},{3,7},{5,1},{7,3},{8,12},{10,14},{12... | collective-permute-start | bytes 196616 | tf_op jit(solution)/shard_map/ppermute | solution.py:342
  7.2 5.3 %collective-permute-start.1 = (f32[128,128]{1,0:T(8,128)S(1)}, f32[128,128]{1,0:T(8,128)S(1)}, u32[]{:S(2)}, u32[]{:S(2)}) collective-permute-start(f32[128,128]{1,0:T(8,128)S(1)} %get-tuple-element.22), channel_id=1, source_target_pairs={{0,6},{2,4},{4,2},{6,0},{1,7},{3,5},{5,3},{7,1},{8,14},{10,12},{12... | collective-permute-start | bytes 196616 | tf_op jit(solution)/shard_map/ppermute | solution.py:342
  7.2 6.9 %collective-permute-start.6 = (f32[1,128,128]{2,1,0:T(8,128)S(1)}, f32[1,128,128]{2,1,0:T(8,128)S(1)}, u32[]{:S(2)}, u32[]{:S(2)}) collective-permute-start(f32[1,128,128]{2,1,0:T(8,128)S(1)} %get-tuple-element.28), channel_id=1, source_target_pairs={{0,2},{2,0},{4,6},{6,4},{1,3},{3,1},{5,7},{7,5},{8,10},{10,8},{12,... | collective-permute-start | bytes 196616 | tf_op jit(solution)/shard_map/ppermute | solution.py:343
  9.2 5.0 %collective-permute-start.5 = (f32[1,128,128]{2,1,0:T(8,128)S(1)}, f32[1,128,128]{2,1,0:T(8,128)S(1)}, u32[]{:S(2)}, u32[]{:S(2)}) collective-permute-start(f32[1,128,128]{2,1,0:T(8,128)S(1)} %get-tuple-element.27), channel_id=1, source_target_pairs={{0,4},{2,6},{4,0},{6,2},{1,5},{3,7},{5,1},{7,3},{8,12},{10,14},{12... | collective-permute-start | bytes 196616 | tf_op jit(solution)/shard_map/ppermute | solution.py:343
  10.7 5.2 %collective-permute-start.4 = (f32[1,128,128]{2,1,0:T(8,128)S(1)}, f32[1,128,128]{2,1,0:T(8,128)S(1)}, u32[]{:S(2)}, u32[]{:S(2)}) collective-permute-start(f32[1,128,128]{2,1,0:T(8,128)S(1)} %get-tuple-element.26), channel_id=1, source_target_pairs={{0,6},{2,4},{4,2},{6,0},{1,7},{3,5},{5,3},{7,1},{8,14},{10,12},{12... | collective-permute-start | bytes 196616 | tf_op jit(solution)/shard_map/ppermute | solution.py:343
  12.4 9.5 %collective-permute-start.7 = (f32[128,128]{1,0:T(8,128)S(1)}, f32[128,128]{1,0:T(8,128)S(1)}, u32[]{:S(2)}, u32[]{:S(2)}) collective-permute-start(f32[128,128]{1,0:T(8,128)S(1)} %shard_map.70.total_ref), channel_id=1, source_target_pairs={{0,8},{8,0},{16,24},{24,16},{1,9},{9,1},{17,25},{25,17},{2,10},{10... | collective-permute-start | bytes 196616 | tf_op jit(solution)/shard_map/ppermute | solution.py:348
  15.9 13.8 %collective-permute-start.10 = (f32[2,128,128]{2,1,0:T(8,128)S(1)}, f32[2,128,128]{2,1,0:T(8,128)S(1)}, u32[]{:S(2)}, u32[]{:S(2)}) collective-permute-start(f32[2,128,128]{2,1,0:T(8,128)S(1)} %shard_map.72.slots_ref), channel_id=1, source_target_pairs={{0,6},{2,4},{4,2},{6,0},{1,7},{3,5},{5,3},{7,1},{8,14},{10,12},{12... | collective-permute-start | bytes 393224 | tf_op jit(solution)/shard_map/ppermute | solution.py:360
  16.1 7.4 %collective-permute-start.8 = (f32[128,128]{1,0:T(8,128)S(1)}, f32[128,128]{1,0:T(8,128)S(1)}, u32[]{:S(2)}, u32[]{:S(2)}) collective-permute-start(f32[128,128]{1,0:T(8,128)S(1)} %shard_map.70.total_ref), channel_id=1, source_target_pairs={{0,16},{8,24},{16,0},{24,8},{1,17},{9,25},{17,1},{25,9},{2,18},{10... | collective-permute-start | bytes 196616 | tf_op jit(solution)/shard_map/ppermute | solution.py:348
  19.0 11.9 %collective-permute-start.12 = (f32[2,128,128]{2,1,0:T(8,128)S(1)}, f32[2,128,128]{2,1,0:T(8,128)S(1)}, u32[]{:S(2)}, u32[]{:S(2)}) collective-permute-start(f32[2,128,128]{2,1,0:T(8,128)S(1)} %shard_map.72.slots_ref), channel_id=1, source_target_pairs={{0,4},{2,6},{4,0},{6,2},{1,5},{3,7},{5,1},{7,3},{8,12},{10,14},{12... | collective-permute-start | bytes 393224 | tf_op jit(solution)/shard_map/ppermute | solution.py:360
  20.6 6.1 %collective-permute-start.9 = (f32[128,128]{1,0:T(8,128)S(1)}, f32[128,128]{1,0:T(8,128)S(1)}, u32[]{:S(2)}, u32[]{:S(2)}) collective-permute-start(f32[128,128]{1,0:T(8,128)S(1)} %shard_map.70.total_ref), channel_id=1, source_target_pairs={{0,24},{8,16},{16,8},{24,0},{1,25},{9,17},{17,9},{25,1},{2,26},{10... | collective-permute-start | bytes 196616 | tf_op jit(solution)/shard_map/ppermute | solution.py:348
  21.9 9.1 %collective-permute-start.14 = (f32[2,128,128]{2,1,0:T(8,128)S(1)}, f32[2,128,128]{2,1,0:T(8,128)S(1)}, u32[]{:S(2)}, u32[]{:S(2)}) collective-permute-start(f32[2,128,128]{2,1,0:T(8,128)S(1)} %shard_map.72.slots_ref), channel_id=1, source_target_pairs={{0,2},{2,0},{4,6},{6,4},{1,3},{3,1},{5,7},{7,5},{8,10},{10,8},{12,... | collective-permute-start | bytes 393224 | tf_op jit(solution)/shard_map/ppermute | solution.py:360
  26.6 5.2 %collective-permute-start.11 = (f32[128,128]{1,0:T(8,128)S(1)}, f32[128,128]{1,0:T(8,128)S(1)}, u32[]{:S(2)}, u32[]{:S(2)}) collective-permute-start(f32[128,128]{1,0:T(8,128)S(1)} %shard_map.74.refs_1_), channel_id=1, source_target_pairs={{0,6},{2,4},{4,2},{6,0},{1,7},{3,5},{5,3},{7,1},{8,14},{10,12},{12... | collective-permute-start | bytes 196616 | tf_op jit(solution)/shard_map/ppermute | solution.py:367
  28.1 4.5 %collective-permute-start.13 = (f32[128,128]{1,0:T(8,128)S(1)}, f32[128,128]{1,0:T(8,128)S(1)}, u32[]{:S(2)}, u32[]{:S(2)}) collective-permute-start(f32[128,128]{1,0:T(8,128)S(1)} %shard_map.74.refs_1_), channel_id=1, source_target_pairs={{0,4},{2,6},{4,0},{6,2},{1,5},{3,7},{5,1},{7,3},{8,12},{10,14},{12... | collective-permute-start | bytes 196616 | tf_op jit(solution)/shard_map/ppermute | solution.py:367
  29.7 4.3 %collective-permute-start.15 = (f32[128,128]{1,0:T(8,128)S(1)}, f32[128,128]{1,0:T(8,128)S(1)}, u32[]{:S(2)}, u32[]{:S(2)}) collective-permute-start(f32[128,128]{1,0:T(8,128)S(1)} %shard_map.74.refs_1_), channel_id=1, source_target_pairs={{0,2},{2,0},{4,6},{6,4},{1,3},{3,1},{5,7},{7,5},{8,10},{10,8},{12,... | collective-permute-start | bytes 196616 | tf_op jit(solution)/shard_map/ppermute | solution.py:367

commit v7 on v6

--- a/solution.py
+++ b/solution.py
@@ -37,8 +37,14 @@
     return lax.rem(place + step, count)
 
 
+def stage_plan(stages):
+    if stages == 4:
+        return [[2, 3, 0, 1], [3, 2, 0, 1], [1, 0, 3, 2]]
+    return [[(i + step) % stages for i in range(stages)] for step in range(1, stages)]
+
+
 def plan_of(group):
-    return list(range(group - 1, 0, -1))
+    return [group - 1][: group - 1] + list(range(1, group - 1))
 
 
 def source_of(place, count, step):
@@ -231,9 +237,12 @@
     *arrived, earlier_ref = refs
     stage = lax.axis_index("tm")
     earlier = jnp.zeros(earlier_ref.shape, jnp.float32)
-    for step, ref in enumerate(arrived, 1):
-        source = source_of(stage, stages, step)
-        earlier = earlier + ref[...] * jnp.where(source < stage, 1.0, 0.0)
+    for targets, ref in zip(stage_plan(stages), arrived):
+        ahead = jnp.float32(0.0)
+        for source, target in enumerate(targets):
+            if source < target:
+                ahead = jnp.where(stage == target, 1.0, ahead)
+        earlier = earlier + ref[...] * ahead
     earlier_ref[...] = earlier
 
 
@@ -344,8 +353,8 @@
     total = call(functools.partial(gather_kernel, norm_factor), totals, f32(height, LANES), 1000000)
 
     came = []
-    for step in range(1, stages):
-        came.append(lax.ppermute(total, "tm", pairing(stages, step)))
+    for targets in stage_plan(stages):
+        came.append(lax.ppermute(total, "tm", list(enumerate(targets))))
     scaled = call(
         functools.partial(scale_kernel, norm_factor), [leads[0]], shapes[1], 1000000
     )

time: 34.9 us -> 34.1 us (0.977)
  waiting for transfers between devices: 8.57 us -> 7.01 us
  starting transfers between devices: 21.2 us -> 22 us
    ppermute x3, waiting for transfers between devices: 1.79 us -> 0.67 us  [per_device(): leads.append(lax.ppermute(products[i][1], 'mem', pairing(group, step)))]
    ppermute x3, waiting for transfers between devices: 3.22 us -> 2.74 us  [per_device(): came.append(lax.ppermute(total, 'tm', list(enumerate(targets))))]
    ppermute x3, starting transfers between devices: 3.16 us -> 3.57 us  [per_device(): slots_far.append(lax.ppermute(slots, 'mem', pairing(group, step)))]
    ppermute x3, starting transfers between devices: 5.98 us -> 6.35 us  [per_device(): came.append(lax.ppermute(total, 'tm', list(enumerate(targets))))]
  transfers between devices with their start and end apart: 16 -> 16, of which waited for: 6 -> 5; matrix products, arithmetic and copies ran while one was open for 0% -> 0% of each run, Pallas kernels for 10% -> 10%
where the time goes in v7:
time: 34.1 us; the launch traced here: 34 us
  starting transfers between devices  22 us (65%)
  waiting for transfers between devices  7.01 us (21%)
  Pallas kernels  4.79 us (14%)
    ppermute x3, starting transfers between devices, per_device(): came.append(lax.ppermute(total, 'tm', list(enumerate(targets))))  6.35 us
    ppermute x3, starting transfers between devices, per_device(): totals.append(lax.ppermute(products[i][0], 'mem', pairing(group, step)))  4.49 us
    ppermute x3, starting transfers between devices, per_device(): slots_far.append(lax.ppermute(slots, 'mem', pairing(group, step)))  3.57 us
    ppermute x3, starting transfers between devices, per_device(): earlier_far.append(lax.ppermute(earlier, 'mem', pairing(group, step)))  3.55 us
    ppermute x3, starting transfers between devices, per_device(): leads.append(lax.ppermute(products[i][1], 'mem', pairing(group, step)))  3.55 us
    ppermute x3, waiting for transfers between devices, per_device(): came.append(lax.ppermute(total, 'tm', list(enumerate(targets))))  2.74 us
    pallas_call x3, Pallas kernels, put(): pl.pallas_call(functools.partial(place_kernel, group, steps, bool(first))...  2.21 us
    ppermute x3, waiting for transfers between devices, per_device(): earlier_far.append(lax.ppermute(earlier, 'mem', pairing(group, step)))  2.18 us
  transfers between devices with their start and end apart: 16, of which 5 were waited for; matrix products, arithmetic and copies ran while one was open for 0% of the time, Pallas kernels for 10%

profile of v7, /device:TPU:0, one launch (start us, length us, event | category | flops | bytes accessed | tf_op | source)
XLA Modules:
  0.0 34.0 jit_solution(2329520554934744191)
XLA Ops:
  0.0 0.0 copy-start
  0.0 0.5 %collective-permute-start = (f32[10,2,4,256]{3,2,1,0:T(4,128)}, f32[10,2,4,256]{3,2,1,0:T(4,128)S(1)}, u32[]{:S(2)}, u32[]{:S(2)}) collective-permute-start(f32[10,2,4,256]{3,2,1,0:T(4,128)} %param.6), channel_id=1, source_target_pairs={{0,1},{1,0},{2,3},{3,2},{4,5},{5,4},{6,7},{7,6},{8,9},{9,8},{10,11... | collective-permute-start | bytes 245768 | tf_op jit(solution)/shard_map/ppermute | solution.py:331
  0.5 1.2 %shard_map.64 = (f32[160,128]{1,0:T(8,128)S(1)}, f32[64,2,8,128]{3,2,1,0:T(8,128)S(1)}, f32[4,20,128]{2,1,0:T(8,128)S(1)}, f32[3,2,8,128]{3,2,1,0:T(8,128)S(1)}) custom-call(f32[2,64]{1,0:T(2,128)} %bitcast.27, s32[4]{0:T(128)} %counts_hbm.1, s32[3]{0:T(128)} %index_hbm.1, f32[3]{0:T(128)} %weight_hbm.1, f32[160,128]{1,0:T(8,128)} %bitcast.26), custom_call_target="tpu_custom_call" | custom-call | flops 1000000000 | bytes 1000000000 | tf_op jit(solution)/shard_map/pallas_call | solution.py:306
  1.7 0.0 collective-permute-done
  1.7 0.4 %shard_map.65.field_ref = f32[160,128]{1,0:T(8,128)S(1)} custom-call(f32[4,20,128]{2,1,0:T(8,128)S(1)} %get-tuple-element.19.mask_ref, f32[160,128]{1,0:T(8,128)S(1)} %get-tuple-element.20.own_ref, f32[160,128]{1,0:T(8,128)S(1)} %bitcast.25), custom_call_target="tpu_custom_call" | custom-call | flops 1000 | bytes 1000 | tf_op jit(solution)/shard_map/pallas_call | solution.py:281
  2.1 0.0 copy-done
  2.1 0.2 shard_map.69
  2.3 2.9 %collective-permute-start.3 = (f32[128,128]{1,0:T(8,128)S(1)}, f32[128,128]{1,0:T(8,128)S(1)}, u32[]{:S(2)}, u32[]{:S(2)}) collective-permute-start(f32[128,128]{1,0:T(8,128)S(1)} %get-tuple-element.24), channel_id=1, source_target_pairs={{0,4},{2,6},{4,0},{6,2},{1,5},{3,7},{5,1},{7,3},{8,12},{10,14},{12... | collective-permute-start | bytes 196616 | tf_op jit(solution)/shard_map/ppermute | solution.py:351
  5.2 0.2 shard_map.68
  5.4 1.6 %collective-permute-start.2 = (f32[128,128]{1,0:T(8,128)S(1)}, f32[128,128]{1,0:T(8,128)S(1)}, u32[]{:S(2)}, u32[]{:S(2)}) collective-permute-start(f32[128,128]{1,0:T(8,128)S(1)} %get-tuple-element.23), channel_id=1, source_target_pairs={{0,2},{2,0},{4,6},{6,4},{1,3},{3,1},{5,7},{7,5},{8,10},{10,8},{12,... | collective-permute-start | bytes 196616 | tf_op jit(solution)/shard_map/ppermute | solution.py:351
  7.0 0.2 shard_map.67
  7.2 0.1 collective-permute-start.1
  7.2 2.0 %collective-permute-start.6 = (f32[1,128,128]{2,1,0:T(8,128)S(1)}, f32[1,128,128]{2,1,0:T(8,128)S(1)}, u32[]{:S(2)}, u32[]{:S(2)}) collective-permute-start(f32[1,128,128]{2,1,0:T(8,128)S(1)} %get-tuple-element.28), channel_id=1, source_target_pairs={{0,4},{2,6},{4,0},{6,2},{1,5},{3,7},{5,1},{7,3},{8,12},{10,14},{12... | collective-permute-start | bytes 196616 | tf_op jit(solution)/shard_map/ppermute | solution.py:352
  9.2 1.5 %collective-permute-start.5 = (f32[1,128,128]{2,1,0:T(8,128)S(1)}, f32[1,128,128]{2,1,0:T(8,128)S(1)}, u32[]{:S(2)}, u32[]{:S(2)}) collective-permute-start(f32[1,128,128]{2,1,0:T(8,128)S(1)} %get-tuple-element.27), channel_id=1, source_target_pairs={{0,2},{2,0},{4,6},{6,4},{1,3},{3,1},{5,7},{7,5},{8,10},{10,8},{12,... | collective-permute-start | bytes 196616 | tf_op jit(solution)/shard_map/ppermute | solution.py:352
  10.7 0.0 collective-permute-done.3.refs_3_
  10.7 0.1 collective-permute-start.4
  10.8 0.2 shard_map.66
  11.0 0.0 collective-permute-done.2.refs_2_
  11.0 1.4 %collective-permute-done.1.refs_1_ = f32[128,128]{1,0:T(8,128)S(1)} collective-permute-done((f32[128,128]{1,0:T(8,128)S(1)}, f32[128,128]{1,0:T(8,128)S(1)}, u32[]{:S(2)}, u32[]{:S(2)}) %collective-permute-start.1) | collective-permute-done | bytes 65568 | tf_op jit(solution)/shard_map/ppermute | solution.py:351
  12.4 2.8 %collective-permute-start.7 = (f32[128,128]{1,0:T(8,128)S(1)}, f32[128,128]{1,0:T(8,128)S(1)}, u32[]{:S(2)}, u32[]{:S(2)}) collective-permute-start(f32[128,128]{1,0:T(8,128)S(1)} %shard_map.70.total_ref), channel_id=1, source_target_pairs={{0,16},{8,24},{16,0},{24,8},{1,17},{9,25},{17,1},{25,9},{2,18},{10... | collective-permute-start | bytes 196616 | tf_op jit(solution)/shard_map/ppermute | solution.py:357
  15.2 0.0 collective-permute-done.6.refs_2_
  15.2 0.0 collective-permute-done.5.refs_1_
  15.2 0.7 %collective-permute-done.4.refs_0_ = f32[1,128,128]{2,1,0:T(8,128)S(1)} collective-permute-done((f32[1,128,128]{2,1,0:T(8,128)S(1)}, f32[1,128,128]{2,1,0:T(8,128)S(1)}, u32[]{:S(2)}, u32[]{:S(2)}) %collective-permute-start.4) | collective-permute-done | bytes 65568 | tf_op jit(solution)/shard_map/ppermute | solution.py:352
  15.9 0.8 %collective-permute-start.10 = (f32[2,128,128]{2,1,0:T(8,128)S(1)}, f32[2,128,128]{2,1,0:T(8,128)S(1)}, u32[]{:S(2)}, u32[]{:S(2)}) collective-permute-start(f32[2,128,128]{2,1,0:T(8,128)S(1)} %shard_map.72.slots_ref), channel_id=1, source_target_pairs={{0,6},{2,4},{4,2},{6,0},{1,7},{3,5},{5,3},{7,1},{8,14},{10,12},{12... | collective-permute-start | bytes 393224 | tf_op jit(solution)/shard_map/ppermute | solution.py:369
  16.7 3.6 %collective-permute-start.8 = (f32[128,128]{1,0:T(8,128)S(1)}, f32[128,128]{1,0:T(8,128)S(1)}, u32[]{:S(2)}, u32[]{:S(2)}) collective-permute-start(f32[128,128]{1,0:T(8,128)S(1)} %shard_map.70.total_ref), channel_id=1, source_target_pairs={{0,24},{8,16},{16,0},{24,8},{1,25},{9,17},{17,1},{25,9},{2,26},{10... | collective-permute-start | bytes 196616 | tf_op jit(solution)/shard_map/ppermute | solution.py:357
  20.3 1.3 %collective-permute-start.12 = (f32[2,128,128]{2,1,0:T(8,128)S(1)}, f32[2,128,128]{2,1,0:T(8,128)S(1)}, u32[]{:S(2)}, u32[]{:S(2)}) collective-permute-start(f32[2,128,128]{2,1,0:T(8,128)S(1)} %shard_map.72.slots_ref), channel_id=1, source_target_pairs={{0,2},{2,0},{4,6},{6,4},{1,3},{3,1},{5,7},{7,5},{8,10},{10,8},{12,... | collective-permute-start | bytes 393224 | tf_op jit(solution)/shard_map/ppermute | solution.py:369
  21.5 0.0 collective-permute-start.9
  21.5 0.0 collective-permute-done.7.refs_0_
  21.6 1.5 %collective-permute-start.14 = (f32[2,128,128]{2,1,0:T(8,128)S(1)}, f32[2,128,128]{2,1,0:T(8,128)S(1)}, u32[]{:S(2)}, u32[]{:S(2)}) collective-permute-start(f32[2,128,128]{2,1,0:T(8,128)S(1)} %shard_map.72.slots_ref), channel_id=1, source_target_pairs={{0,4},{2,6},{4,0},{6,2},{1,5},{3,7},{5,1},{7,3},{8,12},{10,14},{12... | collective-permute-start | bytes 393224 | tf_op jit(solution)/shard_map/ppermute | solution.py:369
  23.1 0.0 collective-permute-done.8.refs_1_
  23.1 2.7 %collective-permute-done.9.refs_2_ = f32[128,128]{1,0:T(8,128)S(1)} collective-permute-done((f32[128,128]{1,0:T(8,128)S(1)}, f32[128,128]{1,0:T(8,128)S(1)}, u32[]{:S(2)}, u32[]{:S(2)}) %collective-permute-start.9) | collective-permute-done | bytes 65568 | tf_op jit(solution)/shard_map/ppermute | solution.py:357
  25.8 1.6 %collective-permute-start.11 = (f32[128,128]{1,0:T(8,128)S(1)}, f32[128,128]{1,0:T(8,128)S(1)}, u32[]{:S(2)}, u32[]{:S(2)}) collective-permute-start(f32[128,128]{1,0:T(8,128)S(1)} %shard_map.74.refs_1_), channel_id=1, source_target_pairs={{0,6},{2,4},{4,2},{6,0},{1,7},{3,5},{5,3},{7,1},{8,14},{10,12},{12... | collective-permute-start | bytes 196616 | tf_op jit(solution)/shard_map/ppermute | solution.py:376
  27.4 1.5 %collective-permute-start.13 = (f32[128,128]{1,0:T(8,128)S(1)}, f32[128,128]{1,0:T(8,128)S(1)}, u32[]{:S(2)}, u32[]{:S(2)}) collective-permute-start(f32[128,128]{1,0:T(8,128)S(1)} %shard_map.74.refs_1_), channel_id=1, source_target_pairs={{0,2},{2,0},{4,6},{6,4},{1,3},{3,1},{5,7},{7,5},{8,10},{10,8},{12,... | collective-permute-start | bytes 196616 | tf_op jit(solution)/shard_map/ppermute | solution.py:376
  28.9 0.0 collective-permute-done.10.slots_ref
  28.9 0.5 %collective-permute-start.15 = (f32[128,128]{1,0:T(8,128)S(1)}, f32[128,128]{1,0:T(8,128)S(1)}, u32[]{:S(2)}, u32[]{:S(2)}) collective-permute-start(f32[128,128]{1,0:T(8,128)S(1)} %shard_map.74.refs_1_), channel_id=1, source_target_pairs={{0,4},{2,6},{4,0},{6,2},{1,5},{3,7},{5,1},{7,3},{8,12},{10,14},{12... | collective-permute-start | bytes 196616 | tf_op jit(solution)/shard_map/ppermute | solution.py:376
  29.4 0.7 %shard_map.75.refs_0_ = f32[3,512,128]{2,1,0:T(8,128)} custom-call(f32[3,128,128]{2,1,0:T(8,128)S(1)} %shard_map.73.refs_0_, f32[128,128]{1,0:T(8,128)S(1)} %shard_map.74.refs_1_), custom_call_target="tpu_custom_call" | custom-call | flops 1000000 | tf_op jit(solution)/shard_map/pallas_call | solution.py:380
  30.2 0.0 collective-permute-done.12.slots_ref
  30.2 0.0 collective-permute-done.14.slots_ref
  30.3 0.8 %collective-permute-done.11.refs_2_ = f32[128,128]{1,0:T(8,128)S(1)} collective-permute-done((f32[128,128]{1,0:T(8,128)S(1)}, f32[128,128]{1,0:T(8,128)S(1)}, u32[]{:S(2)}, u32[]{:S(2)}) %collective-permute-start.11) | collective-permute-done | bytes 65568 | tf_op jit(solution)/shard_map/ppermute | solution.py:376
  31.1 0.7 %shard_map.77.refs_0_ = f32[3,512,128]{2,1,0:T(8,128)} custom-call(f32[3,512,128]{2,1,0:T(8,128)} %shard_map.75.refs_0_, f32[3,128,128]{2,1,0:T(8,128)S(1)} %shard_map.76.refs_1_, f32[128,128]{1,0:T(8,128)S(1)} %collective-permute-done.11.refs_2_), custom_call_target="tpu_custom_call", output_to_operand_aliasing={{}: (0, {})} | custom-call | flops 1000000 | tf_op jit(solution)/shard_map/pallas_call | solution.py:380
  31.8 0.0 collective-permute-done.13.refs_2_
  31.8 1.3 %collective-permute-done.15.refs_4_ = f32[128,128]{1,0:T(8,128)S(1)} collective-permute-done((f32[128,128]{1,0:T(8,128)S(1)}, f32[128,128]{1,0:T(8,128)S(1)}, u32[]{:S(2)}, u32[]{:S(2)}) %collective-permute-start.15) | collective-permute-done | bytes 65568 | tf_op jit(solution)/shard_map/ppermute | solution.py:376
  33.2 0.8 %shard_map.80 = f32[3,512,128]{2,1,0:T(8,128)} custom-call(f32[3,512,128]{2,1,0:T(8,128)} %shard_map.77.refs_0_, f32[3,128,128]{2,1,0:T(8,128)S(1)} %shard_map.78.refs_1_, f32[128,128]{1,0:T(8,128)S(1)} %collective-permute-done.13.refs_2_, f32[3,128,128]{2,1,0:T(8,128)S(1)} %shard_map.79.refs_3_, ...), custom_call_target="tpu_custom_call", output_to_operand_aliasing={{}: (0, {})} | custom-call | flops 1000000 | tf_op jit(solution)/shard_map/pallas_call | solution.py:380
  (8 shorter events, 0.2 us)
Async XLA Ops:
  0.0 2.1 %copy-start = (bf16[10,2,64,4,256]{4,3,2,1,0:T(4,128)(2,1)S(1)}, bf16[10,2,64,4,256]{4,3,2,1,0:T(4,128)(2,1)}, u32[]{:S(2)}) copy-start(bf16[10,2,64,4,256]{4,3,2,1,0:T(4,128)(2,1)} %param.9) | copy-start | bytes 7864324
  0.0 1.7 %collective-permute-start = (f32[10,2,4,256]{3,2,1,0:T(4,128)}, f32[10,2,4,256]{3,2,1,0:T(4,128)S(1)}, u32[]{:S(2)}, u32[]{:S(2)}) collective-permute-start(f32[10,2,4,256]{3,2,1,0:T(4,128)} %param.6), channel_id=1, source_target_pairs={{0,1},{1,0},{2,3},{3,2},{4,5},{5,4},{6,7},{7,6},{8,9},{9,8},{10,11... | collective-permute-start | bytes 245768 | tf_op jit(solution)/shard_map/ppermute | solution.py:331
  2.3 8.4 %collective-permute-start.3 = (f32[128,128]{1,0:T(8,128)S(1)}, f32[128,128]{1,0:T(8,128)S(1)}, u32[]{:S(2)}, u32[]{:S(2)}) collective-permute-start(f32[128,128]{1,0:T(8,128)S(1)} %get-tuple-element.24), channel_id=1, source_target_pairs={{0,4},{2,6},{4,0},{6,2},{1,5},{3,7},{5,1},{7,3},{8,12},{10,14},{12... | collective-permute-start | bytes 196616 | tf_op jit(solution)/shard_map/ppermute | solution.py:351
  5.4 5.6 %collective-permute-start.2 = (f32[128,128]{1,0:T(8,128)S(1)}, f32[128,128]{1,0:T(8,128)S(1)}, u32[]{:S(2)}, u32[]{:S(2)}) collective-permute-start(f32[128,128]{1,0:T(8,128)S(1)} %get-tuple-element.23), channel_id=1, source_target_pairs={{0,2},{2,0},{4,6},{6,4},{1,3},{3,1},{5,7},{7,5},{8,10},{10,8},{12,... | collective-permute-start | bytes 196616 | tf_op jit(solution)/shard_map/ppermute | solution.py:351
  7.2 5.3 %collective-permute-start.1 = (f32[128,128]{1,0:T(8,128)S(1)}, f32[128,128]{1,0:T(8,128)S(1)}, u32[]{:S(2)}, u32[]{:S(2)}) collective-permute-start(f32[128,128]{1,0:T(8,128)S(1)} %get-tuple-element.22), channel_id=1, source_target_pairs={{0,6},{2,4},{4,2},{6,0},{1,7},{3,5},{5,3},{7,1},{8,14},{10,12},{12... | collective-permute-start | bytes 196616 | tf_op jit(solution)/shard_map/ppermute | solution.py:351
  7.2 8.0 %collective-permute-start.6 = (f32[1,128,128]{2,1,0:T(8,128)S(1)}, f32[1,128,128]{2,1,0:T(8,128)S(1)}, u32[]{:S(2)}, u32[]{:S(2)}) collective-permute-start(f32[1,128,128]{2,1,0:T(8,128)S(1)} %get-tuple-element.28), channel_id=1, source_target_pairs={{0,4},{2,6},{4,0},{6,2},{1,5},{3,7},{5,1},{7,3},{8,12},{10,14},{12... | collective-permute-start | bytes 196616 | tf_op jit(solution)/shard_map/ppermute | solution.py:352
  9.2 6.0 %collective-permute-start.5 = (f32[1,128,128]{2,1,0:T(8,128)S(1)}, f32[1,128,128]{2,1,0:T(8,128)S(1)}, u32[]{:S(2)}, u32[]{:S(2)}) collective-permute-start(f32[1,128,128]{2,1,0:T(8,128)S(1)} %get-tuple-element.27), channel_id=1, source_target_pairs={{0,2},{2,0},{4,6},{6,4},{1,3},{3,1},{5,7},{7,5},{8,10},{10,8},{12,... | collective-permute-start | bytes 196616 | tf_op jit(solution)/shard_map/ppermute | solution.py:352
  10.7 5.2 %collective-permute-start.4 = (f32[1,128,128]{2,1,0:T(8,128)S(1)}, f32[1,128,128]{2,1,0:T(8,128)S(1)}, u32[]{:S(2)}, u32[]{:S(2)}) collective-permute-start(f32[1,128,128]{2,1,0:T(8,128)S(1)} %get-tuple-element.26), channel_id=1, source_target_pairs={{0,6},{2,4},{4,2},{6,0},{1,7},{3,5},{5,3},{7,1},{8,14},{10,12},{12... | collective-permute-start | bytes 196616 | tf_op jit(solution)/shard_map/ppermute | solution.py:352
  12.4 9.1 %collective-permute-start.7 = (f32[128,128]{1,0:T(8,128)S(1)}, f32[128,128]{1,0:T(8,128)S(1)}, u32[]{:S(2)}, u32[]{:S(2)}) collective-permute-start(f32[128,128]{1,0:T(8,128)S(1)} %shard_map.70.total_ref), channel_id=1, source_target_pairs={{0,16},{8,24},{16,0},{24,8},{1,17},{9,25},{17,1},{25,9},{2,18},{10... | collective-permute-start | bytes 196616 | tf_op jit(solution)/shard_map/ppermute | solution.py:357
  15.9 13.0 %collective-permute-start.10 = (f32[2,128,128]{2,1,0:T(8,128)S(1)}, f32[2,128,128]{2,1,0:T(8,128)S(1)}, u32[]{:S(2)}, u32[]{:S(2)}) collective-permute-start(f32[2,128,128]{2,1,0:T(8,128)S(1)} %shard_map.72.slots_ref), channel_id=1, source_target_pairs={{0,6},{2,4},{4,2},{6,0},{1,7},{3,5},{5,3},{7,1},{8,14},{10,12},{12... | collective-permute-start | bytes 393224 | tf_op jit(solution)/shard_map/ppermute | solution.py:369
  16.7 6.4 %collective-permute-start.8 = (f32[128,128]{1,0:T(8,128)S(1)}, f32[128,128]{1,0:T(8,128)S(1)}, u32[]{:S(2)}, u32[]{:S(2)}) collective-permute-start(f32[128,128]{1,0:T(8,128)S(1)} %shard_map.70.total_ref), channel_id=1, source_target_pairs={{0,24},{8,16},{16,0},{24,8},{1,25},{9,17},{17,1},{25,9},{2,26},{10... | collective-permute-start | bytes 196616 | tf_op jit(solution)/shard_map/ppermute | solution.py:357
  20.3 9.9 %collective-permute-start.12 = (f32[2,128,128]{2,1,0:T(8,128)S(1)}, f32[2,128,128]{2,1,0:T(8,128)S(1)}, u32[]{:S(2)}, u32[]{:S(2)}) collective-permute-start(f32[2,128,128]{2,1,0:T(8,128)S(1)} %shard_map.72.slots_ref), channel_id=1, source_target_pairs={{0,2},{2,0},{4,6},{6,4},{1,3},{3,1},{5,7},{7,5},{8,10},{10,8},{12,... | collective-permute-start | bytes 393224 | tf_op jit(solution)/shard_map/ppermute | solution.py:369
  21.5 4.3 %collective-permute-start.9 = (f32[128,128]{1,0:T(8,128)S(1)}, f32[128,128]{1,0:T(8,128)S(1)}, u32[]{:S(2)}, u32[]{:S(2)}) collective-permute-start(f32[128,128]{1,0:T(8,128)S(1)} %shard_map.70.total_ref), channel_id=1, source_target_pairs={{0,8},{8,0},{16,24},{24,16},{1,9},{9,1},{17,25},{25,17},{2,10},{10... | collective-permute-start | bytes 196616 | tf_op jit(solution)/shard_map/ppermute | solution.py:357
  21.6 8.7 %collective-permute-start.14 = (f32[2,128,128]{2,1,0:T(8,128)S(1)}, f32[2,128,128]{2,1,0:T(8,128)S(1)}, u32[]{:S(2)}, u32[]{:S(2)}) collective-permute-start(f32[2,128,128]{2,1,0:T(8,128)S(1)} %shard_map.72.slots_ref), channel_id=1, source_target_pairs={{0,4},{2,6},{4,0},{6,2},{1,5},{3,7},{5,1},{7,3},{8,12},{10,14},{12... | collective-permute-start | bytes 393224 | tf_op jit(solution)/shard_map/ppermute | solution.py:369
  25.8 5.2 %collective-permute-start.11 = (f32[128,128]{1,0:T(8,128)S(1)}, f32[128,128]{1,0:T(8,128)S(1)}, u32[]{:S(2)}, u32[]{:S(2)}) collective-permute-start(f32[128,128]{1,0:T(8,128)S(1)} %shard_map.74.refs_1_), channel_id=1, source_target_pairs={{0,6},{2,4},{4,2},{6,0},{1,7},{3,5},{5,3},{7,1},{8,14},{10,12},{12... | collective-permute-start | bytes 196616 | tf_op jit(solution)/shard_map/ppermute | solution.py:376
  27.4 4.4 %collective-permute-start.13 = (f32[128,128]{1,0:T(8,128)S(1)}, f32[128,128]{1,0:T(8,128)S(1)}, u32[]{:S(2)}, u32[]{:S(2)}) collective-permute-start(f32[128,128]{1,0:T(8,128)S(1)} %shard_map.74.refs_1_), channel_id=1, source_target_pairs={{0,2},{2,0},{4,6},{6,4},{1,3},{3,1},{5,7},{7,5},{8,10},{10,8},{12,... | collective-permute-start | bytes 196616 | tf_op jit(solution)/shard_map/ppermute | solution.py:376
  28.9 4.3 %collective-permute-start.15 = (f32[128,128]{1,0:T(8,128)S(1)}, f32[128,128]{1,0:T(8,128)S(1)}, u32[]{:S(2)}, u32[]{:S(2)}) collective-permute-start(f32[128,128]{1,0:T(8,128)S(1)} %shard_map.74.refs_1_), channel_id=1, source_target_pairs={{0,4},{2,6},{4,0},{6,2},{1,5},{3,7},{5,1},{7,3},{8,12},{10,14},{12... | collective-permute-start | bytes 196616 | tf_op jit(solution)/shard_map/ppermute | solution.py:376
